TPU v7x, 32 devices: a whole 2x2x4 slice. The times are simulated.
32 devices in a mesh: blk: 2 (over x), wide: 16 (over z, y, core).
Axes of the slice: x: 2, y: 2, z: 4, core: 2. Of those that a mesh axis runs over, the one named last changes fastest.
Arguments:
- volume: float32 [2, 2, 512, 896], P('blk', None, 'wide'), may hold values from -1.6 to 1.6
- path_lengths: float32 [2, 2, 2], replicated, may hold values from 0.5 to 2
- probe: float32 [2, 128, 128], replicated, may hold values from -6 to 6
- measured: bfloat16 [2, 16, 14, 128, 128], P('blk', 'wide'), may hold values from 0.19921875 to 3
- jitter: int32 [2, 2, 16, 14], P(None, 'blk', 'wide'), may hold values from 0 to 15
- step_sizes: float32 [2], replicated, may hold values from 0.02 to 0.2
Outputs:
- new_volume: float32 [2, 2, 512, 896], P('blk', None, 'wide')
- misfit: float32 [], replicated
All inputs are finite; a program needn't handle non-finite values.
Results may differ from a plain program's by a relative error of at most 0.0003.
Values sent between devices are 32-bit elements; how exact they have to be, the bound alone decides.
No kernel may reach another device: no remote copies, remote signals or barrier semaphores. Data moves between devices by JAX's collectives and lax.ppermute only.
A program may use at most 64 MiB of HBM per device.

v0:
```python
import math

import jax
import jax.numpy as jnp
from jax import lax
from jax.sharding import PartitionSpec as P

ROWS_DEV = 32
PATCH = 128
CSTEP = 64


highest = lax.Precision.HIGHEST
floor_value = 0.25


def passed_along(value, axis, steps):
    count = lax.axis_size(axis)
    pairs = [(source, (source + steps) % count) for source in range(count)]
    return lax.ppermute(value, axis, pairs)


def from_behind(shard, axis, by):
    count = lax.axis_size(axis)
    pairs = [(i, i + by) for i in range(count) if 0 <= i + by < count]
    return lax.ppermute(shard, axis, pairs)


def dft_tables(length):
    grid = jnp.arange(length, dtype=jnp.int32)
    product = grid[:, None] * grid[None, :] % length
    angles = product.astype(jnp.float32) * (2.0 * math.pi / length)
    factor = 1.0 / math.sqrt(length)
    return (jnp.cos(angles) * factor, -jnp.sin(angles) * factor)


def left_apply(table, batch):
    return jnp.einsum("jk,bkl->bjl", table, batch, precision=highest)


def right_apply(batch, table):
    return jnp.einsum("bjk,kl->bjl", batch, table, precision=highest)


def transform(real_in, imag_in, cos_table, sin_table):
    mid_real = left_apply(cos_table, real_in) - left_apply(sin_table, imag_in)
    mid_imag = left_apply(cos_table, imag_in) + left_apply(sin_table, real_in)
    out_real = right_apply(mid_real, cos_table) - right_apply(mid_imag, sin_table)
    out_imag = right_apply(mid_real, sin_table) + right_apply(mid_imag, cos_table)
    return (out_real, out_imag)


def strip_update(
    strip_real,
    strip_imaginary,
    probe,
    measured,
    jitter_rows,
    jitter_cols,
    row_corner,
    column_corner,
):
    patch_len = probe.shape[-1]
    number = measured.shape[0]
    cos_table, sin_table = dft_tables(patch_len)
    starts_row = row_corner + jitter_rows
    starts_col = column_corner + CSTEP * jnp.arange(number, dtype=jnp.int32) + jitter_cols

    def window(image, top, left):
        return lax.dynamic_slice(image, (top, left), (patch_len, patch_len))

    pick = jax.vmap(window, in_axes=(None, 0, 0))
    obj_real = pick(strip_real, starts_row, starts_col)
    obj_imag = pick(strip_imaginary, starts_row, starts_col)
    probe_real = probe[0]
    probe_imag = probe[1]
    wave_real = probe_real * obj_real - probe_imag * obj_imag
    wave_imag = probe_real * obj_imag + probe_imag * obj_real
    far_real, far_imag = transform(wave_real, wave_imag, cos_table, sin_table)
    modulus = jnp.sqrt(far_real * far_real + far_imag * far_imag)
    target = measured.astype(jnp.float32)
    error = modulus - target
    partial_misfit = jnp.sum(error * error)
    ratio = target / jnp.maximum(modulus, floor_value)
    back_real, back_imag = transform(ratio * far_real, ratio * far_imag, cos_table, -sin_table)
    diff_real = back_real - wave_real
    diff_imag = back_imag - wave_imag
    corr_real = probe_real * diff_real + probe_imag * diff_imag
    corr_imag = probe_real * diff_imag - probe_imag * diff_real

    def place(position, sums):
        acc_real, acc_imag = sums
        top = starts_row[position]
        left = starts_col[position]
        acc_real = lax.dynamic_update_slice(
            acc_real, window(acc_real, top, left) + corr_real[position], (top, left)
        )
        acc_imag = lax.dynamic_update_slice(
            acc_imag, window(acc_imag, top, left) + corr_imag[position], (top, left)
        )
        return (acc_real, acc_imag)

    zeros = jnp.zeros(strip_real.shape, strip_real.dtype)
    acc_real, acc_imag = lax.fori_loop(0, number, place, (zeros, zeros))
    return (acc_real, acc_imag, partial_misfit)


def body(volume, path_lengths, probe, measured, jitter, step_sizes):
    group = lax.axis_index("blk")
    groups = lax.axis_size("blk")
    column = lax.axis_index("wide")
    columns = lax.axis_size("wide")
    slab = volume[0]
    row_len = slab.shape[1]
    col_len = slab.shape[2]
    margin = probe.shape[-1] // 2
    own_paths = lax.dynamic_index_in_dim(path_lengths, group, 1, keepdims=False)

    def slab_term(angle, weight):
        coeffs = lax.dynamic_index_in_dim(own_paths, angle, 0, keepdims=False) * weight
        return jnp.einsum("l,lrc->rc", coeffs, slab, precision=highest)

    def cycle_step(section, carried):
        carried = passed_along(carried, "blk", 1)
        angle = (group - section) % groups
        weight = jnp.where(section < groups, 1.0, 0.0).astype(jnp.float32)
        return carried + slab_term(angle, weight)

    projection = lax.fori_loop(
        1, groups + 1, cycle_step, slab_term(group, jnp.ones((), jnp.float32))
    )
    sources = (2, 1, 0, -1, -2)
    pieces_real = []
    pieces_imag = []
    for offset in sources:
        if offset == 0:
            got_phase = projection
        else:
            got_phase = from_behind(projection, "wide", offset)
        source = column - offset
        valid = ((source >= 0) & (source < columns)).astype(jnp.float32)
        pieces_real.append(jnp.cos(got_phase) * valid)
        pieces_imag.append(jnp.sin(got_phase) * valid)
    ext_real = jnp.concatenate(pieces_real, 0)
    ext_imag = jnp.concatenate(pieces_imag, 0)
    strip_real = jnp.pad(ext_real, ((0, 0), (margin, margin)))
    strip_imaginary = jnp.pad(ext_imag, ((0, 0), (margin, margin)))
    row_corner = ROWS_DEV // 4
    column_corner = PATCH // 4 - ROWS_DEV // 4
    acc_real, acc_imag, local_misfit = strip_update(
        strip_real,
        strip_imaginary,
        probe,
        measured[0, 0],
        jitter[0, 0, 0],
        jitter[1, 0, 0],
        row_corner,
        column_corner,
    )
    acc_real = acc_real[:, margin : margin + col_len]
    acc_imag = acc_imag[:, margin : margin + col_len]

    def rows_of(array, slot):
        return array[slot * row_len : (slot + 1) * row_len]

    total_real = rows_of(acc_real, 2)
    total_imag = rows_of(acc_imag, 2)
    for offset in (-2, -1, 1, 2):
        got_real, got_imag = from_behind(
            (rows_of(acc_real, 2 + offset), rows_of(acc_imag, 2 + offset)), "wide", offset
        )
        total_real = total_real + got_real
        total_imag = total_imag + got_imag
    gradient = rows_of(ext_real, 2) * total_imag - rows_of(ext_imag, 2) * total_real
    total_misfit = lax.psum(local_misfit, ("blk", "wide"))
    scaled = step_sizes[:, None] * own_paths
    coeffs = scaled
    update = jnp.einsum(
        "al,arc->lrc",
        coeffs,
        lax.all_gather(gradient[None], "blk", axis=0, tiled=True),
        precision=highest,
    )
    return ((slab - update)[None], total_misfit)


def solution(mesh):
    in_specs = (
        P("blk", None, "wide", None),
        P(),
        P(),
        P("blk", "wide", None, None, None),
        P(None, "blk", "wide", None),
        P(),
    )
    out_specs = (P("blk", None, "wide", None), P())
    return jax.shard_map(body, mesh=mesh, in_specs=in_specs, out_specs=out_specs, check_vma=False)
```

profile of v0, /device:TPU:0, one launch (start us, length us, event | category | flops | bytes accessed | tf_op | source)
XLA Modules:
  0.0 310.8 jit_solution(9081547119739849727)
XLA Ops:
  3.4 11.1 %while.32 = (s32[]{:T(128)}, f32[32,896]{1,0:T(8,128)S(1)}, s32[]{:T(128)}, f32[2,2]{1,0:T(2,128)S(1)}, f32[2,32,896]{2,1,0:T(8,128)S(1)}, /*index=5*/s32[]{:T(128)}, s32[]{:T(128)}, s32[]{:T(128)}, f32[]{:T(128)}, f32[]{:T(128)}) while((s32[]{:T(128)}, f32[32,896]{1,0:T(8,128)S(1)}, s32[]{:T(128)}, f32[2,2]{1,0:T(2,128)S(1)}, ...), condition=%wide.region_1.2_spmd, body=%wide.region_0.1_spmd.sunk | while | flops 716821 | bytes 1147718 | solution.py:129
  3.4 3.0 collective-permute-start
  7.4 2.2 collective-permute-done
  9.6 1.8 collective-permute-start
  12.4 2.1 collective-permute-done
  14.5 3.7 %collective-permute-start.1 = (f32[32,896]{1,0:T(8,128)S(1)}, f32[32,896]{1,0:T(8,128)S(1)}, u32[]{:S(2)}, u32[]{:S(2)}) collective-permute-start(f32[32,896]{1,0:T(8,128)S(1)} %get-tuple-element.260), channel_id=1, source_target_pairs={{0,2},{1,3},{2,4},{3,5},{4,6},{5,7},{6,8},{7,9},{8,10},{9,11},{10,... | collective-permute-start | bytes 344072 | tf_op jit(solution)/shard_map/ppermute | solution.py:26
  24.9 5.7 %collective-permute-done.4 = f32[32,896]{1,0:T(8,128)S(1)} collective-permute-done((f32[32,896]{1,0:T(8,128)S(1)}, f32[32,896]{1,0:T(8,128)S(1)}, u32[]{:S(2)}, u32[]{:S(2)}) %collective-permute-start.4) | collective-permute-done | bytes 114720 | tf_op jit(solution)/shard_map/ppermute | solution.py:26
  31.4 28.7 %while.34 = (s32[]{:T(128)}, f32[160,1024]{1,0:T(8,128)S(1)}, s32[14,2]{0,1:T(2,128)S(1)}, f32[14,128,128]{2,1,0:T(8,128)S(1)}, s32[]{:T(128)}) while((s32[]{:T(128)}, f32[160,1024]{1,0:T(8,128)S(1)}, s32[14,2]{0,1:T(2,128)S(1)}, f32[14,128,128]{2,1,0:T(8,128)S(1)}, s32[]{:T(128)}) %tuple.120), condition=%wide.while_cond, body=%wide.while_body.sunk | while | flops 2 | bytes 131181 | solution.py:70
  60.3 26.8 %while.35 = (s32[]{:T(128)}, f32[160,1024]{1,0:T(8,128)S(1)}, s32[14,2]{0,1:T(2,128)S(1)}, f32[14,128,128]{2,1,0:T(8,128)S(1)}, s32[]{:T(128)}) while((s32[]{:T(128)}, f32[160,1024]{1,0:T(8,128)S(1)}, s32[14,2]{0,1:T(2,128)S(1)}, f32[14,128,128]{2,1,0:T(8,128)S(1)}, s32[]{:T(128)}) %tuple.127), condition=%wide.while_cond.1, body=%wide.while_body.1.sunk | while | flops 2 | bytes 131181 | solution.py:70
  97.9 2.0 convolution_subtract_fusion.2
  99.9 2.6 fusion.13
  102.5 2.2 fusion.14
  104.7 2.2 fusion.18
  106.9 2.2 fusion.8
  110.9 2.0 fusion.38
  112.9 2.2 fusion.7
  116.8 1.9 multiply_subtract_fusion
  118.9 118.6 %while.33 = (s32[]{:T(128)}, f32[160,1024]{1,0:T(8,128)S(1)}, f32[160,1024]{1,0:T(8,128)S(1)}, s32[14]{0:T(128)S(1)}, s32[14]{0:T(128)S(1)}, /*index=5*/f32[14,1...) while((s32[]{:T(128)}, f32[160,1024]{1,0:T(8,128)S(1)}, ...), condition=%wide.region_3.4_spmd, body=%wide.region_2.3_spmd.sunk | while | flops 32776 | bytes 655581 | solution.py:104
  238.9 3.0 collective-permute-start.11
  242.0 4.1 %collective-permute-start.12 = (f32[32,896]{1,0:T(8,128)S(1)}, f32[32,896]{1,0:T(8,128)S(1)}, u32[]{:S(2)}, u32[]{:S(2)}) collective-permute-start(f32[32,896]{1,0:T(8,128)S(1)} %get-tuple-element.348), channel_id=1, source_target_pairs={{0,2},{1,3},{2,4},{3,5},{4,6},{5,7},{6,8},{7,9},{8,10},{9,11},{10,... | collective-permute-start | bytes 344072 | tf_op jit(solution)/shard_map/ppermute | solution.py:26
  248.9 3.4 %collective-permute-start.7 = (f32[32,896]{1,0:T(8,128)S(1)}, f32[32,896]{1,0:T(8,128)S(1)}, u32[]{:S(2)}, u32[]{:S(2)}) collective-permute-start(f32[32,896]{1,0:T(8,128)S(1)} %get-tuple-element.345), channel_id=1, source_target_pairs={{0,1},{1,2},{2,3},{3,4},{4,5},{5,6},{6,7},{7,8},{8,9},{9,10},{10,1... | collective-permute-start | bytes 344072 | tf_op jit(solution)/shard_map/ppermute | solution.py:26
  252.3 4.3 %collective-permute-start.8 = (f32[32,896]{1,0:T(8,128)S(1)}, f32[32,896]{1,0:T(8,128)S(1)}, u32[]{:S(2)}, u32[]{:S(2)}) collective-permute-start(f32[32,896]{1,0:T(8,128)S(1)} %get-tuple-element.344), channel_id=1, source_target_pairs={{0,2},{1,3},{2,4},{3,5},{4,6},{5,7},{6,8},{7,9},{8,10},{9,11},{10,... | collective-permute-start | bytes 344072 | tf_op jit(solution)/shard_map/ppermute | solution.py:26
  257.9 43.5 %psum.7 = f32[]{:T(128)} all-reduce(f32[]{:T(128)} %get-tuple-element.365), channel_id=1, replica_groups=mesh['blk'=2,'wide'=16] {'blk','wide'}, use_global_device_ids=true, to_apply=%region_5.6 | all-reduce | flops 1 | bytes 8 | tf_op jit(solution)/shard_map/psum | solution.py:175
  301.9 5.8 %all-gather = f32[64,896]{1,0:T(8,128)S(1)} all-gather(f32[32,896]{1,0:T(8,128)S(1)} %multiply_subtract_fusion.2), channel_id=2, replica_groups=mesh['blk'=2,'wide'=16] {'blk'}, dimensions={0}, use_global_device_ids=true | all-gather | bytes 344064 | tf_op jit(solution)/shard_map/all_gather | solution.py:181
  (225 shorter events, 156.7 us)
Async XLA Ops:
  0.6 1.2 copy-start
  1.8 0.7 copy-start.1
  3.4 18.8 %copy-start.4 = (f32[2,128,128]{2,1,0:T(8,128)S(1)}, f32[2,128,128]{2,1,0:T(8,128)}, u32[]{:S(2)}) copy-start(f32[2,128,128]{2,1,0:T(8,128)} %param.12) | copy-start | bytes 393220
  3.4 6.2 %collective-permute-start = (f32[32,896]{1,0:T(8,128)S(1)}, f32[32,896]{1,0:T(8,128)S(1)}, u32[]{:S(2)}, u32[]{:S(2)}) collective-permute-start(f32[32,896]{1,0:T(8,128)S(1)} %get-tuple-element.514), channel_id=1, source_target_pairs={{0,16},{16,0},{1,17},{17,1},{2,18},{18,2},{3,19},{19,3},{4,20},{20... | collective-permute-start | bytes 344072 | tf_op jit(solution)/shard_map/while/body/eval_jaxpr/ppermute | solution.py:20
  9.6 4.9 %collective-permute-start = (f32[32,896]{1,0:T(8,128)S(1)}, f32[32,896]{1,0:T(8,128)S(1)}, u32[]{:S(2)}, u32[]{:S(2)}) collective-permute-start(f32[32,896]{1,0:T(8,128)S(1)} %get-tuple-element.514), channel_id=1, source_target_pairs={{0,16},{16,0},{1,17},{17,1},{2,18},{18,2},{3,19},{19,3},{4,20},{20... | collective-permute-start | bytes 344072 | tf_op jit(solution)/shard_map/while/body/eval_jaxpr/ppermute | solution.py:20
  14.5 7.6 %copy-start.5 = (s32[2,1,1,14]{3,2,1,0:T(1,128)S(1)}, s32[2,1,1,14]{3,2,1,0:T(1,128)}, u32[]{:S(2)}) copy-start(s32[2,1,1,14]{3,2,1,0:T(1,128)} %param.14) | copy-start | bytes 340
  14.5 7.7 %collective-permute-start.1 = (f32[32,896]{1,0:T(8,128)S(1)}, f32[32,896]{1,0:T(8,128)S(1)}, u32[]{:S(2)}, u32[]{:S(2)}) collective-permute-start(f32[32,896]{1,0:T(8,128)S(1)} %get-tuple-element.260), channel_id=1, source_target_pairs={{0,2},{1,3},{2,4},{3,5},{4,6},{5,7},{6,8},{7,9},{8,10},{9,11},{10,... | collective-permute-start | bytes 344072 | tf_op jit(solution)/shard_map/ppermute | solution.py:26
  18.2 4.5 %collective-permute-start.2 = (f32[32,896]{1,0:T(8,128)S(1)}, f32[32,896]{1,0:T(8,128)S(1)}, u32[]{:S(2)}, u32[]{:S(2)}) collective-permute-start(f32[32,896]{1,0:T(8,128)S(1)} %get-tuple-element.260), channel_id=1, source_target_pairs={{0,1},{1,2},{2,3},{3,4},{4,5},{5,6},{6,7},{7,8},{8,9},{9,10},{10,1... | collective-permute-start | bytes 344072 | tf_op jit(solution)/shard_map/ppermute | solution.py:26
  19.5 5.0 %collective-permute-start.3 = (f32[32,896]{1,0:T(8,128)S(1)}, f32[32,896]{1,0:T(8,128)S(1)}, u32[]{:S(2)}, u32[]{:S(2)}) collective-permute-start(f32[32,896]{1,0:T(8,128)S(1)} %get-tuple-element.260), channel_id=1, source_target_pairs={{1,0},{2,1},{3,2},{4,3},{5,4},{6,5},{7,6},{8,7},{9,8},{10,9},{11,1... | collective-permute-start | bytes 344072 | tf_op jit(solution)/shard_map/ppermute | solution.py:26
  20.8 9.8 %collective-permute-start.4 = (f32[32,896]{1,0:T(8,128)S(1)}, f32[32,896]{1,0:T(8,128)S(1)}, u32[]{:S(2)}, u32[]{:S(2)}) collective-permute-start(f32[32,896]{1,0:T(8,128)S(1)} %get-tuple-element.260), channel_id=1, source_target_pairs={{2,0},{3,1},{4,2},{5,3},{6,4},{7,5},{8,6},{9,7},{10,8},{11,9},{12,... | collective-permute-start | bytes 344072 | tf_op jit(solution)/shard_map/ppermute | solution.py:26
  97.9 2.0 copy-start.3
  237.6 11.3 %collective-permute-start.10 = (f32[32,896]{1,0:T(8,128)S(1)}, f32[32,896]{1,0:T(8,128)S(1)}, u32[]{:S(2)}, u32[]{:S(2)}) collective-permute-start(f32[32,896]{1,0:T(8,128)S(1)} %get-tuple-element.350), channel_id=1, source_target_pairs={{1,0},{2,1},{3,2},{4,3},{5,4},{6,5},{7,6},{8,7},{9,8},{10,9},{11,1... | collective-permute-start | bytes 344072 | tf_op jit(solution)/shard_map/ppermute | solution.py:26
  238.9 13.4 %collective-permute-start.11 = (f32[32,896]{1,0:T(8,128)S(1)}, f32[32,896]{1,0:T(8,128)S(1)}, u32[]{:S(2)}, u32[]{:S(2)}) collective-permute-start(f32[32,896]{1,0:T(8,128)S(1)} %get-tuple-element.349), channel_id=1, source_target_pairs={{0,1},{1,2},{2,3},{3,4},{4,5},{5,6},{6,7},{7,8},{8,9},{9,10},{10,1... | collective-permute-start | bytes 344072 | tf_op jit(solution)/shard_map/ppermute | solution.py:26
  242.0 14.6 %collective-permute-start.12 = (f32[32,896]{1,0:T(8,128)S(1)}, f32[32,896]{1,0:T(8,128)S(1)}, u32[]{:S(2)}, u32[]{:S(2)}) collective-permute-start(f32[32,896]{1,0:T(8,128)S(1)} %get-tuple-element.348), channel_id=1, source_target_pairs={{0,2},{1,3},{2,4},{3,5},{4,6},{5,7},{6,8},{7,9},{8,10},{9,11},{10,... | collective-permute-start | bytes 344072 | tf_op jit(solution)/shard_map/ppermute | solution.py:26
  246.3 55.1 %collective-permute-start.5 = (f32[32,896]{1,0:T(8,128)S(1)}, f32[32,896]{1,0:T(8,128)S(1)}, u32[]{:S(2)}, u32[]{:S(2)}) collective-permute-start(f32[32,896]{1,0:T(8,128)S(1)} %get-tuple-element.343), channel_id=1, source_target_pairs={{2,0},{3,1},{4,2},{5,3},{6,4},{7,5},{8,6},{9,7},{10,8},{11,9},{12,... | collective-permute-start | bytes 344072 | tf_op jit(solution)/shard_map/ppermute | solution.py:26
  247.6 53.8 %collective-permute-start.6 = (f32[32,896]{1,0:T(8,128)S(1)}, f32[32,896]{1,0:T(8,128)S(1)}, u32[]{:S(2)}, u32[]{:S(2)}) collective-permute-start(f32[32,896]{1,0:T(8,128)S(1)} %get-tuple-element.346), channel_id=1, source_target_pairs={{1,0},{2,1},{3,2},{4,3},{5,4},{6,5},{7,6},{8,7},{9,8},{10,9},{11,1... | collective-permute-start | bytes 344072 | tf_op jit(solution)/shard_map/ppermute | solution.py:26
  248.9 52.5 %collective-permute-start.7 = (f32[32,896]{1,0:T(8,128)S(1)}, f32[32,896]{1,0:T(8,128)S(1)}, u32[]{:S(2)}, u32[]{:S(2)}) collective-permute-start(f32[32,896]{1,0:T(8,128)S(1)} %get-tuple-element.345), channel_id=1, source_target_pairs={{0,1},{1,2},{2,3},{3,4},{4,5},{5,6},{6,7},{7,8},{8,9},{9,10},{10,1... | collective-permute-start | bytes 344072 | tf_op jit(solution)/shard_map/ppermute | solution.py:26
  252.3 49.1 %collective-permute-start.8 = (f32[32,896]{1,0:T(8,128)S(1)}, f32[32,896]{1,0:T(8,128)S(1)}, u32[]{:S(2)}, u32[]{:S(2)}) collective-permute-start(f32[32,896]{1,0:T(8,128)S(1)} %get-tuple-element.344), channel_id=1, source_target_pairs={{0,2},{1,3},{2,4},{3,5},{4,6},{5,7},{6,8},{7,9},{8,10},{9,11},{10,... | collective-permute-start | bytes 344072 | tf_op jit(solution)/shard_map/ppermute | solution.py:26
  256.6 44.8 %collective-permute-start.9 = (f32[32,896]{1,0:T(8,128)S(1)}, f32[32,896]{1,0:T(8,128)S(1)}, u32[]{:S(2)}, u32[]{:S(2)}) collective-permute-start(f32[32,896]{1,0:T(8,128)S(1)} %get-tuple-element.347), channel_id=1, source_target_pairs={{2,0},{3,1},{4,2},{5,3},{6,4},{7,5},{8,6},{9,7},{10,8},{11,9},{12,... | collective-permute-start | bytes 344072 | tf_op jit(solution)/shard_map/ppermute | solution.py:26
  301.9 5.9 %copy-start.2 = (f32[1,2,32,896]{3,1,2,0:T(2,128)S(1)}, f32[1,2,32,896]{3,1,2,0:T(2,128)}, u32[]{:S(2)}) copy-start(f32[1,2,32,896]{3,1,2,0:T(2,128)} %copy-done.1) | copy-start | bytes 688132
  307.7 0.7 copy-start.6
where the time goes:
time: 317 us; the launch traced here: 311 us
  local copies, waits for them, and re-layouts  124 us (39%)
  loops' own time  52.6 us (17%)
  blocking collectives  49.3 us (16%)
  matrix products  35.2 us (11%)
  starting transfers between devices  32.4 us (10%)
  waiting for transfers between devices  11 us (3%)
  other arithmetic  4.47 us (1%)
    gather x84, local copies, waits for them, and re-layouts  54.7 us
    another operation x1, loops' own time, strip_update(): acc_real, acc_imag = lax.fori_loop(0, number, place, (zeros, zeros))  51.7 us
    psum x1, blocking collectives, body(): total_misfit = lax.psum(local_misfit, ('blk', 'wide'))  43.5 us
    ppermute x12, starting transfers between devices, from_behind(): return lax.ppermute(shard, axis, pairs)  27.6 us
    dynamic_update_slice x14, local copies, waits for them, and re-layouts, place(): lax.dynamic_update_slice(acc_imag, window(acc_imag, top, left) + corr_ima...  24 us
    dynamic_update_slice x14, local copies, waits for them, and re-layouts, place(): lax.dynamic_update_slice(acc_real, window(acc_real, top, left) + corr_rea...  24 us
    dot_general x8, matrix products, left_apply(): return jnp.einsum('jk,bkl->bjl', table, batch, precision=highest)  15.7 us
    dot_general x8, matrix products, right_apply(): return jnp.einsum('bjk,kl->bjl', batch, table, precision=highest)  15.5 us
  transfers between devices with their start and end apart: 14, of which 4 were waited for; matrix products, arithmetic and copies ran while one was open for 1% of the time, Pallas kernels for 0%

commit v1 on v0

v1 whole, which is shorter than its diff:
```python
import functools
import math

import jax
import jax.numpy as jnp
import numpy as np
from jax import lax
from jax.experimental import pallas as pl
from jax.experimental.pallas import tpu as pltpu
from jax.sharding import PartitionSpec as P

ROWS_DEV = 32
CSTEP = 64
JIT = 16
FLOOR_RATIO = 4.0
LANES = 128
SUBS = 8
HALF_PI = (1.5703125, 4.837512969970703125e-4, 7.54978995489188216e-8)


def dft_tables(length):
    grid = np.arange(length)
    angles = (grid[:, None] * grid[None, :] % length) * (2.0 * math.pi / length)
    cos = np.cos(angles) / math.sqrt(length)
    sin = -np.sin(angles) / math.sqrt(length)
    table = np.block([[cos, sin], [-sin, cos]])
    high = table.astype(jnp.bfloat16)
    low = (table - high.astype(np.float64)).astype(jnp.bfloat16)
    right = lambda h, l: np.concatenate([h, h, l], 0)
    left = lambda h, l: np.concatenate([h, h, l], 1)
    return right(high, low), left(high.T, low.T), left(high, low), right(high.T, low.T)


def sin_cos(x):
    turns = jnp.floor(x * (2.0 / math.pi) + 0.5)
    r = x - turns * HALF_PI[0]
    r = r - turns * HALF_PI[1]
    r = r - turns * HALF_PI[2]
    quadrant = turns.astype(jnp.int32)
    z = r * r
    s = r + r * z * (-1.6666654611e-1 + z * (8.3321608736e-3 + z * -1.9515295891e-4))
    c = 1.0 - 0.5 * z + z * z * (
        4.166664568298827e-2 + z * (-1.388731625493765e-3 + z * 2.443315711809948e-5)
    )
    odd = (quadrant & 1) == 1
    sin = jnp.where(odd, c, s)
    cos = jnp.where(odd, s, c)
    sin = jnp.where((quadrant & 2) == 2, -sin, sin)
    cos = jnp.where(((quadrant + 1) & 2) == 2, -cos, cos)
    return sin, cos


def parts_of(x):
    high = x.astype(jnp.bfloat16)
    low = (x - high.astype(jnp.float32)).astype(jnp.bfloat16)
    return high, low


def window_place(position, patch):
    corner = patch // 4 - ROWS_DEV // 4 - patch // 2 + CSTEP * position
    tile = corner // LANES
    return tile, corner - tile * LANES


def strip_kernel(
    far,
    jitter,
    ends,
    own,
    mate,
    cross,
    relay,
    probe,
    measured,
    fwd_right,
    fwd_left,
    inv_left,
    inv_right,
    grad,
    misfit,
    obj_real,
    obj_imag,
    wave,
    twice,
    mid,
    back,
):
    number, patch, _ = measured.shape
    rows = own.shape[0]
    tiles = own.shape[1] // LANES
    near = ROWS_DEV // 4 + JIT
    dot = functools.partial(lax.dot, preferred_element_type=jnp.float32)

    is_odd = ends[0] == 1
    odd = jnp.full((SUBS, LANES), ends[0], jnp.int32) == 1
    up2_ok = ends[1].astype(jnp.float32)
    up1_ok = ends[2].astype(jnp.float32)
    dn1_ok = ends[3].astype(jnp.float32)
    dn2_ok = ends[4].astype(jnp.float32)

    for half in range(2):
        twice[0, half * patch : (half + 1) * patch, :] = probe[0]
        twice[1, half * patch : (half + 1) * patch, :] = probe[1]

    def put(row, phase, ok):
        s, c = sin_cos(phase)
        if ok is not None:
            s = s * ok
            c = c * ok
        obj_real[row : row + SUBS, :] = c
        obj_imag[row : row + SUBS, :] = s

    for r in range(0, rows, SUBS):
        put(2 * rows + r, own[r : r + SUBS, :], None)
    wide_odd = jnp.full((SUBS, own.shape[1]), ends[0], jnp.int32) == 1
    for r in range(0, far, SUBS):
        top = rows - far + r
        put(top, jnp.where(wide_odd, relay[r : r + SUBS, :], cross[r : r + SUBS, :]), up2_ok)
    for r in range(0, rows, SUBS):
        put(rows + r, jnp.where(wide_odd, mate[r : r + SUBS, :], cross[far + r : far + r + SUBS, :]), up1_ok)
    for r in range(0, rows, SUBS):
        put(3 * rows + r, jnp.where(wide_odd, cross[r : r + SUBS, :], mate[r : r + SUBS, :]), dn1_ok)
    for r in range(0, far, SUBS):
        put(4 * rows + r, jnp.where(wide_odd, cross[rows + r : rows + r + SUBS, :], relay[r : r + SUBS, :]), dn2_ok)

    lane = lax.broadcasted_iota(jnp.int32, (SUBS, LANES), 1)
    sub = lax.broadcasted_iota(jnp.int32, (SUBS, LANES), 0)

    def first_row(p):
        return ROWS_DEV // 4 + jitter[0, p]

    def masks(p):
        _, corner = window_place(p, patch)
        after = lane >= corner + jitter[1, p]
        below = [sub + k * SUBS >= first_row(p) for k in range(near // SUBS)]
        return after, below

    def pick(ref, p, k, after, below):
        tile, _ = window_place(p, patch)

        def at(row):
            left = ref[row : row + SUBS, tile * LANES : (tile + 1) * LANES] if tile >= 0 else 0.0
            right = (
                ref[row : row + SUBS, (tile + 1) * LANES : (tile + 2) * LANES]
                if tile + 1 < tiles
                else 0.0
            )
            return jnp.where(after, left, right)

        row = k * SUBS
        if row + SUBS <= ROWS_DEV // 4:
            return at(row + patch)
        if row < near:
            return jnp.where(below[k], at(row), at(row + patch))
        return at(row)

    steps = patch // SUBS
    for p in range(number):
        after, below = masks(p)
        _, corner = window_place(p, patch)
        shift = corner + jitter[1, p]
        start = patch - first_row(p)
        p_real = pltpu.roll(twice[0, pl.ds(start, patch), :], shift, 1)
        p_imag = pltpu.roll(twice[1, pl.ds(start, patch), :], shift, 1)
        for k in range(steps):
            o_real = pick(obj_real, p, k, after, below)
            o_imag = pick(obj_imag, p, k, after, below)
            a = p_real[k * SUBS : (k + 1) * SUBS]
            b = p_imag[k * SUBS : (k + 1) * SUBS]
            row = p * patch + k * SUBS
            wave[row : row + SUBS, :LANES] = a * o_real - b * o_imag
            wave[row : row + SUBS, LANES:] = a * o_imag + b * o_real

    for p in range(0, number, 2):
        high, low = parts_of(wave[p * patch : (p + 2) * patch, :])
        mid[p * patch : (p + 2) * patch, :] = dot(jnp.concatenate([high, low, high], 1), fwd_right[...])

    def upright(value):
        top = jnp.concatenate([value[:patch, :LANES], value[patch:, :LANES]], 1)
        low = jnp.concatenate([value[:patch, LANES:], value[patch:, LANES:]], 1)
        return jnp.concatenate([top, low], 0)

    total = jnp.zeros((SUBS, LANES), jnp.float32)
    for p in range(0, number, 2):
        high, low = parts_of(upright(mid[p * patch : (p + 2) * patch, :]))
        spectrum = dot(fwd_left[...], jnp.concatenate([high, low, high], 0))
        real, imag = spectrum[:patch], spectrum[patch:]
        target = jnp.concatenate([measured[p], measured[p + 1]], 1).astype(jnp.float32)
        power = real * real + imag * imag
        inverse = lax.rsqrt(jnp.maximum(power, 1e-30))
        error = power * inverse - target
        square = error * error
        for k in range(steps):
            for half in range(2):
                total += square[k * SUBS : (k + 1) * SUBS, half * LANES : (half + 1) * LANES]
        ratio = target * jnp.minimum(inverse, FLOOR_RATIO)
        high, low = parts_of(jnp.concatenate([ratio * real, ratio * imag], 0))
        undone = dot(inv_left[...], jnp.concatenate([high, low, high], 0))
        for half in range(2):
            row = (p + half) * patch
            lanes = slice(half * LANES, (half + 1) * LANES)
            back[row : row + patch, :LANES] = undone[:patch, lanes]
            back[row : row + patch, LANES:] = undone[patch:, lanes]
    misfit[...] = total

    for p in range(0, number, 2):
        high, low = parts_of(back[p * patch : (p + 2) * patch, :])
        out = dot(jnp.concatenate([high, low, high], 1), inv_right[...])
        w = wave[p * patch : (p + 2) * patch, :]
        mid[p * patch : (p + 2) * patch, :LANES] = w[:, :LANES] * out[:, LANES:] - w[:, LANES:] * out[:, :LANES]

    for t in range(tiles):
        meets = []
        for p in range(number):
            tile, _ = window_place(p, patch)
            if t in (tile, tile + 1):
                after, below = masks(p)
                meets.append((p, after if t == tile else jnp.logical_not(after), below))
        cols = slice(t * LANES, (t + 1) * LANES)
        for k in range(steps):
            row = k * SUBS
            here = there = None
            for p, mask, below in meets:
                term = jnp.where(mask, mid[p * patch + row : p * patch + row + SUBS, :LANES], 0.0)
                if row + SUBS <= ROWS_DEV // 4:
                    there = term if there is None else there + term
                elif row < near:
                    kept = jnp.where(below[k], term, 0.0)
                    here = kept if here is None else here + kept
                    there = (term - kept) if there is None else there + (term - kept)
                else:
                    here = term if here is None else here + term
            if here is not None:
                grad[row : row + SUBS, cols] = here
            else:
                grad[row : row + SUBS, cols] = jnp.zeros((SUBS, LANES), jnp.float32)
            if there is not None:
                grad[row + patch : row + patch + SUBS, cols] = there
    for row in range(patch + near, 5 * rows, SUBS):
        grad[row : row + SUBS, :] = jnp.zeros((SUBS, grad.shape[1]), jnp.float32)


def strip_gradient(far, jitter, ends, own, mate, cross, relay, probe, measured):
    number, patch, _ = measured.shape
    rows, cols = own.shape
    tables = dft_tables(patch)
    vmem = pl.BlockSpec(memory_space=pltpu.VMEM)
    smem = pl.BlockSpec(memory_space=pltpu.SMEM)
    f32 = jnp.float32
    return pl.pallas_call(
        functools.partial(strip_kernel, far),
        out_shape=(
            jax.ShapeDtypeStruct((5 * rows, cols), f32),
            jax.ShapeDtypeStruct((SUBS, LANES), f32),
        ),
        in_specs=[smem, smem] + [vmem] * 10,
        out_specs=(vmem, vmem),
        scratch_shapes=[
            pltpu.VMEM((5 * rows, cols), f32),
            pltpu.VMEM((5 * rows, cols), f32),
            pltpu.VMEM((number * patch, 2 * LANES), f32),
            pltpu.VMEM((2, 2 * patch, patch), f32),
            pltpu.VMEM((number * patch, 2 * LANES), f32),
            pltpu.VMEM((number * patch, 2 * LANES), f32),
        ],
        compiler_params=pltpu.CompilerParams(vmem_limit_bytes=40 * 1024 * 1024),
        cost_estimate=pl.CostEstimate(
            flops=24 * number * patch**3 * 4, bytes_accessed=4 * number * patch * patch, transcendentals=0
        ),
        name="strip",
    )(jitter, ends, own, mate, cross, relay, probe, measured, *tables)


def permuted(value, axis, target):
    count = lax.axis_size(axis)
    pairs = [(i, target(i)) for i in range(count) if 0 <= target(i) < count]
    return lax.ppermute(value, axis, pairs)


def with_mate(value):
    return permuted(value, "wide", lambda i: i ^ 1)


def across(value):
    return permuted(value, "wide", lambda i: i + 1 if i % 2 else i - 1)


def summed(value, axis):
    count = lax.axis_size(axis)
    if count & (count - 1):
        return lax.psum(value, axis)
    step = 1
    while step < count:
        value = value + permuted(value, axis, lambda i: i ^ step)
        step *= 2
    return value


def body(volume, path_lengths, probe, measured, jitter, step_sizes):
    group = lax.axis_index("blk")
    groups = lax.axis_size("blk")
    column = lax.axis_index("wide")
    columns = lax.axis_size("wide")
    slab = volume[0]
    rows = slab.shape[1]
    far = rows - ROWS_DEV // 4
    own_paths = lax.dynamic_index_in_dim(path_lengths, group, 1, keepdims=False)

    def slab_term(angle):
        coeffs = lax.dynamic_index_in_dim(own_paths, angle, 0, keepdims=False)
        return jnp.sum(coeffs[:, None, None] * slab, 0)

    def to_group(value, step):
        return lax.ppermute(value, "blk", [(i, (i + step) % groups) for i in range(groups)])

    own = slab_term(group)
    for step in range(1, groups):
        own = own + to_group(slab_term((group + step) % groups), step)

    odd = column % 2 == 1
    mate = with_mate(own)
    cross = across(
        jnp.where(
            odd,
            jnp.concatenate([mate[rows - far :], own], 0),
            jnp.concatenate([own, mate[:far]], 0),
        )
    )
    relay = with_mate(jnp.where(odd, cross[:far], cross[rows:]))
    ends = jnp.stack(
        [
            column % 2,
            (column >= 2).astype(jnp.int32),
            (column >= 1).astype(jnp.int32),
            (column + 1 < columns).astype(jnp.int32),
            (column + 2 < columns).astype(jnp.int32),
        ]
    )
    part, local = strip_gradient(
        far, jitter[:, 0, 0], ends, own, mate, cross, relay, probe, measured[0, 0]
    )
    up2 = part[rows - far : rows]
    up1 = part[rows : 2 * rows]
    mine = part[2 * rows : 3 * rows]
    dn1 = part[3 * rows : 4 * rows]
    dn2 = part[4 * rows : 4 * rows + far]

    def tail(value):
        return jnp.pad(value, ((rows - far, 0), (0, 0)))

    def head(value):
        return jnp.pad(value, ((0, rows - far), (0, 0)))

    got = with_mate(jnp.where(odd, up2, dn2))
    met = across(
        jnp.where(
            odd,
            jnp.concatenate([dn1 + head(got), dn2], 0),
            jnp.concatenate([up2, up1 + tail(got)], 0),
        )
    )
    last = with_mate(jnp.where(odd, up1 + tail(met[:far]), dn1 + head(met[rows:])))
    gradient = mine + last + jnp.where(odd, met[far:], met[:rows])
    total = jnp.sum(summed(summed(local, "wide"), "blk"))

    def share(angle, grad):
        coeffs = lax.dynamic_index_in_dim(own_paths, angle, 0, keepdims=False)
        scale = lax.dynamic_index_in_dim(step_sizes, angle, 0, keepdims=False)
        return (coeffs * scale)[:, None, None] * grad[None]

    update = share(group, gradient)
    for step in range(1, groups):
        update = update + share((group - step) % groups, to_group(gradient, step))
    return ((slab - update)[None], total)


def solution(mesh):
    in_specs = (
        P("blk", None, "wide", None),
        P(),
        P(),
        P("blk", "wide", None, None, None),
        P(None, "blk", "wide", None),
        P(),
    )
    out_specs = (P("blk", None, "wide", None), P())
    return jax.shard_map(body, mesh=mesh, in_specs=in_specs, out_specs=out_specs, check_vma=False)
```

time: 317 us -> 61.1 us (0.19); the launches traced: 311 us -> 60.8 us
  local copies, waits for them, and re-layouts: 124 us -> 3.7 us
  loops' own time: 52.6 us -> 0 us
  blocking collectives: 49.3 us -> 0 us
  matrix products: 35.2 us -> 0 us
  Pallas kernels: 0 us -> 4.9 us
  waiting for transfers between devices: 11 us -> 15.7 us
    gather x84 -> x0, local copies, waits for them, and re-layouts: 54.7 us -> none
    another operation x4 -> x0, loops' own time: 52.6 us -> none  [the longest x1 51.7 us: strip_update(): acc_real, acc_imag = lax.fori_loop(0, number, place, (zeros, zeros))]
    dynamic_update_slice x28 -> x0, local copies, waits for them, and re-layouts: 47.9 us -> none  [the longest x14 24 us: place(): lax.dynamic_update_slice(acc_imag, window(acc_imag, top, left) + corr_ima...]
    psum x1 -> x0, blocking collectives: 43.5 us -> none  [body(): total_misfit = lax.psum(local_misfit, ('blk', 'wide'))]
    dot_general x20 -> x0, matrix products: 35.2 us -> none  [the longest x8 15.7 us: left_apply(): return jnp.einsum('jk,bkl->bjl', table, batch, precision=highest)]
    dynamic_slice x29 -> x1, local copies, waits for them, and re-layouts: 17.4 us -> 0.59 us  [share(): scale = lax.dynamic_index_in_dim(step_sizes, angle, 0, keepdims=False)]
    all_gather x1 -> x0, blocking collectives: 5.83 us -> none  [body(): lax.all_gather(gradient[None], 'blk', axis=0, tiled=True)]
    pallas_call x0 -> x1, Pallas kernels: none -> 4.9 us  [strip_gradient(): pl.pallas_call(functools.partial(strip_kernel, far), out_shape=(jax.Shape...]
  transfers between devices with their start and end apart: 14 -> 13, of which waited for: 4 -> 10; matrix products, arithmetic and copies ran while one was open for 1% -> 1% of each run, Pallas kernels for 0% -> 0%
where the time goes in v1:
time: 61.1 us; the launch traced here: 60.8 us
  starting transfers between devices  31.6 us (52%)
  waiting for transfers between devices  15.7 us (26%)
  Pallas kernels  4.9 us (8%)
  other arithmetic  4 us (7%)
  local copies, waits for them, and re-layouts  3.7 us (6%)
  between operations  0.87 us (1%)
    ppermute x11, starting transfers between devices, permuted(): return lax.ppermute(value, axis, pairs)  28 us
    ppermute x11, waiting for transfers between devices, permuted(): return lax.ppermute(value, axis, pairs)  10.4 us
    ppermute x2, waiting for transfers between devices, to_group(): lax.ppermute(value, 'blk', [(i, (i + step) % groups) for i in range(group...  5.33 us
    pallas_call x1, Pallas kernels, strip_gradient(): pl.pallas_call(functools.partial(strip_kernel, far), out_shape=(jax.Shape...  4.9 us
    ppermute x2, starting transfers between devices, to_group(): lax.ppermute(value, 'blk', [(i, (i + step) % groups) for i in range(group...  3.62 us
    unnamed x20, local copies, waits for them, and re-layouts  3 us
    mul x2, other arithmetic, share(): return (coeffs * scale)[:, None, None] * grad[None]  1.31 us
  transfers between devices with their start and end apart: 13, of which 10 were waited for; matrix products, arithmetic and copies ran while one was open for 1% of the time, Pallas kernels for 0%

profile of v1, /device:TPU:0, one launch (start us, length us, event | category | flops | bytes accessed | tf_op | source)
XLA Modules:
  0.0 60.8 jit_solution(16387632654250484012)
XLA Ops:
  1.9 0.7 %copy-done.9 = f32[2,2,2]{2,1,0:T(2,128)S(1)} copy-done((f32[2,2,2]{2,1,0:T(2,128)S(1)}, f32[2,2,2]{2,1,0:T(2,128)}, u32[]{:S(2)}) %copy-start.9) | copy-done | bytes 56
  3.9 1.1 %fusion.1 = (f32[32,896]{1,0:T(8,128)S(1)}, f32[32,896]{1,0:T(8,128)S(1)}) fusion(f32[1,2,32,896]{3,2,1,0:T(8,128)} %param.10, f32[2]{0:T(128)S(1)} %get-tuple-element.20, f32[2]{0:T(128)S(1)} %get-tuple-element.9), kind=kLoop, calls=%fused_computation.3 | loop fusion | flops 172032 | bytes 458768 | tf_op jit(solution)/shard_map/reduce_sum | solution.py:311
  5.0 3.0 %collective-permute-start = (f32[32,896]{1,0:T(8,128)S(1)}, f32[32,896]{1,0:T(8,128)S(1)}, u32[]{:S(2)}, u32[]{:S(2)}) collective-permute-start(f32[32,896]{1,0:T(8,128)S(1)} %get-tuple-element.6), channel_id=1, source_target_pairs={{0,16},{16,0},{1,17},{17,1},{2,18},{18,2},{3,19},{19,3},{4,20},{20... | collective-permute-start | bytes 344072 | tf_op jit(solution)/shard_map/ppermute | solution.py:314
  8.1 3.1 %collective-permute-done = f32[32,896]{1,0:T(8,128)S(1)} collective-permute-done((f32[32,896]{1,0:T(8,128)S(1)}, f32[32,896]{1,0:T(8,128)S(1)}, u32[]{:S(2)}, u32[]{:S(2)}) %collective-permute-start) | collective-permute-done | bytes 114720 | tf_op jit(solution)/shard_map/ppermute | solution.py:314
  11.3 1.3 %collective-permute-done.1.mate = f32[32,896]{1,0:T(8,128)S(1)} collective-permute-done((f32[32,896]{1,0:T(8,128)S(1)}, f32[32,896]{1,0:T(8,128)S(1)}, u32[]{:S(2)}, u32[]{:S(2)}) %collective-permute-start.1) | collective-permute-done | bytes 114720 | tf_op jit(solution)/shard_map/ppermute | solution.py:277
  12.7 0.8 %collective-permute-start.2 = (f32[56,896]{1,0:T(8,128)S(1)}, f32[56,896]{1,0:T(8,128)S(1)}, u32[]{:S(2)}, u32[]{:S(2)}) collective-permute-start(f32[56,896]{1,0:T(8,128)S(1)} %maximum_select_fusion), channel_id=1, source_target_pairs={{1,2},{2,1},{3,4},{4,3},{5,6},{6,5},{7,8},{8,7},{9,10},{10,9},{11,... | collective-permute-start | bytes 602120 | tf_op jit(solution)/shard_map/ppermute | solution.py:277
  13.5 8.0 %collective-permute-start.3 = (f32[24,896]{1,0:T(8,128)S(1)}, f32[24,896]{1,0:T(8,128)S(1)}, u32[]{:S(2)}, u32[]{:S(2)}) collective-permute-start(f32[24,896]{1,0:T(8,128)S(1)} %slice_select_fusion.1), channel_id=1, source_target_pairs={{0,1},{1,0},{2,3},{3,2},{4,5},{5,4},{6,7},{7,6},{8,9},{9,8},{10,11... | collective-permute-start | bytes 258056 | tf_op jit(solution)/shard_map/ppermute | solution.py:277
  21.6 0.8 %collective-permute-done.3.relay = f32[24,896]{1,0:T(8,128)S(1)} collective-permute-done((f32[24,896]{1,0:T(8,128)S(1)}, f32[24,896]{1,0:T(8,128)S(1)}, u32[]{:S(2)}, u32[]{:S(2)}) %collective-permute-start.3) | collective-permute-done | bytes 86048 | tf_op jit(solution)/shard_map/ppermute | solution.py:277
  23.1 1.0 %copy-done.6 = bf16[768,256]{1,0:T(8,128)(2,1)S(1)} copy-done((bf16[768,256]{1,0:T(8,128)(2,1)S(1)}, bf16[768,256]{1,0:T(8,128)(2,1)}, u32[]{:S(2)}) %copy-start.6) | copy-done | bytes 393240
  24.1 4.9 %strip.1 = (f32[160,896]{1,0:T(8,128)S(1)}, f32[8,128]{1,0:T(8,128)S(1)}) custom-call(s32[2,14]{1,0:T(2,128)S(1)} %bitcast.24, s32[5]{0:T(128)S(1)} %stack.39.ends, f32[32,896]{1,0:T(8,128)S(1)} %add.107.own, f32[32,896]{1,0:T(8,128)S(1)} %collective-permute-done.1.mate, f32[56,896]{1,0:T(8,128)S(1)} %collective-permute-done.2.cross, ...), custom_call_target="tpu_custom_call" | custom-call | flops 2818572288 | bytes 917504 | tf_op jit(solution)/shard_map/strip/pallas_call | solution.py:250
  29.4 0.9 %collective-permute-done.4 = f32[24,896]{1,0:T(8,128)S(1)} collective-permute-done((f32[24,896]{1,0:T(8,128)S(1)}, f32[24,896]{1,0:T(8,128)S(1)}, u32[]{:S(2)}, u32[]{:S(2)}) %collective-permute-start.4) | collective-permute-done | bytes 86048 | tf_op jit(solution)/shard_map/ppermute | solution.py:277
  30.4 0.7 %collective-permute-start.5 = (f32[56,896]{1,0:T(8,128)S(1)}, f32[56,896]{1,0:T(8,128)S(1)}, u32[]{:S(2)}, u32[]{:S(2)}) collective-permute-start(f32[56,896]{1,0:T(8,128)S(1)} %maximum_select_fusion.1), channel_id=1, source_target_pairs={{1,2},{2,1},{3,4},{4,3},{5,6},{6,5},{7,8},{8,7},{9,10},{10,9},{11,... | collective-permute-start | bytes 602120 | tf_op jit(solution)/shard_map/ppermute | solution.py:277
  31.2 8.9 %collective-permute-start.6 = (f32[32,896]{1,0:T(8,128)S(1)}, f32[32,896]{1,0:T(8,128)S(1)}, u32[]{:S(2)}, u32[]{:S(2)}) collective-permute-start(f32[32,896]{1,0:T(8,128)S(1)} %add_select_fusion), channel_id=1, source_target_pairs={{0,1},{1,0},{2,3},{3,2},{4,5},{5,4},{6,7},{7,6},{8,9},{9,8},{10,11... | collective-permute-start | bytes 344072 | tf_op jit(solution)/shard_map/ppermute | solution.py:277
  40.2 1.1 %collective-permute-done.8 = f32[8,128]{1,0:T(8,128)S(1)} collective-permute-done((f32[8,128]{1,0:T(8,128)S(1)}, f32[8,128]{1,0:T(8,128)S(1)}, u32[]{:S(2)}, u32[]{:S(2)}) %collective-permute-start.8) | collective-permute-done | bytes 4128 | tf_op jit(solution)/shard_map/ppermute | solution.py:277
  41.3 2.5 %collective-permute-start.9 = (f32[8,128]{1,0:T(8,128)S(1)}, f32[8,128]{1,0:T(8,128)S(1)}, u32[]{:S(2)}, u32[]{:S(2)}) collective-permute-start(f32[8,128]{1,0:T(8,128)S(1)} %add.117), channel_id=1, source_target_pairs={{0,2},{1,3},{2,0},{3,1},{4,6},{5,7},{6,4},{7,5},{8,10},{9,11},{10,... | collective-permute-start | bytes 12296 | tf_op jit(solution)/shard_map/ppermute | solution.py:277
  43.8 1.6 %collective-permute-done.9 = f32[8,128]{1,0:T(8,128)S(1)} collective-permute-done((f32[8,128]{1,0:T(8,128)S(1)}, f32[8,128]{1,0:T(8,128)S(1)}, u32[]{:S(2)}, u32[]{:S(2)}) %collective-permute-start.9) | collective-permute-done | bytes 4128 | tf_op jit(solution)/shard_map/ppermute | solution.py:277
  45.4 2.0 %collective-permute-start.10 = (f32[8,128]{1,0:T(8,128)S(1)}, f32[8,128]{1,0:T(8,128)S(1)}, u32[]{:S(2)}, u32[]{:S(2)}) collective-permute-start(f32[8,128]{1,0:T(8,128)S(1)} %add.118), channel_id=1, source_target_pairs={{0,4},{1,5},{2,6},{3,7},{4,0},{5,1},{6,2},{7,3},{8,12},{9,13},{10,... | collective-permute-start | bytes 12296 | tf_op jit(solution)/shard_map/ppermute | solution.py:277
  47.4 1.6 %collective-permute-done.10 = f32[8,128]{1,0:T(8,128)S(1)} collective-permute-done((f32[8,128]{1,0:T(8,128)S(1)}, f32[8,128]{1,0:T(8,128)S(1)}, u32[]{:S(2)}, u32[]{:S(2)}) %collective-permute-start.10) | collective-permute-done | bytes 4128 | tf_op jit(solution)/shard_map/ppermute | solution.py:277
  49.0 3.0 %collective-permute-start.11 = (f32[8,128]{1,0:T(8,128)S(1)}, f32[8,128]{1,0:T(8,128)S(1)}, u32[]{:S(2)}, u32[]{:S(2)}) collective-permute-start(f32[8,128]{1,0:T(8,128)S(1)} %add.119), channel_id=1, source_target_pairs={{0,8},{1,9},{2,10},{3,11},{4,12},{5,13},{6,14},{7,15},{8,0},{9,1},... | collective-permute-start | bytes 12296 | tf_op jit(solution)/shard_map/ppermute | solution.py:277
  52.1 1.6 %collective-permute-done.11 = f32[8,128]{1,0:T(8,128)S(1)} collective-permute-done((f32[8,128]{1,0:T(8,128)S(1)}, f32[8,128]{1,0:T(8,128)S(1)}, u32[]{:S(2)}, u32[]{:S(2)}) %collective-permute-start.11) | collective-permute-done | bytes 4128 | tf_op jit(solution)/shard_map/ppermute | solution.py:277
  53.7 1.5 %collective-permute-start.12 = (f32[8,128]{1,0:T(8,128)S(1)}, f32[8,128]{1,0:T(8,128)S(1)}, u32[]{:S(2)}, u32[]{:S(2)}) collective-permute-start(f32[8,128]{1,0:T(8,128)S(1)} %add.120), channel_id=1, source_target_pairs={{0,16},{16,0},{1,17},{17,1},{2,18},{18,2},{3,19},{19,3},{4,20},{20... | collective-permute-start | bytes 12296 | tf_op jit(solution)/shard_map/ppermute | solution.py:277
  55.8 1.5 %collective-permute-done.12 = f32[8,128]{1,0:T(8,128)S(1)} collective-permute-done((f32[8,128]{1,0:T(8,128)S(1)}, f32[8,128]{1,0:T(8,128)S(1)}, u32[]{:S(2)}, u32[]{:S(2)}) %collective-permute-start.12) | collective-permute-done | bytes 4128 | tf_op jit(solution)/shard_map/ppermute | solution.py:277
  57.9 2.2 %collective-permute-done.7 = f32[32,896]{1,0:T(8,128)S(1)} collective-permute-done((f32[32,896]{1,0:T(8,128)S(1)}, f32[32,896]{1,0:T(8,128)S(1)}, u32[]{:S(2)}, u32[]{:S(2)}) %collective-permute-start.7) | collective-permute-done | bytes 114720 | tf_op jit(solution)/shard_map/ppermute | solution.py:314
  60.1 0.8 %add_subtract_fusion = f32[1,2,32,896]{3,2,1,0:T(8,128)} fusion(f32[1,2,32,896]{3,2,1,0:T(8,128)S(1)} %copy-done.7, f32[32,896]{1,0:T(8,128)S(1)} %collective-permute-done.7, f32[2]{0:T(128)S(1)} %get-tuple-element.19, f32[32,896]{1,0:T(8,128)S(1)} %fusion.2, f32[2]{0:T(128)S(1)} %get-tuple-element.8), kind=kLoop, calls=%fused_computation.4 | loop fusion | flops 229376 | bytes 688144 | tf_op jit(solution)/shard_map/sub | solution.py:374
  (44 shorter events, 5.3 us)
Async XLA Ops:
  0.7 0.7 %copy-start.8 = (f32[2]{0:T(128)S(1)}, f32[2]{0:T(128)}, u32[]{:S(2)}) copy-start(f32[2]{0:T(128)} %param.15) | copy-start | bytes 28
  1.9 0.7 %copy-start.9 = (f32[2,2,2]{2,1,0:T(2,128)S(1)}, f32[2,2,2]{2,1,0:T(2,128)}, u32[]{:S(2)}) copy-start(f32[2,2,2]{2,1,0:T(2,128)} %param.11) | copy-start | bytes 100
  3.9 18.5 %copy-start.5 = (bf16[256,768]{1,0:T(8,128)(2,1)S(1)}, bf16[256,768]{1,0:T(8,128)(2,1)}, u32[]{:S(2)}) copy-start(bf16[256,768]{1,0:T(8,128)(2,1)} %constant.118.clone.fwd_left) | copy-start | bytes 1179652
  5.0 6.2 %collective-permute-start = (f32[32,896]{1,0:T(8,128)S(1)}, f32[32,896]{1,0:T(8,128)S(1)}, u32[]{:S(2)}, u32[]{:S(2)}) collective-permute-start(f32[32,896]{1,0:T(8,128)S(1)} %get-tuple-element.6), channel_id=1, source_target_pairs={{0,16},{16,0},{1,17},{17,1},{2,18},{18,2},{3,19},{19,3},{4,20},{20... | collective-permute-start | bytes 344072 | tf_op jit(solution)/shard_map/ppermute | solution.py:314
  11.2 11.2 %copy-start.4 = (bf16[256,768]{1,0:T(8,128)(2,1)S(1)}, bf16[256,768]{1,0:T(8,128)(2,1)}, u32[]{:S(2)}) copy-start(bf16[256,768]{1,0:T(8,128)(2,1)} %constant.119.clone.inv_left) | copy-start | bytes 1179652
  11.2 1.4 %collective-permute-start.1 = (f32[32,896]{1,0:T(8,128)S(1)}, f32[32,896]{1,0:T(8,128)S(1)}, u32[]{:S(2)}, u32[]{:S(2)}) collective-permute-start(f32[32,896]{1,0:T(8,128)S(1)} %add.107.own), channel_id=1, source_target_pairs={{0,1},{1,0},{2,3},{3,2},{4,5},{5,4},{6,7},{7,6},{8,9},{9,8},{10,11... | collective-permute-start | bytes 344072 | tf_op jit(solution)/shard_map/ppermute | solution.py:277
  12.6 9.8 %copy-start.3 = (bf16[768,256]{1,0:T(8,128)(2,1)S(1)}, bf16[768,256]{1,0:T(8,128)(2,1)}, u32[]{:S(2)}) copy-start(bf16[768,256]{1,0:T(8,128)(2,1)} %constant.120.clone.inv_right) | copy-start | bytes 1179652
  12.7 9.8 %copy-start = (bf16[1,1,14,128,128]{4,3,2,1,0:T(8,128)(2,1)S(1)}, bf16[1,1,14,128,128]{4,3,2,1,0:T(8,128)(2,1)}, u32[]{:S(2)}) copy-start(bf16[1,1,14,128,128]{4,3,2,1,0:T(8,128)(2,1)} %param.13) | copy-start | bytes 1376260
  12.7 9.8 %copy-start.1 = (f32[2,128,128]{2,1,0:T(8,128)S(1)}, f32[2,128,128]{2,1,0:T(8,128)}, u32[]{:S(2)}) copy-start(f32[2,128,128]{2,1,0:T(8,128)} %probe.1) | copy-start | bytes 393220
  12.7 0.8 %collective-permute-start.2 = (f32[56,896]{1,0:T(8,128)S(1)}, f32[56,896]{1,0:T(8,128)S(1)}, u32[]{:S(2)}, u32[]{:S(2)}) collective-permute-start(f32[56,896]{1,0:T(8,128)S(1)} %maximum_select_fusion), channel_id=1, source_target_pairs={{1,2},{2,1},{3,4},{4,3},{5,6},{6,5},{7,8},{8,7},{9,10},{10,9},{11,... | collective-permute-start | bytes 602120 | tf_op jit(solution)/shard_map/ppermute | solution.py:277
  13.5 8.9 %collective-permute-start.3 = (f32[24,896]{1,0:T(8,128)S(1)}, f32[24,896]{1,0:T(8,128)S(1)}, u32[]{:S(2)}, u32[]{:S(2)}) collective-permute-start(f32[24,896]{1,0:T(8,128)S(1)} %slice_select_fusion.1), channel_id=1, source_target_pairs={{0,1},{1,0},{2,3},{3,2},{4,5},{5,4},{6,7},{7,6},{8,9},{9,8},{10,11... | collective-permute-start | bytes 258056 | tf_op jit(solution)/shard_map/ppermute | solution.py:277
  22.4 0.7 %copy-start.2 = (s32[2,1,1,14]{3,2,1,0:T(1,128)S(1)}, s32[2,1,1,14]{3,2,1,0:T(1,128)}, u32[]{:S(2)}) copy-start(s32[2,1,1,14]{3,2,1,0:T(1,128)} %param.14) | copy-start | bytes 340
  23.1 1.0 %copy-start.6 = (bf16[768,256]{1,0:T(8,128)(2,1)S(1)}, bf16[768,256]{1,0:T(8,128)(2,1)}, u32[]{:S(2)}) copy-start(bf16[768,256]{1,0:T(8,128)(2,1)} %constant.117.clone.fwd_right) | copy-start | bytes 1179652
  29.0 1.3 %collective-permute-start.4 = (f32[24,896]{1,0:T(8,128)S(1)}, f32[24,896]{1,0:T(8,128)S(1)}, u32[]{:S(2)}, u32[]{:S(2)}) collective-permute-start(f32[24,896]{1,0:T(8,128)S(1)} %get-tuple-element.13), channel_id=1, source_target_pairs={{0,1},{1,0},{2,3},{3,2},{4,5},{5,4},{6,7},{7,6},{8,9},{9,8},{10,11... | collective-permute-start | bytes 258056 | tf_op jit(solution)/shard_map/ppermute | solution.py:277
  30.4 0.7 %collective-permute-start.5 = (f32[56,896]{1,0:T(8,128)S(1)}, f32[56,896]{1,0:T(8,128)S(1)}, u32[]{:S(2)}, u32[]{:S(2)}) collective-permute-start(f32[56,896]{1,0:T(8,128)S(1)} %maximum_select_fusion.1), channel_id=1, source_target_pairs={{1,2},{2,1},{3,4},{4,3},{5,6},{6,5},{7,8},{8,7},{9,10},{10,9},{11,... | collective-permute-start | bytes 602120 | tf_op jit(solution)/shard_map/ppermute | solution.py:277
  31.2 24.0 %collective-permute-start.6 = (f32[32,896]{1,0:T(8,128)S(1)}, f32[32,896]{1,0:T(8,128)S(1)}, u32[]{:S(2)}, u32[]{:S(2)}) collective-permute-start(f32[32,896]{1,0:T(8,128)S(1)} %add_select_fusion), channel_id=1, source_target_pairs={{0,1},{1,0},{2,3},{3,2},{4,5},{5,4},{6,7},{7,6},{8,9},{9,8},{10,11... | collective-permute-start | bytes 344072 | tf_op jit(solution)/shard_map/ppermute | solution.py:277
  40.1 1.2 %collective-permute-start.8 = (f32[8,128]{1,0:T(8,128)S(1)}, f32[8,128]{1,0:T(8,128)S(1)}, u32[]{:S(2)}, u32[]{:S(2)}) collective-permute-start(f32[8,128]{1,0:T(8,128)S(1)} %get-tuple-element.5), channel_id=1, source_target_pairs={{0,1},{1,0},{2,3},{3,2},{4,5},{5,4},{6,7},{7,6},{8,9},{9,8},{10,11... | collective-permute-start | bytes 12296 | tf_op jit(solution)/shard_map/ppermute | solution.py:277
  41.3 4.1 %collective-permute-start.9 = (f32[8,128]{1,0:T(8,128)S(1)}, f32[8,128]{1,0:T(8,128)S(1)}, u32[]{:S(2)}, u32[]{:S(2)}) collective-permute-start(f32[8,128]{1,0:T(8,128)S(1)} %add.117), channel_id=1, source_target_pairs={{0,2},{1,3},{2,0},{3,1},{4,6},{5,7},{6,4},{7,5},{8,10},{9,11},{10,... | collective-permute-start | bytes 12296 | tf_op jit(solution)/shard_map/ppermute | solution.py:277
  45.4 3.6 %collective-permute-start.10 = (f32[8,128]{1,0:T(8,128)S(1)}, f32[8,128]{1,0:T(8,128)S(1)}, u32[]{:S(2)}, u32[]{:S(2)}) collective-permute-start(f32[8,128]{1,0:T(8,128)S(1)} %add.118), channel_id=1, source_target_pairs={{0,4},{1,5},{2,6},{3,7},{4,0},{5,1},{6,2},{7,3},{8,12},{9,13},{10,... | collective-permute-start | bytes 12296 | tf_op jit(solution)/shard_map/ppermute | solution.py:277
  49.0 4.6 %collective-permute-start.11 = (f32[8,128]{1,0:T(8,128)S(1)}, f32[8,128]{1,0:T(8,128)S(1)}, u32[]{:S(2)}, u32[]{:S(2)}) collective-permute-start(f32[8,128]{1,0:T(8,128)S(1)} %add.119), channel_id=1, source_target_pairs={{0,8},{1,9},{2,10},{3,11},{4,12},{5,13},{6,14},{7,15},{8,0},{9,1},... | collective-permute-start | bytes 12296 | tf_op jit(solution)/shard_map/ppermute | solution.py:277
  53.7 6.4 %copy-start.7 = (f32[1,2,32,896]{3,2,1,0:T(8,128)S(1)}, f32[1,2,32,896]{3,2,1,0:T(8,128)}, u32[]{:S(2)}) copy-start(f32[1,2,32,896]{3,2,1,0:T(8,128)} %param.10) | copy-start | bytes 688132
  53.7 3.6 %collective-permute-start.12 = (f32[8,128]{1,0:T(8,128)S(1)}, f32[8,128]{1,0:T(8,128)S(1)}, u32[]{:S(2)}, u32[]{:S(2)}) collective-permute-start(f32[8,128]{1,0:T(8,128)S(1)} %add.120), channel_id=1, source_target_pairs={{0,16},{16,0},{1,17},{17,1},{2,18},{18,2},{3,19},{19,3},{4,20},{20... | collective-permute-start | bytes 12296 | tf_op jit(solution)/shard_map/ppermute | solution.py:277
  55.2 4.9 %collective-permute-start.7 = (f32[32,896]{1,0:T(8,128)S(1)}, f32[32,896]{1,0:T(8,128)S(1)}, u32[]{:S(2)}, u32[]{:S(2)}) collective-permute-start(f32[32,896]{1,0:T(8,128)S(1)} %fusion.2), channel_id=1, source_target_pairs={{0,16},{16,0},{1,17},{17,1},{2,18},{18,2},{3,19},{19,3},{4,20},{20... | collective-permute-start | bytes 344072 | tf_op jit(solution)/shard_map/ppermute | solution.py:314

commit v2 on v1

--- a/solution.py
+++ b/solution.py
@@ -26,9 +26,7 @@
     table = np.block([[cos, sin], [-sin, cos]])
     high = table.astype(jnp.bfloat16)
     low = (table - high.astype(np.float64)).astype(jnp.bfloat16)
-    right = lambda h, l: np.concatenate([h, h, l], 0)
-    left = lambda h, l: np.concatenate([h, h, l], 1)
-    return right(high, low), left(high.T, low.T), left(high, low), right(high.T, low.T)
+    return np.stack([high, low, high.T, low.T])
 
 
 def sin_cos(x):
@@ -62,66 +60,138 @@
     return tile, corner - tile * LANES
 
 
+def terms_kernel(groups, slab, paths, jitter, steps, *outs):
+    terms, factors, scalars = outs[:groups], outs[groups], outs[groups + 1]
+    group = lax.axis_index("blk")
+    column = lax.axis_index("wide")
+    columns = lax.axis_size("wide")
+    layers, rows, _ = slab.shape
+    for step in range(groups):
+        angle = lax.rem(group + step, groups)
+        for r in range(0, rows, SUBS):
+            sums = slab[0, r : r + SUBS, :] * paths[angle, group, 0]
+            for layer in range(1, layers):
+                sums = sums + slab[layer, r : r + SUBS, :] * paths[angle, group, layer]
+            terms[step][r : r + SUBS, :] = sums
+        source = lax.rem(group - step + groups, groups)
+        for layer in range(layers):
+            factors[step, layer] = jnp.full((SUBS, LANES), steps[source] * paths[source, group, layer], jnp.float32)
+    number = jitter.shape[1]
+    for p in range(number):
+        scalars[0, p] = jitter[0, p]
+        scalars[1, p] = jitter[1, p]
+        scalars[2, p] = 0
+    scalars[2, 0] = lax.rem(column, 2)
+    scalars[2, 1] = lax.rem(column // 2, 2)
+    scalars[2, 2] = (column >= 2).astype(jnp.int32)
+    scalars[2, 3] = (column >= 1).astype(jnp.int32)
+    scalars[2, 4] = (column + 1 < columns).astype(jnp.int32)
+    scalars[2, 5] = (column + 2 < columns).astype(jnp.int32)
+
+
+def slab_terms(slab, paths, jitter, steps, groups):
+    layers, rows, cols = slab.shape
+    vmem = pl.BlockSpec(memory_space=pltpu.VMEM)
+    smem = pl.BlockSpec(memory_space=pltpu.SMEM)
+    f32 = jnp.float32
+    term = jax.ShapeDtypeStruct((rows, cols), f32)
+    out = pl.pallas_call(
+        functools.partial(terms_kernel, groups),
+        out_shape=[term] * groups
+        + [
+            jax.ShapeDtypeStruct((groups, layers, SUBS, LANES), f32),
+            jax.ShapeDtypeStruct((3, jitter.shape[1]), jnp.int32),
+        ],
+        in_specs=[vmem, smem, smem, smem],
+        out_specs=[vmem] * (groups + 1) + [smem],
+        name="terms",
+    )(slab, paths, jitter, steps)
+    return out[:groups], out[groups], out[groups + 1]
+
+
+def update_kernel(slab, factors, *refs):
+    grads, out = refs[:-1], refs[-1]
+    layers, rows, cols = slab.shape
+    for layer in range(layers):
+        for r in range(0, rows, SUBS):
+            for c in range(0, cols, LANES):
+                value = slab[layer, r : r + SUBS, c : c + LANES]
+                for step, grad in enumerate(grads):
+                    value = value - factors[step, layer] * grad[r : r + SUBS, c : c + LANES]
+                out[layer, r : r + SUBS, c : c + LANES] = value
+
+
+def updated(slab, factors, grads):
+    vmem = pl.BlockSpec(memory_space=pltpu.VMEM)
+    return pl.pallas_call(
+        update_kernel,
+        out_shape=jax.ShapeDtypeStruct(slab.shape, slab.dtype),
+        in_specs=[vmem] * (2 + len(grads)),
+        out_specs=vmem,
+        compiler_params=pltpu.CompilerParams(vmem_limit_bytes=8 * 1024 * 1024),
+        name="update",
+    )(slab, factors, *grads)
+
+
 def strip_kernel(
-    far,
-    jitter,
-    ends,
+    scalars,
     own,
     mate,
-    cross,
+    pair,
+    next_pair,
     relay,
     probe,
     measured,
-    fwd_right,
-    fwd_left,
-    inv_left,
-    inv_right,
-    grad,
-    misfit,
+    tables,
+    mine,
+    to_mate,
+    by_pair,
+    by_next,
     obj_real,
     obj_imag,
+    grad,
     wave,
     twice,
     mid,
     back,
 ):
     number, patch, _ = measured.shape
-    rows = own.shape[0]
-    tiles = own.shape[1] // LANES
+    rows, cols = own.shape
+    tiles = cols // LANES
+    far = rows - ROWS_DEV // 4
     near = ROWS_DEV // 4 + JIT
     dot = functools.partial(lax.dot, preferred_element_type=jnp.float32)
-
-    is_odd = ends[0] == 1
-    odd = jnp.full((SUBS, LANES), ends[0], jnp.int32) == 1
-    up2_ok = ends[1].astype(jnp.float32)
-    up1_ok = ends[2].astype(jnp.float32)
-    dn1_ok = ends[3].astype(jnp.float32)
-    dn2_ok = ends[4].astype(jnp.float32)
+    jitter = scalars
+
+    def flag(index):
+        return jnp.full((SUBS, cols), scalars[2, index], jnp.int32) == 1
+
+    is_second = flag(0)
+    is_lower = flag(1)
+    fwd_high, fwd_low, inv_high, inv_low = (tables[i] for i in range(4))
 
     for half in range(2):
         twice[0, half * patch : (half + 1) * patch, :] = probe[0]
         twice[1, half * patch : (half + 1) * patch, :] = probe[1]
 
-    def put(row, phase, ok):
+    def put(row, phase, index):
         s, c = sin_cos(phase)
-        if ok is not None:
+        if index is not None:
+            ok = scalars[2, index].astype(jnp.float32)
             s = s * ok
             c = c * ok
         obj_real[row : row + SUBS, :] = c
         obj_imag[row : row + SUBS, :] = s
 
     for r in range(0, rows, SUBS):
-        put(2 * rows + r, own[r : r + SUBS, :], None)
-    wide_odd = jnp.full((SUBS, own.shape[1]), ends[0], jnp.int32) == 1
-    for r in range(0, far, SUBS):
-        top = rows - far + r
-        put(top, jnp.where(wide_odd, relay[r : r + SUBS, :], cross[r : r + SUBS, :]), up2_ok)
-    for r in range(0, rows, SUBS):
-        put(rows + r, jnp.where(wide_odd, mate[r : r + SUBS, :], cross[far + r : far + r + SUBS, :]), up1_ok)
-    for r in range(0, rows, SUBS):
-        put(3 * rows + r, jnp.where(wide_odd, cross[r : r + SUBS, :], mate[r : r + SUBS, :]), dn1_ok)
-    for r in range(0, far, SUBS):
-        put(4 * rows + r, jnp.where(wide_odd, cross[rows + r : rows + r + SUBS, :], relay[r : r + SUBS, :]), dn2_ok)
+        part = slice(r, r + SUBS)
+        put(2 * rows + r, own[part, :], None)
+        put(rows + r, jnp.where(is_second, mate[part, :], relay[part, :]), 3)
+        put(3 * rows + r, jnp.where(is_second, relay[part, :], mate[part, :]), 4)
+        if r >= rows - far:
+            put(r, jnp.where(is_lower, pair[part, :], next_pair[part, :]), 2)
+        if r < far:
+            put(4 * rows + r, jnp.where(is_lower, next_pair[part, :], pair[part, :]), 5)
 
     lane = lax.broadcasted_iota(jnp.int32, (SUBS, LANES), 1)
     sub = lax.broadcasted_iota(jnp.int32, (SUBS, LANES), 0)
@@ -153,6 +223,12 @@
         if row < near:
             return jnp.where(below[k], at(row), at(row + patch))
         return at(row)
+
+    def against(high, low, t_high, t_low):
+        return dot(jnp.concatenate([high, low, high], 1), jnp.concatenate([t_high, t_high, t_low], 0))
+
+    def onto(t_high, t_low, high, low):
+        return dot(jnp.concatenate([t_high, t_high, t_low], 1), jnp.concatenate([high, low, high], 0))
 
     steps = patch // SUBS
     for p in range(number):
@@ -173,7 +249,7 @@
 
     for p in range(0, number, 2):
         high, low = parts_of(wave[p * patch : (p + 2) * patch, :])
-        mid[p * patch : (p + 2) * patch, :] = dot(jnp.concatenate([high, low, high], 1), fwd_right[...])
+        mid[p * patch : (p + 2) * patch, :] = against(high, low, fwd_high, fwd_low)
 
     def upright(value):
         top = jnp.concatenate([value[:patch, :LANES], value[patch:, :LANES]], 1)
@@ -183,7 +259,7 @@
     total = jnp.zeros((SUBS, LANES), jnp.float32)
     for p in range(0, number, 2):
         high, low = parts_of(upright(mid[p * patch : (p + 2) * patch, :]))
-        spectrum = dot(fwd_left[...], jnp.concatenate([high, low, high], 0))
+        spectrum = onto(inv_high, inv_low, high, low)
         real, imag = spectrum[:patch], spectrum[patch:]
         target = jnp.concatenate([measured[p], measured[p + 1]], 1).astype(jnp.float32)
         power = real * real + imag * imag
@@ -195,17 +271,18 @@
                 total += square[k * SUBS : (k + 1) * SUBS, half * LANES : (half + 1) * LANES]
         ratio = target * jnp.minimum(inverse, FLOOR_RATIO)
         high, low = parts_of(jnp.concatenate([ratio * real, ratio * imag], 0))
-        undone = dot(inv_left[...], jnp.concatenate([high, low, high], 0))
+        undone = onto(fwd_high, fwd_low, high, low)
         for half in range(2):
             row = (p + half) * patch
             lanes = slice(half * LANES, (half + 1) * LANES)
             back[row : row + patch, :LANES] = undone[:patch, lanes]
             back[row : row + patch, LANES:] = undone[patch:, lanes]
-    misfit[...] = total
+    to_mate[2 * rows : 2 * rows + SUBS, :] = jnp.zeros((SUBS, cols), jnp.float32)
+    to_mate[2 * rows : 2 * rows + SUBS, :LANES] = total
 
     for p in range(0, number, 2):
         high, low = parts_of(back[p * patch : (p + 2) * patch, :])
-        out = dot(jnp.concatenate([high, low, high], 1), inv_right[...])
+        out = against(high, low, inv_high, inv_low)
         w = wave[p * patch : (p + 2) * patch, :]
         mid[p * patch : (p + 2) * patch, :LANES] = w[:, :LANES] * out[:, LANES:] - w[:, LANES:] * out[:, :LANES]
 
@@ -240,22 +317,30 @@
         grad[row : row + SUBS, :] = jnp.zeros((SUBS, grad.shape[1]), jnp.float32)
 
 
-def strip_gradient(far, jitter, ends, own, mate, cross, relay, probe, measured):
+    for r in range(0, rows, SUBS):
+        part = slice(r, r + SUBS)
+        up2, up1, here, dn1, dn2 = (grad[k * rows + r : k * rows + r + SUBS, :] for k in range(5))
+        mine[part, :] = here
+        to_mate[part, :] = jnp.where(is_second, up1, dn1)
+        to_mate[rows + r : rows + r + SUBS, :] = jnp.where(is_second, dn1, up1)
+        by_pair[part, :] = jnp.where(is_lower, up2, dn2)
+        by_next[part, :] = jnp.where(is_lower, dn2, up2)
+
+
+def strip_gradient(scalars, own, mate, pair, next_pair, relay, probe, measured):
     number, patch, _ = measured.shape
     rows, cols = own.shape
-    tables = dft_tables(patch)
     vmem = pl.BlockSpec(memory_space=pltpu.VMEM)
     smem = pl.BlockSpec(memory_space=pltpu.SMEM)
     f32 = jnp.float32
+    row = jax.ShapeDtypeStruct((rows, cols), f32)
     return pl.pallas_call(
-        functools.partial(strip_kernel, far),
-        out_shape=(
-            jax.ShapeDtypeStruct((5 * rows, cols), f32),
-            jax.ShapeDtypeStruct((SUBS, LANES), f32),
-        ),
-        in_specs=[smem, smem] + [vmem] * 10,
-        out_specs=(vmem, vmem),
+        strip_kernel,
+        out_shape=(row, jax.ShapeDtypeStruct((2 * rows + SUBS, cols), f32), row, row),
+        in_specs=[smem] + [vmem] * 8,
+        out_specs=(vmem,) * 4,
         scratch_shapes=[
+            pltpu.VMEM((5 * rows, cols), f32),
             pltpu.VMEM((5 * rows, cols), f32),
             pltpu.VMEM((5 * rows, cols), f32),
             pltpu.VMEM((number * patch, 2 * LANES), f32),
@@ -268,7 +353,7 @@
             flops=24 * number * patch**3 * 4, bytes_accessed=4 * number * patch * patch, transcendentals=0
         ),
         name="strip",
-    )(jitter, ends, own, mate, cross, relay, probe, measured, *tables)
+    )(scalars, own, mate, pair, next_pair, relay, probe, measured, dft_tables(patch))
 
 
 def permuted(value, axis, target):
@@ -281,97 +366,59 @@
     return permuted(value, "wide", lambda i: i ^ 1)
 
 
-def across(value):
-    return permuted(value, "wide", lambda i: i + 1 if i % 2 else i - 1)
-
-
-def summed(value, axis):
-    count = lax.axis_size(axis)
-    if count & (count - 1):
-        return lax.psum(value, axis)
-    step = 1
-    while step < count:
+def with_pair(value):
+    return permuted(value, "wide", lambda i: i ^ 2)
+
+
+def to_next(value, back=False):
+    return permuted(value, "wide", lambda i: i + 4 if (i // 2 % 2 == 0) != back else i - 4)
+
+
+def joined(value, axis, steps):
+    for step in steps:
         value = value + permuted(value, axis, lambda i: i ^ step)
-        step *= 2
     return value
 
 
 def body(volume, path_lengths, probe, measured, jitter, step_sizes):
-    group = lax.axis_index("blk")
     groups = lax.axis_size("blk")
     column = lax.axis_index("wide")
     columns = lax.axis_size("wide")
     slab = volume[0]
     rows = slab.shape[1]
-    far = rows - ROWS_DEV // 4
-    own_paths = lax.dynamic_index_in_dim(path_lengths, group, 1, keepdims=False)
-
-    def slab_term(angle):
-        coeffs = lax.dynamic_index_in_dim(own_paths, angle, 0, keepdims=False)
-        return jnp.sum(coeffs[:, None, None] * slab, 0)
 
     def to_group(value, step):
         return lax.ppermute(value, "blk", [(i, (i + step) % groups) for i in range(groups)])
 
-    own = slab_term(group)
+    terms, factors, scalars = slab_terms(slab, path_lengths, jitter[:, 0, 0], step_sizes, groups)
+    own = terms[0]
     for step in range(1, groups):
-        own = own + to_group(slab_term((group + step) % groups), step)
-
-    odd = column % 2 == 1
+        own = own + to_group(terms[step], step)
+
+    even = column % 2 == column // 2 % 2
+    pair = with_pair(own)
     mate = with_mate(own)
-    cross = across(
-        jnp.where(
-            odd,
-            jnp.concatenate([mate[rows - far :], own], 0),
-            jnp.concatenate([own, mate[:far]], 0),
-        )
+    next_pair = to_next(pair)
+    relay = with_mate(jnp.where(even, pair, next_pair))
+    mine, to_mate, by_pair, by_next = strip_gradient(
+        scalars, own, mate, pair, next_pair, relay, probe, measured[0, 0]
     )
-    relay = with_mate(jnp.where(odd, cross[:far], cross[rows:]))
-    ends = jnp.stack(
-        [
-            column % 2,
-            (column >= 2).astype(jnp.int32),
-            (column >= 1).astype(jnp.int32),
-            (column + 1 < columns).astype(jnp.int32),
-            (column + 2 < columns).astype(jnp.int32),
-        ]
-    )
-    part, local = strip_gradient(
-        far, jitter[:, 0, 0], ends, own, mate, cross, relay, probe, measured[0, 0]
-    )
-    up2 = part[rows - far : rows]
-    up1 = part[rows : 2 * rows]
-    mine = part[2 * rows : 3 * rows]
-    dn1 = part[3 * rows : 4 * rows]
-    dn2 = part[4 * rows : 4 * rows + far]
-
-    def tail(value):
-        return jnp.pad(value, ((rows - far, 0), (0, 0)))
-
-    def head(value):
-        return jnp.pad(value, ((0, rows - far), (0, 0)))
-
-    got = with_mate(jnp.where(odd, up2, dn2))
-    met = across(
-        jnp.where(
-            odd,
-            jnp.concatenate([dn1 + head(got), dn2], 0),
-            jnp.concatenate([up2, up1 + tail(got)], 0),
-        )
-    )
-    last = with_mate(jnp.where(odd, up1 + tail(met[:far]), dn1 + head(met[rows:])))
-    gradient = mine + last + jnp.where(odd, met[far:], met[:rows])
-    total = jnp.sum(summed(summed(local, "wide"), "blk"))
-
-    def share(angle, grad):
-        coeffs = lax.dynamic_index_in_dim(own_paths, angle, 0, keepdims=False)
-        scale = lax.dynamic_index_in_dim(step_sizes, angle, 0, keepdims=False)
-        return (coeffs * scale)[:, None, None] * grad[None]
-
-    update = share(group, gradient)
-    for step in range(1, groups):
-        update = update + share((group - step) % groups, to_group(gradient, step))
-    return ((slab - update)[None], total)
+    got = with_mate(to_mate)
+    mine = mine + got[:rows]
+    passed = got[rows : 2 * rows]
+    local = to_mate[2 * rows :, :LANES] + got[2 * rows :, :LANES]
+    zero = jnp.zeros_like(passed)
+    arrived = to_next(by_next + jnp.where(even, zero, passed), back=True)
+    local = joined(local, "wide", [4])
+    arrived, local = lax.optimization_barrier((arrived, local))
+    gradient = mine + with_pair(by_pair + jnp.where(even, passed, zero) + arrived)
+    others = [2**k for k in range(1, columns.bit_length() - 1) if k != 2]
+    local = joined(local, "wide", others[1:])
+    gradient, local = lax.optimization_barrier((gradient, local))
+    grads = [gradient] + [to_group(gradient, step) for step in range(1, groups)]
+    local = joined(local, "wide", others[:1])
+    local = joined(local, "blk", [2**k for k in range(groups.bit_length() - 1)])
+    return (updated(slab, factors, grads)[None], jnp.sum(local))
 
 
 def solution(mesh):

time: 61.1 us -> 54.7 us (0.90)
  starting transfers between devices: 31.6 us -> 20 us
  waiting for transfers between devices: 15.7 us -> 23.7 us
  local copies, waits for them, and re-layouts: 3.7 us -> 1.06 us
  other arithmetic: 4 us -> 1.6 us
  Pallas kernels: 4.9 us -> 7.3 us
    ppermute x11, starting transfers between devices: 28 us -> 16.4 us  [permuted(): return lax.ppermute(value, axis, pairs)]
    ppermute x11, waiting for transfers between devices: 10.4 us -> 18.2 us  [permuted(): return lax.ppermute(value, axis, pairs)]
    pallas_call x1 -> x3, Pallas kernels: 4.9 us -> 7.3 us  [the longest x1 4.83 us: strip_gradient(): pl.pallas_call(strip_kernel, out_shape=(row, jax.ShapeDtypeStruct((2 * ro...]
    unnamed x20 -> x12, local copies, waits for them, and re-layouts: 3 us -> 1.06 us
    mul x2 -> x0, other arithmetic: 1.31 us -> none  [share(): return (coeffs * scale)[:, None, None] * grad[None]]
    reduce_sum x2 -> x1, other arithmetic: 1.71 us -> 0.6 us  [body(): return (updated(slab, factors, grads)[None], jnp.sum(local))]
    add x7 -> x8, other arithmetic: 0.08 us -> 0.99 us  [the longest x1 0.91 us: body(): own = own + to_group(terms[step], step)]
    sub x1 -> x0, other arithmetic: 0.79 us -> none  [body(): return ((slab - update)[None], total)]
where the time goes in v2:
time: 54.7 us; the launch traced here: 54.4 us
  waiting for transfers between devices  23.7 us (43%)
  starting transfers between devices  20 us (37%)
  Pallas kernels  7.3 us (13%)
  other arithmetic  1.6 us (3%)
  local copies, waits for them, and re-layouts  1.06 us (2%)
  between operations  0.8 us (1%)
    ppermute x11, waiting for transfers between devices, permuted(): return lax.ppermute(value, axis, pairs)  18.2 us
    ppermute x11, starting transfers between devices, permuted(): return lax.ppermute(value, axis, pairs)  16.4 us
    ppermute x2, waiting for transfers between devices, to_group(): lax.ppermute(value, 'blk', [(i, (i + step) % groups) for i in range(group...  5.42 us
    pallas_call x1, Pallas kernels, strip_gradient(): pl.pallas_call(strip_kernel, out_shape=(row, jax.ShapeDtypeStruct((2 * ro...  4.83 us
    ppermute x2, starting transfers between devices, to_group(): lax.ppermute(value, 'blk', [(i, (i + step) % groups) for i in range(group...  3.58 us
    pallas_call x1, Pallas kernels, slab_terms(): pl.pallas_call(functools.partial(terms_kernel, groups), out_shape=[term]...  1.74 us
  transfers between devices with their start and end apart: 13, of which 10 were waited for; matrix products, arithmetic and copies ran while one was open for 1% of the time, Pallas kernels for 0%

profile of v2, /device:TPU:0, one launch (start us, length us, event | category | flops | bytes accessed | tf_op | source)
XLA Modules:
  0.0 54.4 jit_solution(10643778506318310926)
XLA Ops:
  0.6 1.7 %terms.1 = (f32[32,896]{1,0:T(8,128)}, f32[32,896]{1,0:T(8,128)}, f32[2,2,8,128]{3,2,1,0:T(8,128)}, s32[3,14]{1,0:T(4,128)}) custom-call(f32[2,32,896]{2,1,0:T(8,128)} %bitcast.4, f32[2,2,2]{2,1,0:T(2,128)} %paths.1, s32[2,14]{1,0:T(2,128)} %bitcast.8, f32[2]{0:T(128)} %steps.1), custom_call_target="tpu_custom_call" | custom-call | tf_op jit(solution)/shard_map/terms/pallas_call | solution.py:98
  2.4 3.0 %collective-permute-start = (f32[32,896]{1,0:T(8,128)}, f32[32,896]{1,0:T(8,128)S(1)}, u32[]{:S(2)}, u32[]{:S(2)}) collective-permute-start(f32[32,896]{1,0:T(8,128)} %get-tuple-element.17), channel_id=1, source_target_pairs={{0,16},{16,0},{1,17},{17,1},{2,18},{18,2},{3,19},{19,3},{4,20},{20... | collective-permute-start | bytes 344072 | tf_op jit(solution)/shard_map/ppermute | solution.py:391
  5.4 3.4 %collective-permute-done = f32[32,896]{1,0:T(8,128)S(1)} collective-permute-done((f32[32,896]{1,0:T(8,128)}, f32[32,896]{1,0:T(8,128)S(1)}, u32[]{:S(2)}, u32[]{:S(2)}) %collective-permute-start) | collective-permute-done | bytes 114720 | tf_op jit(solution)/shard_map/ppermute | solution.py:391
  8.8 0.9 %add.41.own = f32[32,896]{1,0:T(8,128)S(1)} add(f32[32,896]{1,0:T(8,128)} %get-tuple-element.16, f32[32,896]{1,0:T(8,128)S(1)} %collective-permute-done) | non-fusion elementwise | flops 28672 | bytes 344064 | tf_op jit(solution)/shard_map/add | solution.py:396
  9.7 1.8 %collective-permute-start.2 = (f32[32,896]{1,0:T(8,128)S(1)}, f32[32,896]{1,0:T(8,128)S(1)}, u32[]{:S(2)}, u32[]{:S(2)}) collective-permute-start(f32[32,896]{1,0:T(8,128)S(1)} %add.41.own), channel_id=1, source_target_pairs={{0,2},{1,3},{2,0},{3,1},{4,6},{5,7},{6,4},{7,5},{8,10},{9,11},{10,... | collective-permute-start | bytes 344072 | tf_op jit(solution)/shard_map/ppermute | solution.py:362
  11.5 3.0 %collective-permute-done.2.pair = f32[32,896]{1,0:T(8,128)S(1)} collective-permute-done((f32[32,896]{1,0:T(8,128)S(1)}, f32[32,896]{1,0:T(8,128)S(1)}, u32[]{:S(2)}, u32[]{:S(2)}) %collective-permute-start.2) | collective-permute-done | bytes 114720 | tf_op jit(solution)/shard_map/ppermute | solution.py:362
  14.6 3.7 %collective-permute-start.3 = (f32[32,896]{1,0:T(8,128)S(1)}, f32[32,896]{1,0:T(8,128)S(1)}, u32[]{:S(2)}, u32[]{:S(2)}) collective-permute-start(f32[32,896]{1,0:T(8,128)S(1)} %collective-permute-done.2.pair), channel_id=1, source_target_pairs={{0,4},{1,5},{4,8},{5,9},{6,2},{7,3},{8,12},{9,13},{10,6},{11,7},{1... | collective-permute-start | bytes 344072 | tf_op jit(solution)/shard_map/ppermute | solution.py:362
  18.4 2.2 %collective-permute-done.3.next_pair = f32[32,896]{1,0:T(8,128)S(1)} collective-permute-done((f32[32,896]{1,0:T(8,128)S(1)}, f32[32,896]{1,0:T(8,128)S(1)}, u32[]{:S(2)}, u32[]{:S(2)}) %collective-permute-start.3) | collective-permute-done | bytes 114720 | tf_op jit(solution)/shard_map/ppermute | solution.py:362
  20.7 1.3 %collective-permute-done.4.relay = f32[32,896]{1,0:T(8,128)S(1)} collective-permute-done((f32[32,896]{1,0:T(8,128)S(1)}, f32[32,896]{1,0:T(8,128)S(1)}, u32[]{:S(2)}, u32[]{:S(2)}) %collective-permute-start.4) | collective-permute-done | bytes 114720 | tf_op jit(solution)/shard_map/ppermute | solution.py:362
  22.1 1.0 %copy-done.5 = bf16[4,256,256]{2,1,0:T(8,128)(2,1)S(1)} copy-done((bf16[4,256,256]{2,1,0:T(8,128)(2,1)S(1)}, bf16[4,256,256]{2,1,0:T(8,128)(2,1)}, u32[]{:S(2)}) %copy-start.5) | copy-done | bytes 524312
  23.1 4.8 %strip.1 = (f32[32,896]{1,0:T(8,128)S(1)}, f32[72,896]{1,0:T(8,128)S(1)}, f32[32,896]{1,0:T(8,128)S(1)}, f32[32,896]{1,0:T(8,128)S(1)}) custom-call(s32[3,14]{1,0:T(4,128)S(1)} %copy-done.4, f32[32,896]{1,0:T(8,128)S(1)} %add.41.own, f32[32,896]{1,0:T(8,128)S(1)} %collective-permute-done.1.mate, f32[32,896]{1,0:T(8,128)S(1)} %collective-permute-done.2.pair, ...), custom_call_target="tpu_custom_call" | custom-call | flops 2818572288 | bytes 917504 | tf_op jit(solution)/shard_map/strip/pallas_call | solution.py:337
  28.1 1.4 %collective-permute-done.5 = f32[72,896]{1,0:T(8,128)S(1)} collective-permute-done((f32[72,896]{1,0:T(8,128)S(1)}, f32[72,896]{1,0:T(8,128)S(1)}, u32[]{:S(2)}, u32[]{:S(2)}) %collective-permute-start.5) | collective-permute-done | bytes 258080 | tf_op jit(solution)/shard_map/ppermute | solution.py:362
  29.6 1.3 %collective-permute-start.6 = (f32[32,896]{1,0:T(8,128)S(1)}, f32[32,896]{1,0:T(8,128)S(1)}, u32[]{:S(2)}, u32[]{:S(2)}) collective-permute-start(f32[32,896]{1,0:T(8,128)S(1)} %select_add_fusion), channel_id=1, source_target_pairs={{2,6},{3,7},{4,0},{5,1},{6,10},{7,11},{8,4},{9,5},{10,14},{11,15},... | collective-permute-start | bytes 344072 | tf_op jit(solution)/shard_map/ppermute | solution.py:362
  30.9 3.1 %collective-permute-start.7 = (f32[8,128]{1,0:T(8,128)S(1)}, f32[8,128]{1,0:T(8,128)S(1)}, u32[]{:S(2)}, u32[]{:S(2)}) collective-permute-start(f32[8,128]{1,0:T(8,128)S(1)} %slice_add_fusion.1), channel_id=1, source_target_pairs={{0,4},{1,5},{2,6},{3,7},{4,0},{5,1},{6,2},{7,3},{8,12},{9,13},{10,... | collective-permute-start | bytes 12296 | tf_op jit(solution)/shard_map/ppermute | solution.py:362
  34.0 3.4 %collective-permute-done.7 = f32[8,128]{1,0:T(8,128)S(1)} collective-permute-done((f32[8,128]{1,0:T(8,128)S(1)}, f32[8,128]{1,0:T(8,128)S(1)}, u32[]{:S(2)}, u32[]{:S(2)}) %collective-permute-start.7) | collective-permute-done | bytes 4128 | tf_op jit(solution)/shard_map/ppermute | solution.py:362
  37.5 1.7 %collective-permute-start.8 = (f32[32,896]{1,0:T(8,128)S(1)}, f32[32,896]{1,0:T(8,128)S(1)}, u32[]{:S(2)}, u32[]{:S(2)}) collective-permute-start(f32[32,896]{1,0:T(8,128)S(1)} %add_add_fusion), channel_id=1, source_target_pairs={{0,2},{1,3},{2,0},{3,1},{4,6},{5,7},{6,4},{7,5},{8,10},{9,11},{10,... | collective-permute-start | bytes 344072 | tf_op jit(solution)/shard_map/ppermute | solution.py:362
  39.2 2.5 %collective-permute-start.9 = (f32[8,128]{1,0:T(8,128)S(1)}, f32[8,128]{1,0:T(8,128)S(1)}, u32[]{:S(2)}, u32[]{:S(2)}) collective-permute-start(f32[8,128]{1,0:T(8,128)S(1)} %add.48), channel_id=1, source_target_pairs={{0,8},{1,9},{2,10},{3,11},{4,12},{5,13},{6,14},{7,15},{8,0},{9,1},... | collective-permute-start | bytes 12296 | tf_op jit(solution)/shard_map/ppermute | solution.py:362
  41.7 2.0 %collective-permute-done.9 = f32[8,128]{1,0:T(8,128)S(1)} collective-permute-done((f32[8,128]{1,0:T(8,128)S(1)}, f32[8,128]{1,0:T(8,128)S(1)}, u32[]{:S(2)}, u32[]{:S(2)}) %collective-permute-start.9) | collective-permute-done | bytes 4128 | tf_op jit(solution)/shard_map/ppermute | solution.py:362
  44.2 3.3 %collective-permute-done.11 = f32[8,128]{1,0:T(8,128)S(1)} collective-permute-done((f32[8,128]{1,0:T(8,128)S(1)}, f32[8,128]{1,0:T(8,128)S(1)}, u32[]{:S(2)}, u32[]{:S(2)}) %collective-permute-start.11) | collective-permute-done | bytes 4128 | tf_op jit(solution)/shard_map/ppermute | solution.py:362
  47.4 1.5 %collective-permute-start.12 = (f32[8,128]{1,0:T(8,128)S(1)}, f32[8,128]{1,0:T(8,128)S(1)}, u32[]{:S(2)}, u32[]{:S(2)}) collective-permute-start(f32[8,128]{1,0:T(8,128)S(1)} %add.52), channel_id=1, source_target_pairs={{0,16},{16,0},{1,17},{17,1},{2,18},{18,2},{3,19},{19,3},{4,20},{20... | collective-permute-start | bytes 12296 | tf_op jit(solution)/shard_map/ppermute | solution.py:362
  49.5 1.6 %collective-permute-done.12 = f32[8,128]{1,0:T(8,128)S(1)} collective-permute-done((f32[8,128]{1,0:T(8,128)S(1)}, f32[8,128]{1,0:T(8,128)S(1)}, u32[]{:S(2)}, u32[]{:S(2)}) %collective-permute-start.12) | collective-permute-done | bytes 4128 | tf_op jit(solution)/shard_map/ppermute | solution.py:362
  51.0 0.6 %add_reduce_fusion = f32[]{:T(128)} fusion(f32[8,128]{1,0:T(8,128)S(1)} %add.52, f32[8,128]{1,0:T(8,128)S(1)} %collective-permute-done.12), kind=kLoop, calls=%fused_computation.6 | loop fusion | flops 2047 | bytes 8196 | tf_op jit(solution)/shard_map/reduce_sum | solution.py:421
  51.6 2.1 %collective-permute-done.10.refs_1_ = f32[32,896]{1,0:T(8,128)S(1)} collective-permute-done((f32[32,896]{1,0:T(8,128)S(1)}, f32[32,896]{1,0:T(8,128)S(1)}, u32[]{:S(2)}, u32[]{:S(2)}) %collective-permute-start.10) | collective-permute-done | bytes 114720 | tf_op jit(solution)/shard_map/ppermute | solution.py:391
  53.7 0.7 %update.1 = f32[2,32,896]{2,1,0:T(8,128)} custom-call(f32[2,32,896]{2,1,0:T(8,128)S(1)} %bitcast.5, f32[2,2,8,128]{3,2,1,0:T(8,128)S(1)} %copy-done.1, f32[32,896]{1,0:T(8,128)S(1)} %fusion.refs_0_, f32[32,896]{1,0:T(8,128)S(1)} %collective-permute-done.10.refs_1_), custom_call_target="tpu_custom_call" | custom-call | tf_op jit(solution)/shard_map/update/pallas_call | solution.py:126
  (27 shorter events, 1.4 us)
Async XLA Ops:
  0.6 21.4 %copy-start.2 = (bf16[1,1,14,128,128]{4,3,2,1,0:T(8,128)(2,1)S(1)}, bf16[1,1,14,128,128]{4,3,2,1,0:T(8,128)(2,1)}, u32[]{:S(2)}) copy-start(bf16[1,1,14,128,128]{4,3,2,1,0:T(8,128)(2,1)} %param.10) | copy-start | bytes 1376260
  2.4 6.4 %collective-permute-start = (f32[32,896]{1,0:T(8,128)}, f32[32,896]{1,0:T(8,128)S(1)}, u32[]{:S(2)}, u32[]{:S(2)}) collective-permute-start(f32[32,896]{1,0:T(8,128)} %get-tuple-element.17), channel_id=1, source_target_pairs={{0,16},{16,0},{1,17},{17,1},{2,18},{18,2},{3,19},{19,3},{4,20},{20... | collective-permute-start | bytes 344072 | tf_op jit(solution)/shard_map/ppermute | solution.py:391
  9.7 4.9 %collective-permute-start.2 = (f32[32,896]{1,0:T(8,128)S(1)}, f32[32,896]{1,0:T(8,128)S(1)}, u32[]{:S(2)}, u32[]{:S(2)}) collective-permute-start(f32[32,896]{1,0:T(8,128)S(1)} %add.41.own), channel_id=1, source_target_pairs={{0,2},{1,3},{2,0},{3,1},{4,6},{5,7},{6,4},{7,5},{8,10},{9,11},{10,... | collective-permute-start | bytes 344072 | tf_op jit(solution)/shard_map/ppermute | solution.py:362
  14.6 6.1 %collective-permute-start.3 = (f32[32,896]{1,0:T(8,128)S(1)}, f32[32,896]{1,0:T(8,128)S(1)}, u32[]{:S(2)}, u32[]{:S(2)}) collective-permute-start(f32[32,896]{1,0:T(8,128)S(1)} %collective-permute-done.2.pair), channel_id=1, source_target_pairs={{0,4},{1,5},{4,8},{5,9},{6,2},{7,3},{8,12},{9,13},{10,6},{11,7},{1... | collective-permute-start | bytes 344072 | tf_op jit(solution)/shard_map/ppermute | solution.py:362
  18.3 3.7 %copy-start.3 = (f32[2,128,128]{2,1,0:T(8,128)S(1)}, f32[2,128,128]{2,1,0:T(8,128)}, u32[]{:S(2)}) copy-start(f32[2,128,128]{2,1,0:T(8,128)} %probe.1) | copy-start | bytes 393220
  18.3 2.4 %collective-permute-start.1 = (f32[32,896]{1,0:T(8,128)S(1)}, f32[32,896]{1,0:T(8,128)S(1)}, u32[]{:S(2)}, u32[]{:S(2)}) collective-permute-start(f32[32,896]{1,0:T(8,128)S(1)} %add.41.own), channel_id=1, source_target_pairs={{0,1},{1,0},{2,3},{3,2},{4,5},{5,4},{6,7},{7,6},{8,9},{9,8},{10,11... | collective-permute-start | bytes 344072 | tf_op jit(solution)/shard_map/ppermute | solution.py:362
  20.6 1.4 %copy-start.4 = (s32[3,14]{1,0:T(4,128)S(1)}, s32[3,14]{1,0:T(4,128)}, u32[]{:S(2)}) copy-start(s32[3,14]{1,0:T(4,128)} %get-tuple-element.15.scalars) | copy-start | bytes 508
  20.7 1.4 %collective-permute-start.4 = (f32[32,896]{1,0:T(8,128)S(1)}, f32[32,896]{1,0:T(8,128)S(1)}, u32[]{:S(2)}, u32[]{:S(2)}) collective-permute-start(f32[32,896]{1,0:T(8,128)S(1)} %broadcast_select_fusion), channel_id=1, source_target_pairs={{0,1},{1,0},{2,3},{3,2},{4,5},{5,4},{6,7},{7,6},{8,9},{9,8},{10,11... | collective-permute-start | bytes 344072 | tf_op jit(solution)/shard_map/ppermute | solution.py:362
  22.1 1.0 %copy-start.5 = (bf16[4,256,256]{2,1,0:T(8,128)(2,1)S(1)}, bf16[4,256,256]{2,1,0:T(8,128)(2,1)}, u32[]{:S(2)}) copy-start(bf16[4,256,256]{2,1,0:T(8,128)(2,1)} %constant.37.clone.tables) | copy-start | bytes 1572868
  27.9 1.6 %collective-permute-start.5 = (f32[72,896]{1,0:T(8,128)S(1)}, f32[72,896]{1,0:T(8,128)S(1)}, u32[]{:S(2)}, u32[]{:S(2)}) collective-permute-start(f32[72,896]{1,0:T(8,128)S(1)} %get-tuple-element.19), channel_id=1, source_target_pairs={{0,1},{1,0},{2,3},{3,2},{4,5},{5,4},{6,7},{7,6},{8,9},{9,8},{10,11... | collective-permute-start | bytes 774152 | tf_op jit(solution)/shard_map/ppermute | solution.py:362
  29.6 7.9 %collective-permute-start.6 = (f32[32,896]{1,0:T(8,128)S(1)}, f32[32,896]{1,0:T(8,128)S(1)}, u32[]{:S(2)}, u32[]{:S(2)}) collective-permute-start(f32[32,896]{1,0:T(8,128)S(1)} %select_add_fusion), channel_id=1, source_target_pairs={{2,6},{3,7},{4,0},{5,1},{6,10},{7,11},{8,4},{9,5},{10,14},{11,15},... | collective-permute-start | bytes 344072 | tf_op jit(solution)/shard_map/ppermute | solution.py:362
  30.9 6.6 %collective-permute-start.7 = (f32[8,128]{1,0:T(8,128)S(1)}, f32[8,128]{1,0:T(8,128)S(1)}, u32[]{:S(2)}, u32[]{:S(2)}) collective-permute-start(f32[8,128]{1,0:T(8,128)S(1)} %slice_add_fusion.1), channel_id=1, source_target_pairs={{0,4},{1,5},{2,6},{3,7},{4,0},{5,1},{6,2},{7,3},{8,12},{9,13},{10,... | collective-permute-start | bytes 12296 | tf_op jit(solution)/shard_map/ppermute | solution.py:362
  37.5 6.3 %collective-permute-start.8 = (f32[32,896]{1,0:T(8,128)S(1)}, f32[32,896]{1,0:T(8,128)S(1)}, u32[]{:S(2)}, u32[]{:S(2)}) collective-permute-start(f32[32,896]{1,0:T(8,128)S(1)} %add_add_fusion), channel_id=1, source_target_pairs={{0,2},{1,3},{2,0},{3,1},{4,6},{5,7},{6,4},{7,5},{8,10},{9,11},{10,... | collective-permute-start | bytes 344072 | tf_op jit(solution)/shard_map/ppermute | solution.py:362
  39.2 4.5 %collective-permute-start.9 = (f32[8,128]{1,0:T(8,128)S(1)}, f32[8,128]{1,0:T(8,128)S(1)}, u32[]{:S(2)}, u32[]{:S(2)}) collective-permute-start(f32[8,128]{1,0:T(8,128)S(1)} %add.48), channel_id=1, source_target_pairs={{0,8},{1,9},{2,10},{3,11},{4,12},{5,13},{6,14},{7,15},{8,0},{9,1},... | collective-permute-start | bytes 12296 | tf_op jit(solution)/shard_map/ppermute | solution.py:362
  43.7 10.0 %copy-start = (f32[1,2,32,896]{3,2,1,0:T(8,128)S(1)}, f32[1,2,32,896]{3,2,1,0:T(8,128)}, u32[]{:S(2)}) copy-start(f32[1,2,32,896]{3,2,1,0:T(8,128)} %param.7) | copy-start | bytes 688132
  43.7 10.0 %copy-start.1 = (f32[2,2,8,128]{3,2,1,0:T(8,128)S(1)}, f32[2,2,8,128]{3,2,1,0:T(8,128)}, u32[]{:S(2)}) copy-start(f32[2,2,8,128]{3,2,1,0:T(8,128)} %get-tuple-element.14.factors) | copy-start | bytes 49156
  43.8 3.7 %collective-permute-start.11 = (f32[8,128]{1,0:T(8,128)S(1)}, f32[8,128]{1,0:T(8,128)S(1)}, u32[]{:S(2)}, u32[]{:S(2)}) collective-permute-start(f32[8,128]{1,0:T(8,128)S(1)} %add.51), channel_id=1, source_target_pairs={{0,2},{1,3},{2,0},{3,1},{4,6},{5,7},{6,4},{7,5},{8,10},{9,11},{10,... | collective-permute-start | bytes 12296 | tf_op jit(solution)/shard_map/ppermute | solution.py:362
  47.4 3.6 %collective-permute-start.12 = (f32[8,128]{1,0:T(8,128)S(1)}, f32[8,128]{1,0:T(8,128)S(1)}, u32[]{:S(2)}, u32[]{:S(2)}) collective-permute-start(f32[8,128]{1,0:T(8,128)S(1)} %add.52), channel_id=1, source_target_pairs={{0,16},{16,0},{1,17},{17,1},{2,18},{18,2},{3,19},{19,3},{4,20},{20... | collective-permute-start | bytes 12296 | tf_op jit(solution)/shard_map/ppermute | solution.py:362
  48.9 4.8 %collective-permute-start.10 = (f32[32,896]{1,0:T(8,128)S(1)}, f32[32,896]{1,0:T(8,128)S(1)}, u32[]{:S(2)}, u32[]{:S(2)}) collective-permute-start(f32[32,896]{1,0:T(8,128)S(1)} %fusion.refs_0_), channel_id=1, source_target_pairs={{0,16},{16,0},{1,17},{17,1},{2,18},{18,2},{3,19},{19,3},{4,20},{20... | collective-permute-start | bytes 344072 | tf_op jit(solution)/shard_map/ppermute | solution.py:391

commit v3 on v2

--- a/solution.py
+++ b/solution.py
@@ -60,24 +60,55 @@
     return tile, corner - tile * LANES
 
 
-def terms_kernel(groups, slab, paths, jitter, steps, *outs):
-    terms, factors, scalars = outs[:groups], outs[groups], outs[groups + 1]
+def term_of(slab, paths, angle, group, row):
+    part = slab[0, row : row + SUBS, :] * paths[angle, group, 0]
+    for layer in range(1, slab.shape[0]):
+        part = part + slab[layer, row : row + SUBS, :] * paths[angle, group, layer]
+    return part
+
+
+def terms_kernel(slab_hbm, paths_hbm, *refs):
+    terms = refs[:-3]
+    slab, paths, sems = refs[-3:]
+    groups = len(terms) + 1
+    group = lax.axis_index("blk")
+    copies = [
+        pltpu.make_async_copy(slab_hbm, slab, sems.at[0]),
+        pltpu.make_async_copy(paths_hbm, paths, sems.at[1]),
+    ]
+    for copy in copies:
+        copy.start()
+    for copy in copies:
+        copy.wait()
+    for step, term in enumerate(terms):
+        angle = lax.rem(group + step + 1, groups)
+        for r in range(0, slab.shape[1], SUBS):
+            term[r : r + SUBS, :] = term_of(slab, paths, angle, group, r)
+
+
+def slab_terms(slab, paths, groups):
+    _, rows, cols = slab.shape
+    f32 = jnp.float32
+    return pl.pallas_call(
+        terms_kernel,
+        out_shape=[jax.ShapeDtypeStruct((rows, cols), f32)] * (groups - 1),
+        in_specs=[pl.BlockSpec(memory_space=pltpu.HBM)] * 2,
+        out_specs=[pl.BlockSpec(memory_space=pltpu.VMEM)] * (groups - 1),
+        scratch_shapes=[
+            pltpu.VMEM(slab.shape, f32),
+            pltpu.SMEM(paths.shape, f32),
+            pltpu.SemaphoreType.DMA((2,)),
+        ],
+        name="terms",
+    )(slab, paths)
+
+
+def own_kernel(groups, slab, paths, jitter, steps, term, factors, scalars):
     group = lax.axis_index("blk")
     column = lax.axis_index("wide")
     columns = lax.axis_size("wide")
     layers, rows, _ = slab.shape
-    for step in range(groups):
-        angle = lax.rem(group + step, groups)
-        for r in range(0, rows, SUBS):
-            sums = slab[0, r : r + SUBS, :] * paths[angle, group, 0]
-            for layer in range(1, layers):
-                sums = sums + slab[layer, r : r + SUBS, :] * paths[angle, group, layer]
-            terms[step][r : r + SUBS, :] = sums
-        source = lax.rem(group - step + groups, groups)
-        for layer in range(layers):
-            factors[step, layer] = jnp.full((SUBS, LANES), steps[source] * paths[source, group, layer], jnp.float32)
-    number = jitter.shape[1]
-    for p in range(number):
+    for p in range(jitter.shape[1]):
         scalars[0, p] = jitter[0, p]
         scalars[1, p] = jitter[1, p]
         scalars[2, p] = 0
@@ -87,26 +118,32 @@
     scalars[2, 3] = (column >= 1).astype(jnp.int32)
     scalars[2, 4] = (column + 1 < columns).astype(jnp.int32)
     scalars[2, 5] = (column + 2 < columns).astype(jnp.int32)
-
-
-def slab_terms(slab, paths, jitter, steps, groups):
+    for step in range(groups):
+        source = lax.rem(group - step + groups, groups)
+        for layer in range(layers):
+            factors[step, layer] = jnp.full((SUBS, LANES), steps[source] * paths[source, group, layer], jnp.float32)
+    for r in range(0, rows, SUBS):
+        term[r : r + SUBS, :] = term_of(slab, paths, group, group, r)
+
+
+def own_term(slab, paths, jitter, steps, groups):
     layers, rows, cols = slab.shape
     vmem = pl.BlockSpec(memory_space=pltpu.VMEM)
     smem = pl.BlockSpec(memory_space=pltpu.SMEM)
     f32 = jnp.float32
-    term = jax.ShapeDtypeStruct((rows, cols), f32)
-    out = pl.pallas_call(
-        functools.partial(terms_kernel, groups),
-        out_shape=[term] * groups
-        + [
+    return pl.pallas_call(
+        functools.partial(own_kernel, groups),
+        out_shape=(
+            jax.ShapeDtypeStruct((rows, cols), f32),
             jax.ShapeDtypeStruct((groups, layers, SUBS, LANES), f32),
             jax.ShapeDtypeStruct((3, jitter.shape[1]), jnp.int32),
-        ],
+        ),
         in_specs=[vmem, smem, smem, smem],
-        out_specs=[vmem] * (groups + 1) + [smem],
-        name="terms",
+        out_specs=(vmem, vmem, smem),
+        compiler_params=pltpu.CompilerParams(vmem_limit_bytes=8 * 1024 * 1024),
+        cost_estimate=pl.CostEstimate(flops=2**24, bytes_accessed=2**20, transcendentals=0),
+        name="own",
     )(slab, paths, jitter, steps)
-    return out[:groups], out[groups], out[groups + 1]
 
 
 def update_kernel(slab, factors, *refs):
@@ -121,6 +158,41 @@
                 out[layer, r : r + SUBS, c : c + LANES] = value
 
 
+def prepare_kernel(number, scalars, probe, tables, rolled, kept, twice):
+    patch = probe.shape[1]
+    for half in range(2):
+        for part in range(2):
+            twice[part, half * patch : (half + 1) * patch, :] = probe[part]
+    for p in range(number):
+        _, corner = window_place(p, patch)
+        shift = corner + scalars[1, p]
+        start = patch - ROWS_DEV // 4 - scalars[0, p]
+        for part in range(2):
+            value = pltpu.roll(twice[part, pl.ds(start, patch), :], shift, 1)
+            rolled[p * patch : (p + 1) * patch, part * LANES : (part + 1) * LANES] = value
+    for i in range(tables.shape[0]):
+        kept[i] = tables[i]
+
+
+def prepared(scalars, probe):
+    number, patch = scalars.shape[1], probe.shape[1]
+    tables = dft_tables(patch)
+    vmem = pl.BlockSpec(memory_space=pltpu.VMEM)
+    return pl.pallas_call(
+        functools.partial(prepare_kernel, number),
+        out_shape=(
+            jax.ShapeDtypeStruct((number * patch, 2 * LANES), jnp.float32),
+            jax.ShapeDtypeStruct(tables.shape, tables.dtype),
+        ),
+        in_specs=[pl.BlockSpec(memory_space=pltpu.SMEM), vmem, vmem],
+        out_specs=(vmem, vmem),
+        scratch_shapes=[pltpu.VMEM((2, 2 * patch, patch), jnp.float32)],
+        compiler_params=pltpu.CompilerParams(vmem_limit_bytes=16 * 1024 * 1024),
+        cost_estimate=pl.CostEstimate(flops=2**27, bytes_accessed=2**22, transcendentals=0),
+        name="prepare",
+    )(scalars, probe, tables)
+
+
 def updated(slab, factors, grads):
     vmem = pl.BlockSpec(memory_space=pltpu.VMEM)
     return pl.pallas_call(
@@ -140,7 +212,7 @@
     pair,
     next_pair,
     relay,
-    probe,
+    rolled,
     measured,
     tables,
     mine,
@@ -151,7 +223,6 @@
     obj_imag,
     grad,
     wave,
-    twice,
     mid,
     back,
 ):
@@ -170,10 +241,6 @@
     is_lower = flag(1)
     fwd_high, fwd_low, inv_high, inv_low = (tables[i] for i in range(4))
 
-    for half in range(2):
-        twice[0, half * patch : (half + 1) * patch, :] = probe[0]
-        twice[1, half * patch : (half + 1) * patch, :] = probe[1]
-
     def put(row, phase, index):
         s, c = sin_cos(phase)
         if index is not None:
@@ -233,17 +300,12 @@
     steps = patch // SUBS
     for p in range(number):
         after, below = masks(p)
-        _, corner = window_place(p, patch)
-        shift = corner + jitter[1, p]
-        start = patch - first_row(p)
-        p_real = pltpu.roll(twice[0, pl.ds(start, patch), :], shift, 1)
-        p_imag = pltpu.roll(twice[1, pl.ds(start, patch), :], shift, 1)
         for k in range(steps):
             o_real = pick(obj_real, p, k, after, below)
             o_imag = pick(obj_imag, p, k, after, below)
-            a = p_real[k * SUBS : (k + 1) * SUBS]
-            b = p_imag[k * SUBS : (k + 1) * SUBS]
             row = p * patch + k * SUBS
+            a = rolled[row : row + SUBS, :LANES]
+            b = rolled[row : row + SUBS, LANES:]
             wave[row : row + SUBS, :LANES] = a * o_real - b * o_imag
             wave[row : row + SUBS, LANES:] = a * o_imag + b * o_real
 
@@ -327,7 +389,7 @@
         by_next[part, :] = jnp.where(is_lower, dn2, up2)
 
 
-def strip_gradient(scalars, own, mate, pair, next_pair, relay, probe, measured):
+def strip_gradient(scalars, own, mate, pair, next_pair, relay, rolled, measured, tables):
     number, patch, _ = measured.shape
     rows, cols = own.shape
     vmem = pl.BlockSpec(memory_space=pltpu.VMEM)
@@ -344,7 +406,6 @@
             pltpu.VMEM((5 * rows, cols), f32),
             pltpu.VMEM((5 * rows, cols), f32),
             pltpu.VMEM((number * patch, 2 * LANES), f32),
-            pltpu.VMEM((2, 2 * patch, patch), f32),
             pltpu.VMEM((number * patch, 2 * LANES), f32),
             pltpu.VMEM((number * patch, 2 * LANES), f32),
         ],
@@ -353,7 +414,7 @@
             flops=24 * number * patch**3 * 4, bytes_accessed=4 * number * patch * patch, transcendentals=0
         ),
         name="strip",
-    )(scalars, own, mate, pair, next_pair, relay, probe, measured, dft_tables(patch))
+    )(scalars, own, mate, pair, next_pair, relay, rolled, measured, tables)
 
 
 def permuted(value, axis, target):
@@ -370,8 +431,14 @@
     return permuted(value, "wide", lambda i: i ^ 2)
 
 
-def to_next(value, back=False):
-    return permuted(value, "wide", lambda i: i + 4 if (i // 2 % 2 == 0) != back else i - 4)
+def across(value):
+    count = lax.axis_size("wide")
+
+    def target(i):
+        j = i + 2 if i // 2 % 2 else i - 2
+        return j if 0 <= j < count else i ^ 1
+
+    return permuted(value, "wide", target)
 
 
 def joined(value, axis, steps):
@@ -380,7 +447,7 @@
     return value
 
 
-def body(volume, path_lengths, probe, measured, jitter, step_sizes):
+def program(volume, path_lengths, probe, measured, jitter, step_sizes):
     groups = lax.axis_size("blk")
     column = lax.axis_index("wide")
     columns = lax.axis_size("wide")
@@ -390,35 +457,39 @@
     def to_group(value, step):
         return lax.ppermute(value, "blk", [(i, (i + step) % groups) for i in range(groups)])
 
-    terms, factors, scalars = slab_terms(slab, path_lengths, jitter[:, 0, 0], step_sizes, groups)
-    own = terms[0]
+    terms = slab_terms(slab, path_lengths, groups)
+    own, factors, scalars = own_term(slab, path_lengths, jitter[:, 0, 0], step_sizes, groups)
     for step in range(1, groups):
-        own = own + to_group(terms[step], step)
+        own = own + to_group(terms[step - 1], step)
 
     even = column % 2 == column // 2 % 2
+    next_pair = across(own)
     pair = with_pair(own)
-    mate = with_mate(own)
-    next_pair = to_next(pair)
-    relay = with_mate(jnp.where(even, pair, next_pair))
+    rolled, tables = prepared(scalars, probe)
+    both = with_mate(jnp.concatenate([own, jnp.where(even, pair, next_pair)], 0))
+    mate, relay = both[:rows], both[rows:]
     mine, to_mate, by_pair, by_next = strip_gradient(
-        scalars, own, mate, pair, next_pair, relay, probe, measured[0, 0]
+        scalars, own, mate, pair, next_pair, relay, rolled, measured[0, 0], tables
     )
     got = with_mate(to_mate)
     mine = mine + got[:rows]
     passed = got[rows : 2 * rows]
     local = to_mate[2 * rows :, :LANES] + got[2 * rows :, :LANES]
     zero = jnp.zeros_like(passed)
-    arrived = to_next(by_next + jnp.where(even, zero, passed), back=True)
-    local = joined(local, "wide", [4])
-    arrived, local = lax.optimization_barrier((arrived, local))
-    gradient = mine + with_pair(by_pair + jnp.where(even, passed, zero) + arrived)
-    others = [2**k for k in range(1, columns.bit_length() - 1) if k != 2]
-    local = joined(local, "wide", others[1:])
-    gradient, local = lax.optimization_barrier((gradient, local))
-    grads = [gradient] + [to_group(gradient, step) for step in range(1, groups)]
-    local = joined(local, "wide", others[:1])
+    from_next = across(by_next + jnp.where(even, zero, passed))
+    from_pair = with_pair(by_pair + jnp.where(even, passed, zero))
     local = joined(local, "blk", [2**k for k in range(groups.bit_length() - 1)])
-    return (updated(slab, factors, grads)[None], jnp.sum(local))
+    wide_steps = [2**k for k in range(2, columns.bit_length() - 1)]
+    local = joined(local, "wide", wide_steps[:1])
+    from_next, from_pair, local = lax.optimization_barrier((from_next, from_pair, local))
+    gradient = mine + from_next + from_pair
+    grads = [gradient]
+    for step in range(1, groups):
+        grads.append(to_group(gradient, step))
+    local = joined(local, "wide", ([2] + wide_steps[1:])[:-1])
+    local = joined(local, "wide", ([2] + wide_steps[1:])[-1:])
+    new = updated(slab, factors, grads)
+    return (new[None], jnp.sum(local))
 
 
 def solution(mesh):
@@ -431,4 +502,4 @@
         P(),
     )
     out_specs = (P("blk", None, "wide", None), P())
-    return jax.shard_map(body, mesh=mesh, in_specs=in_specs, out_specs=out_specs, check_vma=False)
+    return jax.shard_map(program, mesh=mesh, in_specs=in_specs, out_specs=out_specs, check_vma=False)

time: 54.7 us -> 47.7 us (0.87)
  waiting for transfers between devices: 23.7 us -> 15.6 us
  starting transfers between devices: 20 us -> 17 us
  local copies, waits for them, and re-layouts: 1.06 us -> 4.02 us
  Pallas kernels: 7.3 us -> 9.38 us
  other arithmetic: 1.6 us -> 0.72 us
    ppermute x11 -> x10, waiting for transfers between devices: 18.2 us -> 13.8 us  [permuted(): return lax.ppermute(value, axis, pairs)]
    ppermute x2, waiting for transfers between devices: 5.42 us -> 1.75 us  [to_group(): lax.ppermute(value, 'blk', [(i, (i + step) % groups) for i in range(group...]
    ppermute x11 -> x10, starting transfers between devices: 16.4 us -> 13.3 us  [permuted(): return lax.ppermute(value, axis, pairs)]
    unnamed x12 -> x16, local copies, waits for them, and re-layouts: 1.06 us -> 4 us
    pallas_call x1 -> x3, Pallas kernels: 1.74 us -> 4.03 us  [the longest x1 1.67 us: slab_terms(): pl.pallas_call(terms_kernel, out_shape=[jax.ShapeDtypeStruct((rows, cols)...]
    add x5 -> x4, other arithmetic: 0.98 us -> 0.08 us  [the longest x1 0.04 us: program(): gradient = mine + from_next + from_pair]
  transfers between devices with their start and end apart: 13 -> 12, of which waited for: 10 -> 7; matrix products, arithmetic and copies ran while one was open for 1% -> 1% of each run, Pallas kernels for 0% -> 5%
where the time goes in v3:
time: 47.7 us; the launch traced here: 47.4 us
  starting transfers between devices  17 us (36%)
  waiting for transfers between devices  15.6 us (33%)
  Pallas kernels  9.38 us (20%)
  local copies, waits for them, and re-layouts  4.02 us (8%)
  between operations  0.77 us (2%)
  other arithmetic  0.72 us (2%)
    ppermute x10, waiting for transfers between devices, permuted(): return lax.ppermute(value, axis, pairs)  13.8 us
    ppermute x10, starting transfers between devices, permuted(): return lax.ppermute(value, axis, pairs)  13.3 us
    pallas_call x1, Pallas kernels, strip_gradient(): pl.pallas_call(strip_kernel, out_shape=(row, jax.ShapeDtypeStruct((2 * ro...  4.62 us
    unnamed x16, local copies, waits for them, and re-layouts  4 us
    ppermute x2, starting transfers between devices, to_group(): lax.ppermute(value, 'blk', [(i, (i + step) % groups) for i in range(group...  3.63 us
    ppermute x2, waiting for transfers between devices, to_group(): lax.ppermute(value, 'blk', [(i, (i + step) % groups) for i in range(group...  1.75 us
    pallas_call x1, Pallas kernels, slab_terms(): pl.pallas_call(terms_kernel, out_shape=[jax.ShapeDtypeStruct((rows, cols)...  1.67 us
    pallas_call x1, Pallas kernels, own_term(): pl.pallas_call(functools.partial(own_kernel, groups), out_shape=(jax.Shap...  1.25 us
  transfers between devices with their start and end apart: 12, of which 7 were waited for; matrix products, arithmetic and copies ran while one was open for 1% of the time, Pallas kernels for 5%

profile of v3, /device:TPU:0, one launch (start us, length us, event | category | flops | bytes accessed | tf_op | source)
XLA Modules:
  0.0 47.4 jit_solution(17883383319972028078)
XLA Ops:
  0.6 1.7 %terms.1 = f32[32,896]{1,0:T(8,128)} custom-call(f32[2,32,896]{2,1,0:T(8,128)} %bitcast.4, f32[2,2,2]{2,1,0:T(2,128)} %paths_hbm.1), custom_call_target="tpu_custom_call" | custom-call | tf_op jit(solution)/shard_map/terms/pallas_call | solution.py:92
  2.3 3.0 %collective-permute-start = (f32[32,896]{1,0:T(8,128)}, f32[32,896]{1,0:T(8,128)S(1)}, u32[]{:S(2)}, u32[]{:S(2)}) collective-permute-start(f32[32,896]{1,0:T(8,128)} %terms.1), channel_id=1, source_target_pairs={{0,16},{16,0},{1,17},{17,1},{2,18},{18,2},{3,19},{19,3},{4,20},{20... | collective-permute-start | bytes 344072 | tf_op jit(solution)/shard_map/ppermute | solution.py:458
  5.3 0.9 %copy-done = f32[1,2,32,896]{3,2,1,0:T(8,128)S(1)} copy-done((f32[1,2,32,896]{3,2,1,0:T(8,128)S(1)}, f32[1,2,32,896]{3,2,1,0:T(8,128)}, u32[]{:S(2)}) %copy-start) | copy-done | bytes 229400
  6.3 0.7 %copy-done.4 = f32[2,2,2]{2,1,0:T(2,128)S(1)} copy-done((f32[2,2,2]{2,1,0:T(2,128)S(1)}, f32[2,2,2]{2,1,0:T(2,128)}, u32[]{:S(2)}) %copy-start.4) | copy-done | bytes 56
  7.0 0.7 %copy-done.5 = s32[2,1,1,14]{3,2,1,0:T(1,128)S(1)} copy-done((s32[2,1,1,14]{3,2,1,0:T(1,128)S(1)}, s32[2,1,1,14]{3,2,1,0:T(1,128)}, u32[]{:S(2)}) %copy-start.5) | copy-done | bytes 136
  7.7 0.7 %copy-done.6 = f32[2]{0:T(128)S(1)} copy-done((f32[2]{0:T(128)S(1)}, f32[2]{0:T(128)}, u32[]{:S(2)}) %copy-start.6) | copy-done | bytes 32
  8.3 1.2 %own.1 = (f32[32,896]{1,0:T(8,128)S(1)}, f32[2,2,8,128]{3,2,1,0:T(8,128)S(1)}, s32[3,14]{1,0:T(4,128)S(1)}) custom-call(f32[2,32,896]{2,1,0:T(8,128)S(1)} %bitcast.5, f32[2,2,2]{2,1,0:T(2,128)S(1)} %copy-done.4, s32[2,14]{1,0:T(2,128)S(1)} %bitcast.7, f32[2]{0:T(128)S(1)} %copy-done.6), custom_call_target="tpu_custom_call" | custom-call | flops 16777216 | bytes 1048576 | tf_op jit(solution)/shard_map/own/pallas_call | solution.py:134
  9.7 3.0 %collective-permute-start.1 = (f32[32,896]{1,0:T(8,128)S(1)}, f32[32,896]{1,0:T(8,128)S(1)}, u32[]{:S(2)}, u32[]{:S(2)}) collective-permute-start(f32[32,896]{1,0:T(8,128)S(1)} %add.41.own), channel_id=1, source_target_pairs={{0,2},{1,3},{2,0},{3,1},{4,6},{5,7},{6,4},{7,5},{8,10},{9,11},{10,... | collective-permute-start | bytes 344072 | tf_op jit(solution)/shard_map/ppermute | solution.py:423
  12.7 4.0 %collective-permute-done.1.pair = f32[32,896]{1,0:T(8,128)S(1)} collective-permute-done((f32[32,896]{1,0:T(8,128)S(1)}, f32[32,896]{1,0:T(8,128)S(1)}, u32[]{:S(2)}, u32[]{:S(2)}) %collective-permute-start.1) | collective-permute-done | bytes 114720 | tf_op jit(solution)/shard_map/ppermute | solution.py:423
  16.8 1.0 %copy-done.2 = bf16[4,256,256]{2,1,0:T(8,128)(2,1)S(1)} copy-done((bf16[4,256,256]{2,1,0:T(8,128)(2,1)S(1)}, bf16[4,256,256]{2,1,0:T(8,128)(2,1)}, u32[]{:S(2)}) %copy-start.2) | copy-done | bytes 524312
  17.8 1.1 %prepare.1 = (f32[1792,256]{1,0:T(8,128)S(1)}, bf16[4,256,256]{2,1,0:T(8,128)(2,1)S(1)}) custom-call(s32[3,14]{1,0:T(4,128)S(1)} %get-tuple-element.15.scalars, f32[2,128,128]{2,1,0:T(8,128)S(1)} %copy-done.3, bf16[4,256,256]{2,1,0:T(8,128)(2,1)S(1)} %copy-done.2), custom_call_target="tpu_custom_call" | custom-call | flops 134217728 | bytes 4194304 | tf_op jit(solution)/shard_map/prepare/pallas_call | solution.py:181
  19.0 4.6 %strip.1 = (f32[32,896]{1,0:T(8,128)S(1)}, f32[72,896]{1,0:T(8,128)S(1)}, f32[32,896]{1,0:T(8,128)S(1)}, f32[32,896]{1,0:T(8,128)S(1)}) custom-call(s32[3,14]{1,0:T(4,128)S(1)} %get-tuple-element.15.scalars, f32[32,896]{1,0:T(8,128)S(1)} %add.41.own, f32[32,896]{1,0:T(8,128)S(1)} %get-tuple-element.29.mate, f32[32,896]{1,0:T(8,128)S(1)} %collective-permute-done.1.pair, ...), custom_call_target="tpu_custom_call" | custom-call | flops 2818572288 | bytes 917504 | tf_op jit(solution)/shard_map/strip/pallas_call | solution.py:399
  24.2 1.2 %collective-permute-done.4 = f32[72,896]{1,0:T(8,128)S(1)} collective-permute-done((f32[72,896]{1,0:T(8,128)S(1)}, f32[72,896]{1,0:T(8,128)S(1)}, u32[]{:S(2)}, u32[]{:S(2)}) %collective-permute-start.4) | collective-permute-done | bytes 258080 | tf_op jit(solution)/shard_map/ppermute | solution.py:423
  25.4 2.6 %collective-permute-start.6 = (f32[32,896]{1,0:T(8,128)S(1)}, f32[32,896]{1,0:T(8,128)S(1)}, u32[]{:S(2)}, u32[]{:S(2)}) collective-permute-start(f32[32,896]{1,0:T(8,128)S(1)} %get-tuple-element.26), channel_id=1, source_target_pairs={{0,2},{1,3},{2,0},{3,1},{4,6},{5,7},{6,4},{7,5},{8,10},{9,11},{10,... | collective-permute-start | bytes 344072 | tf_op jit(solution)/shard_map/ppermute | solution.py:423
  28.6 3.1 %collective-permute-done.7 = f32[8,128]{1,0:T(8,128)S(1)} collective-permute-done((f32[8,128]{1,0:T(8,128)S(1)}, f32[8,128]{1,0:T(8,128)S(1)}, u32[]{:S(2)}, u32[]{:S(2)}) %collective-permute-start.7) | collective-permute-done | bytes 4128 | tf_op jit(solution)/shard_map/ppermute | solution.py:423
  31.6 1.5 %collective-permute-start.8 = (f32[8,128]{1,0:T(8,128)S(1)}, f32[8,128]{1,0:T(8,128)S(1)}, u32[]{:S(2)}, u32[]{:S(2)}) collective-permute-start(f32[8,128]{1,0:T(8,128)S(1)} %add.48), channel_id=1, source_target_pairs={{0,4},{1,5},{2,6},{3,7},{4,0},{5,1},{6,2},{7,3},{8,12},{9,13},{10,... | collective-permute-start | bytes 12296 | tf_op jit(solution)/shard_map/ppermute | solution.py:423
  33.1 2.1 %collective-permute-done.8 = f32[8,128]{1,0:T(8,128)S(1)} collective-permute-done((f32[8,128]{1,0:T(8,128)S(1)}, f32[8,128]{1,0:T(8,128)S(1)}, u32[]{:S(2)}, u32[]{:S(2)}) %collective-permute-start.8) | collective-permute-done | bytes 4128 | tf_op jit(solution)/shard_map/ppermute | solution.py:423
  35.3 3.0 %collective-permute-start.10 = (f32[8,128]{1,0:T(8,128)S(1)}, f32[8,128]{1,0:T(8,128)S(1)}, u32[]{:S(2)}, u32[]{:S(2)}) collective-permute-start(f32[8,128]{1,0:T(8,128)S(1)} %add.49), channel_id=1, source_target_pairs={{0,2},{1,3},{2,0},{3,1},{4,6},{5,7},{6,4},{7,5},{8,10},{9,11},{10,... | collective-permute-start | bytes 12296 | tf_op jit(solution)/shard_map/ppermute | solution.py:423
  38.3 1.6 %collective-permute-done.10 = f32[8,128]{1,0:T(8,128)S(1)} collective-permute-done((f32[8,128]{1,0:T(8,128)S(1)}, f32[8,128]{1,0:T(8,128)S(1)}, u32[]{:S(2)}, u32[]{:S(2)}) %collective-permute-start.10) | collective-permute-done | bytes 4128 | tf_op jit(solution)/shard_map/ppermute | solution.py:423
  39.9 2.0 %collective-permute-start.11 = (f32[8,128]{1,0:T(8,128)S(1)}, f32[8,128]{1,0:T(8,128)S(1)}, u32[]{:S(2)}, u32[]{:S(2)}) collective-permute-start(f32[8,128]{1,0:T(8,128)S(1)} %add.52), channel_id=1, source_target_pairs={{0,8},{1,9},{2,10},{3,11},{4,12},{5,13},{6,14},{7,15},{8,0},{9,1},... | collective-permute-start | bytes 12296 | tf_op jit(solution)/shard_map/ppermute | solution.py:423
  41.9 0.6 %collective-permute-start.9 = (f32[32,896]{1,0:T(8,128)S(1)}, f32[32,896]{1,0:T(8,128)S(1)}, u32[]{:S(2)}, u32[]{:S(2)}) collective-permute-start(f32[32,896]{1,0:T(8,128)S(1)} %fusion.1.refs_0_), channel_id=1, source_target_pairs={{0,16},{16,0},{1,17},{17,1},{2,18},{18,2},{3,19},{19,3},{4,20},{20... | collective-permute-start | bytes 344072 | tf_op jit(solution)/shard_map/ppermute | solution.py:458
  42.5 1.9 %collective-permute-done.11 = f32[8,128]{1,0:T(8,128)S(1)} collective-permute-done((f32[8,128]{1,0:T(8,128)S(1)}, f32[8,128]{1,0:T(8,128)S(1)}, u32[]{:S(2)}, u32[]{:S(2)}) %collective-permute-start.11) | collective-permute-done | bytes 4128 | tf_op jit(solution)/shard_map/ppermute | solution.py:423
  45.0 1.8 %collective-permute-done.9.refs_1_ = f32[32,896]{1,0:T(8,128)S(1)} collective-permute-done((f32[32,896]{1,0:T(8,128)S(1)}, f32[32,896]{1,0:T(8,128)S(1)}, u32[]{:S(2)}, u32[]{:S(2)}) %collective-permute-start.9) | collective-permute-done | bytes 114720 | tf_op jit(solution)/shard_map/ppermute | solution.py:458
  46.7 0.7 %update.1 = f32[2,32,896]{2,1,0:T(8,128)} custom-call(f32[2,32,896]{2,1,0:T(8,128)S(1)} %bitcast.6, f32[2,2,8,128]{3,2,1,0:T(8,128)S(1)} %get-tuple-element.14.factors, f32[32,896]{1,0:T(8,128)S(1)} %fusion.1.refs_0_, f32[32,896]{1,0:T(8,128)S(1)} %collective-permute-done.9.refs_1_), custom_call_target="tpu_custom_call" | custom-call | tf_op jit(solution)/shard_map/update/pallas_call | solution.py:198
  (32 shorter events, 2.1 us)
Async XLA Ops:
  0.6 16.2 %copy-start.3 = (f32[2,128,128]{2,1,0:T(8,128)S(1)}, f32[2,128,128]{2,1,0:T(8,128)}, u32[]{:S(2)}) copy-start(f32[2,128,128]{2,1,0:T(8,128)} %probe.1) | copy-start | bytes 393220
  2.3 7.2 %collective-permute-start = (f32[32,896]{1,0:T(8,128)}, f32[32,896]{1,0:T(8,128)S(1)}, u32[]{:S(2)}, u32[]{:S(2)}) collective-permute-start(f32[32,896]{1,0:T(8,128)} %terms.1), channel_id=1, source_target_pairs={{0,16},{16,0},{1,17},{17,1},{2,18},{18,2},{3,19},{19,3},{4,20},{20... | collective-permute-start | bytes 344072 | tf_op jit(solution)/shard_map/ppermute | solution.py:458
  5.3 0.9 %copy-start = (f32[1,2,32,896]{3,2,1,0:T(8,128)S(1)}, f32[1,2,32,896]{3,2,1,0:T(8,128)}, u32[]{:S(2)}) copy-start(f32[1,2,32,896]{3,2,1,0:T(8,128)} %param.7) | copy-start | bytes 688132
  6.3 0.7 %copy-start.4 = (f32[2,2,2]{2,1,0:T(2,128)S(1)}, f32[2,2,2]{2,1,0:T(2,128)}, u32[]{:S(2)}) copy-start(f32[2,2,2]{2,1,0:T(2,128)} %paths_hbm.1) | copy-start | bytes 100
  7.0 0.7 %copy-start.5 = (s32[2,1,1,14]{3,2,1,0:T(1,128)S(1)}, s32[2,1,1,14]{3,2,1,0:T(1,128)}, u32[]{:S(2)}) copy-start(s32[2,1,1,14]{3,2,1,0:T(1,128)} %param.11) | copy-start | bytes 340
  7.6 0.7 %copy-start.6 = (f32[2]{0:T(128)S(1)}, f32[2]{0:T(128)}, u32[]{:S(2)}) copy-start(f32[2]{0:T(128)} %steps.1) | copy-start | bytes 28
  8.3 10.7 %copy-start.7 = (bf16[1,1,14,128,128]{4,3,2,1,0:T(8,128)(2,1)S(1)}, bf16[1,1,14,128,128]{4,3,2,1,0:T(8,128)(2,1)}, u32[]{:S(2)}) copy-start(bf16[1,1,14,128,128]{4,3,2,1,0:T(8,128)(2,1)} %param.10) | copy-start | bytes 1376260
  9.6 3.1 %collective-permute-start.2 = (f32[32,896]{1,0:T(8,128)S(1)}, f32[32,896]{1,0:T(8,128)S(1)}, u32[]{:S(2)}, u32[]{:S(2)}) collective-permute-start(f32[32,896]{1,0:T(8,128)S(1)} %add.41.own), channel_id=1, source_target_pairs={{0,1},{1,0},{2,4},{3,5},{4,2},{5,3},{6,8},{7,9},{8,6},{9,7},{10,12... | collective-permute-start | bytes 344072 | tf_op jit(solution)/shard_map/ppermute | solution.py:423
  9.7 7.0 %collective-permute-start.1 = (f32[32,896]{1,0:T(8,128)S(1)}, f32[32,896]{1,0:T(8,128)S(1)}, u32[]{:S(2)}, u32[]{:S(2)}) collective-permute-start(f32[32,896]{1,0:T(8,128)S(1)} %add.41.own), channel_id=1, source_target_pairs={{0,2},{1,3},{2,0},{3,1},{4,6},{5,7},{6,4},{7,5},{8,10},{9,11},{10,... | collective-permute-start | bytes 344072 | tf_op jit(solution)/shard_map/ppermute | solution.py:423
  16.7 2.3 %collective-permute-start.3 = (f32[64,896]{1,0:T(8,128)S(1)}, f32[64,896]{1,0:T(8,128)S(1)}, u32[]{:S(2)}, u32[]{:S(2)}) collective-permute-start(f32[64,896]{1,0:T(8,128)S(1)} %pad_maximum_fusion), channel_id=1, source_target_pairs={{0,1},{1,0},{2,3},{3,2},{4,5},{5,4},{6,7},{7,6},{8,9},{9,8},{10,11... | collective-permute-start | bytes 688136 | tf_op jit(solution)/shard_map/ppermute | solution.py:423
  16.8 1.0 %copy-start.2 = (bf16[4,256,256]{2,1,0:T(8,128)(2,1)S(1)}, bf16[4,256,256]{2,1,0:T(8,128)(2,1)}, u32[]{:S(2)}) copy-start(bf16[4,256,256]{2,1,0:T(8,128)(2,1)} %constant.37.clone.tables) | copy-start | bytes 1572868
  19.0 27.7 %copy-start.1 = (f32[1,2,32,896]{3,2,1,0:T(8,128)S(1)}, f32[1,2,32,896]{3,2,1,0:T(8,128)}, u32[]{:S(2)}) copy-start(f32[1,2,32,896]{3,2,1,0:T(8,128)} %param.7) | copy-start | bytes 688132
  23.6 1.7 %collective-permute-start.4 = (f32[72,896]{1,0:T(8,128)S(1)}, f32[72,896]{1,0:T(8,128)S(1)}, u32[]{:S(2)}, u32[]{:S(2)}) collective-permute-start(f32[72,896]{1,0:T(8,128)S(1)} %get-tuple-element.20), channel_id=1, source_target_pairs={{0,1},{1,0},{2,3},{3,2},{4,5},{5,4},{6,7},{7,6},{8,9},{9,8},{10,11... | collective-permute-start | bytes 774152 | tf_op jit(solution)/shard_map/ppermute | solution.py:423
  25.4 9.9 %collective-permute-start.6 = (f32[32,896]{1,0:T(8,128)S(1)}, f32[32,896]{1,0:T(8,128)S(1)}, u32[]{:S(2)}, u32[]{:S(2)}) collective-permute-start(f32[32,896]{1,0:T(8,128)S(1)} %get-tuple-element.26), channel_id=1, source_target_pairs={{0,2},{1,3},{2,0},{3,1},{4,6},{5,7},{6,4},{7,5},{8,10},{9,11},{10,... | collective-permute-start | bytes 344072 | tf_op jit(solution)/shard_map/ppermute | solution.py:423
  27.9 7.3 %collective-permute-start.5 = (f32[32,896]{1,0:T(8,128)S(1)}, f32[32,896]{1,0:T(8,128)S(1)}, u32[]{:S(2)}, u32[]{:S(2)}) collective-permute-start(f32[32,896]{1,0:T(8,128)S(1)} %get-tuple-element.27), channel_id=1, source_target_pairs={{0,1},{1,0},{2,4},{3,5},{4,2},{5,3},{6,8},{7,9},{8,6},{9,7},{10,12... | collective-permute-start | bytes 344072 | tf_op jit(solution)/shard_map/ppermute | solution.py:423
  28.0 3.6 %collective-permute-start.7 = (f32[8,128]{1,0:T(8,128)S(1)}, f32[8,128]{1,0:T(8,128)S(1)}, u32[]{:S(2)}, u32[]{:S(2)}) collective-permute-start(f32[8,128]{1,0:T(8,128)S(1)} %slice_add_fusion.1), channel_id=1, source_target_pairs={{0,16},{16,0},{1,17},{17,1},{2,18},{18,2},{3,19},{19,3},{4,20},{20... | collective-permute-start | bytes 12296 | tf_op jit(solution)/shard_map/ppermute | solution.py:423
  31.6 3.6 %collective-permute-start.8 = (f32[8,128]{1,0:T(8,128)S(1)}, f32[8,128]{1,0:T(8,128)S(1)}, u32[]{:S(2)}, u32[]{:S(2)}) collective-permute-start(f32[8,128]{1,0:T(8,128)S(1)} %add.48), channel_id=1, source_target_pairs={{0,4},{1,5},{2,6},{3,7},{4,0},{5,1},{6,2},{7,3},{8,12},{9,13},{10,... | collective-permute-start | bytes 12296 | tf_op jit(solution)/shard_map/ppermute | solution.py:423
  35.3 4.6 %collective-permute-start.10 = (f32[8,128]{1,0:T(8,128)S(1)}, f32[8,128]{1,0:T(8,128)S(1)}, u32[]{:S(2)}, u32[]{:S(2)}) collective-permute-start(f32[8,128]{1,0:T(8,128)S(1)} %add.49), channel_id=1, source_target_pairs={{0,2},{1,3},{2,0},{3,1},{4,6},{5,7},{6,4},{7,5},{8,10},{9,11},{10,... | collective-permute-start | bytes 12296 | tf_op jit(solution)/shard_map/ppermute | solution.py:423
  39.9 4.5 %collective-permute-start.11 = (f32[8,128]{1,0:T(8,128)S(1)}, f32[8,128]{1,0:T(8,128)S(1)}, u32[]{:S(2)}, u32[]{:S(2)}) collective-permute-start(f32[8,128]{1,0:T(8,128)S(1)} %add.52), channel_id=1, source_target_pairs={{0,8},{1,9},{2,10},{3,11},{4,12},{5,13},{6,14},{7,15},{8,0},{9,1},... | collective-permute-start | bytes 12296 | tf_op jit(solution)/shard_map/ppermute | solution.py:423
  41.9 4.9 %collective-permute-start.9 = (f32[32,896]{1,0:T(8,128)S(1)}, f32[32,896]{1,0:T(8,128)S(1)}, u32[]{:S(2)}, u32[]{:S(2)}) collective-permute-start(f32[32,896]{1,0:T(8,128)S(1)} %fusion.1.refs_0_), channel_id=1, source_target_pairs={{0,16},{16,0},{1,17},{17,1},{2,18},{18,2},{3,19},{19,3},{4,20},{20... | collective-permute-start | bytes 344072 | tf_op jit(solution)/shard_map/ppermute | solution.py:458

commit v4 on v3

--- a/solution.py
+++ b/solution.py
@@ -60,54 +60,33 @@
     return tile, corner - tile * LANES
 
 
-def term_of(slab, paths, angle, group, row):
-    part = slab[0, row : row + SUBS, :] * paths[angle, group, 0]
+def term_of(slab, paths, angle, group, row, col):
+    part = slab[0, row : row + SUBS, col : col + LANES] * paths[angle, group, 0]
     for layer in range(1, slab.shape[0]):
-        part = part + slab[layer, row : row + SUBS, :] * paths[angle, group, layer]
+        part = part + slab[layer, row : row + SUBS, col : col + LANES] * paths[angle, group, layer]
     return part
 
 
-def terms_kernel(slab_hbm, paths_hbm, *refs):
-    terms = refs[:-3]
-    slab, paths, sems = refs[-3:]
-    groups = len(terms) + 1
+def blocks_of(rows, cols):
+    wide = cols // LANES
+    return [(r // SUBS * wide + c // LANES, r, c) for r in range(0, rows, SUBS) for c in range(0, cols, LANES)]
+
+
+def terms_kernel(groups, slab_hbm, paths_hbm, jitter_hbm, steps_hbm, *refs):
+    terms, factors, scalars = refs[: groups - 1], refs[groups - 1], refs[groups]
+    slab, paths, jitter, steps, sems = refs[groups + 1 :]
     group = lax.axis_index("blk")
+    column = lax.axis_index("wide")
+    columns = lax.axis_size("wide")
+    sources = (slab_hbm, paths_hbm, jitter_hbm, steps_hbm)
     copies = [
-        pltpu.make_async_copy(slab_hbm, slab, sems.at[0]),
-        pltpu.make_async_copy(paths_hbm, paths, sems.at[1]),
+        pltpu.make_async_copy(source, target, sems.at[i])
+        for i, (source, target) in enumerate(zip(sources, (slab, paths, jitter, steps)))
     ]
     for copy in copies:
         copy.start()
-    for copy in copies:
+    for copy in copies[1:]:
         copy.wait()
-    for step, term in enumerate(terms):
-        angle = lax.rem(group + step + 1, groups)
-        for r in range(0, slab.shape[1], SUBS):
-            term[r : r + SUBS, :] = term_of(slab, paths, angle, group, r)
-
-
-def slab_terms(slab, paths, groups):
-    _, rows, cols = slab.shape
-    f32 = jnp.float32
-    return pl.pallas_call(
-        terms_kernel,
-        out_shape=[jax.ShapeDtypeStruct((rows, cols), f32)] * (groups - 1),
-        in_specs=[pl.BlockSpec(memory_space=pltpu.HBM)] * 2,
-        out_specs=[pl.BlockSpec(memory_space=pltpu.VMEM)] * (groups - 1),
-        scratch_shapes=[
-            pltpu.VMEM(slab.shape, f32),
-            pltpu.SMEM(paths.shape, f32),
-            pltpu.SemaphoreType.DMA((2,)),
-        ],
-        name="terms",
-    )(slab, paths)
-
-
-def own_kernel(groups, slab, paths, jitter, steps, term, factors, scalars):
-    group = lax.axis_index("blk")
-    column = lax.axis_index("wide")
-    columns = lax.axis_size("wide")
-    layers, rows, _ = slab.shape
     for p in range(jitter.shape[1]):
         scalars[0, p] = jitter[0, p]
         scalars[1, p] = jitter[1, p]
@@ -118,44 +97,90 @@
     scalars[2, 3] = (column >= 1).astype(jnp.int32)
     scalars[2, 4] = (column + 1 < columns).astype(jnp.int32)
     scalars[2, 5] = (column + 2 < columns).astype(jnp.int32)
+    layers, rows, cols = slab.shape
     for step in range(groups):
         source = lax.rem(group - step + groups, groups)
         for layer in range(layers):
             factors[step, layer] = jnp.full((SUBS, LANES), steps[source] * paths[source, group, layer], jnp.float32)
-    for r in range(0, rows, SUBS):
-        term[r : r + SUBS, :] = term_of(slab, paths, group, group, r)
-
-
-def own_term(slab, paths, jitter, steps, groups):
-    layers, rows, cols = slab.shape
+    copies[0].wait()
+    for step, term in enumerate(terms):
+        angle = lax.rem(group + step + 1, groups)
+        for i, r, c in blocks_of(rows, cols):
+            term[i] = term_of(slab, paths, angle, group, r, c)
+
+
+def listed(slab, extra=0):
+    _, rows, cols = slab.shape
+    return jax.ShapeDtypeStruct((rows // SUBS * (cols // LANES) + extra, SUBS, LANES), jnp.float32)
+
+
+def slab_terms(slab, paths, jitter, steps, groups):
     vmem = pl.BlockSpec(memory_space=pltpu.VMEM)
-    smem = pl.BlockSpec(memory_space=pltpu.SMEM)
-    f32 = jnp.float32
+    out = pl.pallas_call(
+        functools.partial(terms_kernel, groups),
+        out_shape=[listed(slab)] * (groups - 1)
+        + [
+            jax.ShapeDtypeStruct((groups, slab.shape[0], SUBS, LANES), jnp.float32),
+            jax.ShapeDtypeStruct((3, jitter.shape[1]), jnp.int32),
+        ],
+        in_specs=[pl.BlockSpec(memory_space=pltpu.HBM)] * 4,
+        out_specs=[vmem] * groups + [pl.BlockSpec(memory_space=pltpu.SMEM)],
+        scratch_shapes=[
+            pltpu.VMEM(slab.shape, jnp.float32),
+            pltpu.SMEM(paths.shape, jnp.float32),
+            pltpu.SMEM(jitter.shape, jnp.int32),
+            pltpu.SMEM(steps.shape, jnp.float32),
+            pltpu.SemaphoreType.DMA((4,)),
+        ],
+        name="terms",
+    )(slab, paths, jitter, steps)
+    return out[: groups - 1], out[groups - 1], out[groups]
+
+
+def own_kernel(slab, paths, term):
+    group = lax.axis_index("blk")
+    for i, r, c in blocks_of(*slab.shape[1:]):
+        term[i] = term_of(slab, paths, group, group, r, c)
+
+
+def own_term(slab, paths):
     return pl.pallas_call(
-        functools.partial(own_kernel, groups),
-        out_shape=(
-            jax.ShapeDtypeStruct((rows, cols), f32),
-            jax.ShapeDtypeStruct((groups, layers, SUBS, LANES), f32),
-            jax.ShapeDtypeStruct((3, jitter.shape[1]), jnp.int32),
-        ),
-        in_specs=[vmem, smem, smem, smem],
-        out_specs=(vmem, vmem, smem),
+        own_kernel,
+        out_shape=listed(slab),
+        in_specs=[pl.BlockSpec(memory_space=pltpu.VMEM), pl.BlockSpec(memory_space=pltpu.SMEM)],
+        out_specs=pl.BlockSpec(memory_space=pltpu.VMEM),
         compiler_params=pltpu.CompilerParams(vmem_limit_bytes=8 * 1024 * 1024),
         cost_estimate=pl.CostEstimate(flops=2**24, bytes_accessed=2**20, transcendentals=0),
         name="own",
-    )(slab, paths, jitter, steps)
-
-
-def update_kernel(slab, factors, *refs):
-    grads, out = refs[:-1], refs[-1]
+    )(slab, paths)
+
+
+def update_kernel(count, slab, factors, *refs):
+    grads, sums, out, total = refs[:count], refs[count:-2], refs[-2], refs[-1]
     layers, rows, cols = slab.shape
+    blocks = grads[0].shape[0]
+    value = sums[0][0]
+    if len(sums) == 3:
+        value = (value + sums[1][0]) + (grads[1][blocks] + sums[2][0])
+    total[0, 0] = jnp.sum(value)
     for layer in range(layers):
-        for r in range(0, rows, SUBS):
-            for c in range(0, cols, LANES):
-                value = slab[layer, r : r + SUBS, c : c + LANES]
-                for step, grad in enumerate(grads):
-                    value = value - factors[step, layer] * grad[r : r + SUBS, c : c + LANES]
-                out[layer, r : r + SUBS, c : c + LANES] = value
+        for i, r, c in blocks_of(rows, cols):
+            value = slab[layer, r : r + SUBS, c : c + LANES]
+            for step in range(count):
+                value = value - factors[step, layer] * grads[step][i]
+            out[layer, r : r + SUBS, c : c + LANES] = value
+
+
+def updated(slab, factors, grads, sums):
+    vmem = pl.BlockSpec(memory_space=pltpu.VMEM)
+    return pl.pallas_call(
+        functools.partial(update_kernel, len(grads)),
+        out_shape=(jax.ShapeDtypeStruct(slab.shape, slab.dtype), jax.ShapeDtypeStruct((1, 1), jnp.float32)),
+        in_specs=[vmem] * (2 + len(grads) + len(sums)),
+        out_specs=(vmem, pl.BlockSpec(memory_space=pltpu.SMEM)),
+        compiler_params=pltpu.CompilerParams(vmem_limit_bytes=8 * 1024 * 1024),
+        name="update",
+    )(slab, factors, *grads, *sums)
 
 
 def prepare_kernel(number, scalars, probe, tables, rolled, kept, twice):
@@ -193,18 +218,6 @@
     )(scalars, probe, tables)
 
 
-def updated(slab, factors, grads):
-    vmem = pl.BlockSpec(memory_space=pltpu.VMEM)
-    return pl.pallas_call(
-        update_kernel,
-        out_shape=jax.ShapeDtypeStruct(slab.shape, slab.dtype),
-        in_specs=[vmem] * (2 + len(grads)),
-        out_specs=vmem,
-        compiler_params=pltpu.CompilerParams(vmem_limit_bytes=8 * 1024 * 1024),
-        name="update",
-    )(slab, factors, *grads)
-
-
 def strip_kernel(
     scalars,
     own,
@@ -219,46 +232,46 @@
     to_mate,
     by_pair,
     by_next,
+    misfit,
     obj_real,
     obj_imag,
-    grad,
     wave,
     mid,
     back,
 ):
     number, patch, _ = measured.shape
-    rows, cols = own.shape
-    tiles = cols // LANES
+    rows = ROWS_DEV
+    tiles = own.shape[0] * SUBS // rows
     far = rows - ROWS_DEV // 4
     near = ROWS_DEV // 4 + JIT
     dot = functools.partial(lax.dot, preferred_element_type=jnp.float32)
     jitter = scalars
 
     def flag(index):
-        return jnp.full((SUBS, cols), scalars[2, index], jnp.int32) == 1
+        return jnp.full((SUBS, LANES), scalars[2, index], jnp.int32) == 1
 
     is_second = flag(0)
     is_lower = flag(1)
     fwd_high, fwd_low, inv_high, inv_low = (tables[i] for i in range(4))
 
-    def put(row, phase, index):
+    def put(row, tile, phase, index):
         s, c = sin_cos(phase)
         if index is not None:
             ok = scalars[2, index].astype(jnp.float32)
             s = s * ok
             c = c * ok
-        obj_real[row : row + SUBS, :] = c
-        obj_imag[row : row + SUBS, :] = s
-
-    for r in range(0, rows, SUBS):
-        part = slice(r, r + SUBS)
-        put(2 * rows + r, own[part, :], None)
-        put(rows + r, jnp.where(is_second, mate[part, :], relay[part, :]), 3)
-        put(3 * rows + r, jnp.where(is_second, relay[part, :], mate[part, :]), 4)
+        obj_real[row // SUBS * tiles + tile] = c
+        obj_imag[row // SUBS * tiles + tile] = s
+
+    for i, r, c in blocks_of(rows, tiles * LANES):
+        t = c // LANES
+        put(2 * rows + r, t, own[i], None)
+        put(rows + r, t, jnp.where(is_second, mate[i], relay[i]), 3)
+        put(3 * rows + r, t, jnp.where(is_second, relay[i], mate[i]), 4)
         if r >= rows - far:
-            put(r, jnp.where(is_lower, pair[part, :], next_pair[part, :]), 2)
+            put(r, t, jnp.where(is_lower, pair[i], next_pair[i]), 2)
         if r < far:
-            put(4 * rows + r, jnp.where(is_lower, next_pair[part, :], pair[part, :]), 5)
+            put(4 * rows + r, t, jnp.where(is_lower, next_pair[i], pair[i]), 5)
 
     lane = lax.broadcasted_iota(jnp.int32, (SUBS, LANES), 1)
     sub = lax.broadcasted_iota(jnp.int32, (SUBS, LANES), 0)
@@ -276,12 +289,9 @@
         tile, _ = window_place(p, patch)
 
         def at(row):
-            left = ref[row : row + SUBS, tile * LANES : (tile + 1) * LANES] if tile >= 0 else 0.0
-            right = (
-                ref[row : row + SUBS, (tile + 1) * LANES : (tile + 2) * LANES]
-                if tile + 1 < tiles
-                else 0.0
-            )
+            first = row // SUBS * tiles + tile
+            left = ref[first] if tile >= 0 else 0.0
+            right = ref[first + 1] if tile + 1 < tiles else 0.0
             return jnp.where(after, left, right)
 
         row = k * SUBS
@@ -339,8 +349,7 @@
             lanes = slice(half * LANES, (half + 1) * LANES)
             back[row : row + patch, :LANES] = undone[:patch, lanes]
             back[row : row + patch, LANES:] = undone[patch:, lanes]
-    to_mate[2 * rows : 2 * rows + SUBS, :] = jnp.zeros((SUBS, cols), jnp.float32)
-    to_mate[2 * rows : 2 * rows + SUBS, :LANES] = total
+    misfit[0] = total
 
     for p in range(0, number, 2):
         high, low = parts_of(back[p * patch : (p + 2) * patch, :])
@@ -348,6 +357,7 @@
         w = wave[p * patch : (p + 2) * patch, :]
         mid[p * patch : (p + 2) * patch, :LANES] = w[:, :LANES] * out[:, LANES:] - w[:, LANES:] * out[:, :LANES]
 
+    grads = {}
     for t in range(tiles):
         meets = []
         for p in range(number):
@@ -355,7 +365,6 @@
             if t in (tile, tile + 1):
                 after, below = masks(p)
                 meets.append((p, after if t == tile else jnp.logical_not(after), below))
-        cols = slice(t * LANES, (t + 1) * LANES)
         for k in range(steps):
             row = k * SUBS
             here = there = None
@@ -369,45 +378,42 @@
                     there = (term - kept) if there is None else there + (term - kept)
                 else:
                     here = term if here is None else here + term
-            if here is not None:
-                grad[row : row + SUBS, cols] = here
-            else:
-                grad[row : row + SUBS, cols] = jnp.zeros((SUBS, LANES), jnp.float32)
-            if there is not None:
-                grad[row + patch : row + patch + SUBS, cols] = there
-    for row in range(patch + near, 5 * rows, SUBS):
-        grad[row : row + SUBS, :] = jnp.zeros((SUBS, grad.shape[1]), jnp.float32)
-
-
-    for r in range(0, rows, SUBS):
-        part = slice(r, r + SUBS)
-        up2, up1, here, dn1, dn2 = (grad[k * rows + r : k * rows + r + SUBS, :] for k in range(5))
-        mine[part, :] = here
-        to_mate[part, :] = jnp.where(is_second, up1, dn1)
-        to_mate[rows + r : rows + r + SUBS, :] = jnp.where(is_second, dn1, up1)
-        by_pair[part, :] = jnp.where(is_lower, up2, dn2)
-        by_next[part, :] = jnp.where(is_lower, dn2, up2)
+            grads[k, t] = here
+            grads[k + steps, t] = there
+
+    def add_to(slot, r, t):
+        value = grads.get((slot * (rows // SUBS) + r // SUBS, t))
+        return jnp.zeros((SUBS, LANES), jnp.float32) if value is None else value
+
+    for i, r, c in blocks_of(rows, tiles * LANES):
+        up2, up1, here, dn1, dn2 = (add_to(slot, r, c // LANES) for slot in range(5))
+        mine[i] = here
+        to_mate[i] = jnp.where(is_second, up1, dn1)
+        to_mate[own.shape[0] + i] = jnp.where(is_second, dn1, up1)
+        by_pair[i] = jnp.where(is_lower, up2, dn2)
+        by_next[i] = jnp.where(is_lower, dn2, up2)
 
 
 def strip_gradient(scalars, own, mate, pair, next_pair, relay, rolled, measured, tables):
     number, patch, _ = measured.shape
-    rows, cols = own.shape
+    blocks = own.shape[0]
     vmem = pl.BlockSpec(memory_space=pltpu.VMEM)
     smem = pl.BlockSpec(memory_space=pltpu.SMEM)
-    f32 = jnp.float32
-    row = jax.ShapeDtypeStruct((rows, cols), f32)
+
+    def block_list(count):
+        return jax.ShapeDtypeStruct((count, SUBS, LANES), jnp.float32)
+
     return pl.pallas_call(
         strip_kernel,
-        out_shape=(row, jax.ShapeDtypeStruct((2 * rows + SUBS, cols), f32), row, row),
+        out_shape=tuple(block_list(n) for n in (blocks, 2 * blocks, blocks, blocks, 1)),
         in_specs=[smem] + [vmem] * 8,
-        out_specs=(vmem,) * 4,
+        out_specs=(vmem,) * 5,
         scratch_shapes=[
-            pltpu.VMEM((5 * rows, cols), f32),
-            pltpu.VMEM((5 * rows, cols), f32),
-            pltpu.VMEM((5 * rows, cols), f32),
-            pltpu.VMEM((number * patch, 2 * LANES), f32),
-            pltpu.VMEM((number * patch, 2 * LANES), f32),
-            pltpu.VMEM((number * patch, 2 * LANES), f32),
+            pltpu.VMEM((5 * blocks, SUBS, LANES), jnp.float32),
+            pltpu.VMEM((5 * blocks, SUBS, LANES), jnp.float32),
+            pltpu.VMEM((number * patch, 2 * LANES), jnp.float32),
+            pltpu.VMEM((number * patch, 2 * LANES), jnp.float32),
+            pltpu.VMEM((number * patch, 2 * LANES), jnp.float32),
         ],
         compiler_params=pltpu.CompilerParams(vmem_limit_bytes=40 * 1024 * 1024),
         cost_estimate=pl.CostEstimate(
@@ -452,13 +458,12 @@
     column = lax.axis_index("wide")
     columns = lax.axis_size("wide")
     slab = volume[0]
-    rows = slab.shape[1]
 
     def to_group(value, step):
         return lax.ppermute(value, "blk", [(i, (i + step) % groups) for i in range(groups)])
 
-    terms = slab_terms(slab, path_lengths, groups)
-    own, factors, scalars = own_term(slab, path_lengths, jitter[:, 0, 0], step_sizes, groups)
+    terms, factors, scalars = slab_terms(slab, path_lengths, jitter[:, 0, 0], step_sizes, groups)
+    own = own_term(slab, path_lengths)
     for step in range(1, groups):
         own = own + to_group(terms[step - 1], step)
 
@@ -467,29 +472,35 @@
     pair = with_pair(own)
     rolled, tables = prepared(scalars, probe)
     both = with_mate(jnp.concatenate([own, jnp.where(even, pair, next_pair)], 0))
-    mate, relay = both[:rows], both[rows:]
-    mine, to_mate, by_pair, by_next = strip_gradient(
+    blocks = own.shape[0]
+    mate, relay = both[:blocks], both[blocks:]
+    mine, to_mate, by_pair, by_next, local = strip_gradient(
         scalars, own, mate, pair, next_pair, relay, rolled, measured[0, 0], tables
     )
     got = with_mate(to_mate)
-    mine = mine + got[:rows]
-    passed = got[rows : 2 * rows]
-    local = to_mate[2 * rows :, :LANES] + got[2 * rows :, :LANES]
+    if groups != 2:
+        local = joined(local, "blk", [2**k for k in range(groups.bit_length() - 1)])
+    local = joined(local, "wide", [4])
+    mine = mine + got[:blocks]
+    passed = got[blocks:]
     zero = jnp.zeros_like(passed)
+    from_pair = with_pair(by_pair + jnp.where(even, passed, zero))
     from_next = across(by_next + jnp.where(even, zero, passed))
-    from_pair = with_pair(by_pair + jnp.where(even, passed, zero))
-    local = joined(local, "blk", [2**k for k in range(groups.bit_length() - 1)])
-    wide_steps = [2**k for k in range(2, columns.bit_length() - 1)]
-    local = joined(local, "wide", wide_steps[:1])
-    from_next, from_pair, local = lax.optimization_barrier((from_next, from_pair, local))
-    gradient = mine + from_next + from_pair
+    local = joined(local, "wide", [1])
+    local = joined(local, "wide", [2**k for k in range(3, columns.bit_length() - 1)])
+    gradient = mine + (from_next + from_pair)
     grads = [gradient]
-    for step in range(1, groups):
-        grads.append(to_group(gradient, step))
-    local = joined(local, "wide", ([2] + wide_steps[1:])[:-1])
-    local = joined(local, "wide", ([2] + wide_steps[1:])[-1:])
-    new = updated(slab, factors, grads)
-    return (new[None], jnp.sum(local))
+    if groups == 2:
+        grads.append(to_group(jnp.concatenate([gradient, local], 0), 1))
+        sums = [local, with_pair(local)]
+        pairs = [(i, (i + columns) % (2 * columns) ^ 2) for i in range(2 * columns)]
+        sums.append(lax.ppermute(local, ("blk", "wide"), pairs))
+    else:
+        for step in range(1, groups):
+            grads.append(to_group(gradient, step))
+        sums = [joined(local, "wide", [2])]
+    new, total = updated(slab, factors, grads, sums)
+    return (new[None], total[0, 0])
 
 
 def solution(mesh):

time: 47.7 us -> 46 us (0.964)
  local copies, waits for them, and re-layouts: 4.02 us -> 3.38 us
  other arithmetic: 0.72 us -> 0.12 us
  Pallas kernels: 9.38 us -> 8.79 us
    ppermute x0 -> x1, waiting for transfers between devices: none -> 2.51 us  [program(): sums.append(lax.ppermute(local, ('blk', 'wide'), pairs))]
    ppermute x10, waiting for transfers between devices: 13.8 us -> 11.6 us  [permuted(): return lax.ppermute(value, axis, pairs)]
    ppermute x10, starting transfers between devices: 13.3 us -> 11.3 us  [permuted(): return lax.ppermute(value, axis, pairs)]
    ppermute x0 -> x1, starting transfers between devices: none -> 1.5 us  [program(): sums.append(lax.ppermute(local, ('blk', 'wide'), pairs))]
    ppermute x2, starting transfers between devices: 3.63 us -> 4.59 us  [to_group(): lax.ppermute(value, 'blk', [(i, (i + step) % groups) for i in range(group...]
    unnamed x16 -> x18, local copies, waits for them, and re-layouts: 4 us -> 3.36 us
    ppermute x2, waiting for transfers between devices: 1.75 us -> 1.11 us  [to_group(): lax.ppermute(value, 'blk', [(i, (i + step) % groups) for i in range(group...]
    reduce_sum x1 -> x0, other arithmetic: 0.6 us -> none  [program(): return (new[None], jnp.sum(local))]
  transfers between devices with their start and end apart: 12 -> 13, of which waited for: 7 -> 8; matrix products, arithmetic and copies ran while one was open for 1% -> 0% of each run, Pallas kernels for 5% -> 4%
where the time goes in v4:
time: 46 us; the launch traced here: 45.7 us
  starting transfers between devices  17.4 us (38%)
  waiting for transfers between devices  15.2 us (33%)
  Pallas kernels  8.79 us (19%)
  local copies, waits for them, and re-layouts  3.38 us (7%)
  between operations  0.79 us (2%)
    ppermute x10, waiting for transfers between devices, permuted(): return lax.ppermute(value, axis, pairs)  11.6 us
    ppermute x10, starting transfers between devices, permuted(): return lax.ppermute(value, axis, pairs)  11.3 us
    pallas_call x1, Pallas kernels, strip_gradient(): pl.pallas_call(strip_kernel, out_shape=tuple((block_list(n) for n in (blo...  4.61 us
    ppermute x2, starting transfers between devices, to_group(): lax.ppermute(value, 'blk', [(i, (i + step) % groups) for i in range(group...  4.59 us
    unnamed x18, local copies, waits for them, and re-layouts  3.36 us
    ppermute x1, waiting for transfers between devices, program(): sums.append(lax.ppermute(local, ('blk', 'wide'), pairs))  2.51 us
    pallas_call x1, Pallas kernels, slab_terms(): pl.pallas_call(functools.partial(terms_kernel, groups), out_shape=[listed...  1.7 us
    ppermute x1, starting transfers between devices, program(): sums.append(lax.ppermute(local, ('blk', 'wide'), pairs))  1.5 us
  transfers between devices with their start and end apart: 13, of which 8 were waited for; matrix products, arithmetic and copies ran while one was open for 0% of the time, Pallas kernels for 4%

profile of v4, /device:TPU:0, one launch (start us, length us, event | category | flops | bytes accessed | tf_op | source)
XLA Modules:
  0.0 45.7 jit_solution(10566551976885161869)
XLA Ops:
  0.6 1.7 %terms.1 = (f32[28,8,128]{2,1,0:T(8,128)}, f32[2,2,8,128]{3,2,1,0:T(8,128)}, s32[3,14]{1,0:T(4,128)}) custom-call(f32[2,32,896]{2,1,0:T(8,128)} %bitcast.5, f32[2,2,2]{2,1,0:T(2,128)} %paths.1, s32[2,14]{1,0:T(2,128)} %bitcast.9, f32[2]{0:T(128)} %steps_hbm.1), custom_call_target="tpu_custom_call" | custom-call | tf_op jit(solution)/shard_map/terms/pallas_call | solution.py:119
  2.4 3.0 %collective-permute-start = (f32[28,8,128]{2,1,0:T(8,128)}, f32[28,8,128]{2,1,0:T(8,128)S(1)}, u32[]{:S(2)}, u32[]{:S(2)}) collective-permute-start(f32[28,8,128]{2,1,0:T(8,128)} %get-tuple-element.16), channel_id=1, source_target_pairs={{0,16},{16,0},{1,17},{17,1},{2,18},{18,2},{3,19},{19,3},{4,20},{20... | collective-permute-start | bytes 344072 | tf_op jit(solution)/shard_map/ppermute | solution.py:463
  5.4 0.9 %copy-done = f32[1,2,32,896]{3,2,1,0:T(8,128)S(1)} copy-done((f32[1,2,32,896]{3,2,1,0:T(8,128)S(1)}, f32[1,2,32,896]{3,2,1,0:T(8,128)}, u32[]{:S(2)}) %copy-start) | copy-done | bytes 229400
  6.3 0.7 %copy-done.5 = f32[2,2,2]{2,1,0:T(2,128)S(1)} copy-done((f32[2,2,2]{2,1,0:T(2,128)S(1)}, f32[2,2,2]{2,1,0:T(2,128)}, u32[]{:S(2)}) %copy-start.5) | copy-done | bytes 56
  7.0 0.6 %own.1 = f32[28,8,128]{2,1,0:T(8,128)S(1)} custom-call(f32[2,32,896]{2,1,0:T(8,128)S(1)} %bitcast.6, f32[2,2,2]{2,1,0:T(2,128)S(1)} %copy-done.5), custom_call_target="tpu_custom_call" | custom-call | flops 16777216 | bytes 1048576 | tf_op jit(solution)/shard_map/own/pallas_call | solution.py:147
  7.6 1.1 %collective-permute-done = f32[28,8,128]{2,1,0:T(8,128)S(1)} collective-permute-done((f32[28,8,128]{2,1,0:T(8,128)}, f32[28,8,128]{2,1,0:T(8,128)S(1)}, u32[]{:S(2)}, u32[]{:S(2)}) %collective-permute-start) | collective-permute-done | bytes 114720 | tf_op jit(solution)/shard_map/ppermute | solution.py:463
  8.8 3.3 %collective-permute-start.1 = (f32[28,8,128]{2,1,0:T(8,128)S(1)}, f32[28,8,128]{2,1,0:T(8,128)S(1)}, u32[]{:S(2)}, u32[]{:S(2)}) collective-permute-start(f32[28,8,128]{2,1,0:T(8,128)S(1)} %add.35.own), channel_id=1, source_target_pairs={{0,2},{1,3},{2,0},{3,1},{4,6},{5,7},{6,4},{7,5},{8,10},{9,11},{10,... | collective-permute-start | bytes 344072 | tf_op jit(solution)/shard_map/ppermute | solution.py:429
  12.1 3.4 %collective-permute-done.1.pair = f32[28,8,128]{2,1,0:T(8,128)S(1)} collective-permute-done((f32[28,8,128]{2,1,0:T(8,128)S(1)}, f32[28,8,128]{2,1,0:T(8,128)S(1)}, u32[]{:S(2)}, u32[]{:S(2)}) %collective-permute-start.1) | collective-permute-done | bytes 114720 | tf_op jit(solution)/shard_map/ppermute | solution.py:429
  15.6 1.0 %copy-done.2 = bf16[4,256,256]{2,1,0:T(8,128)(2,1)S(1)} copy-done((bf16[4,256,256]{2,1,0:T(8,128)(2,1)S(1)}, bf16[4,256,256]{2,1,0:T(8,128)(2,1)}, u32[]{:S(2)}) %copy-start.2) | copy-done | bytes 524312
  16.7 0.7 %copy-done.6 = s32[3,14]{1,0:T(4,128)S(1)} copy-done((s32[3,14]{1,0:T(4,128)S(1)}, s32[3,14]{1,0:T(4,128)}, u32[]{:S(2)}) %copy-start.6) | copy-done | bytes 192
  17.4 1.1 %prepare.1 = (f32[1792,256]{1,0:T(8,128)S(1)}, bf16[4,256,256]{2,1,0:T(8,128)(2,1)S(1)}) custom-call(s32[3,14]{1,0:T(4,128)S(1)} %copy-done.6, f32[2,128,128]{2,1,0:T(8,128)S(1)} %copy-done.3, bf16[4,256,256]{2,1,0:T(8,128)(2,1)S(1)} %copy-done.2), custom_call_target="tpu_custom_call" | custom-call | flops 134217728 | bytes 4194304 | tf_op jit(solution)/shard_map/prepare/pallas_call | solution.py:206
  18.5 4.6 %strip.1 = (f32[28,8,128]{2,1,0:T(8,128)S(1)}, f32[56,8,128]{2,1,0:T(8,128)S(1)}, f32[28,8,128]{2,1,0:T(8,128)S(1)}, f32[28,8,128]{2,1,0:T(8,128)S(1)}, f32[1,8,128]{2,1,0:T(8,128)S(1)}) custom-call(s32[3,14]{1,0:T(4,128)S(1)} %copy-done.7, f32[28,8,128]{2,1,0:T(8,128)S(1)} %add.35.own, f32[28,8,128]{2,1,0:T(8,128)S(1)} %get-tuple-element.29.mate, ...), custom_call_target="tpu_custom_call" | custom-call | flops 2818572288 | bytes 917504 | tf_op jit(solution)/shard_map/strip/pallas_call | solution.py:406
  23.7 1.1 %collective-permute-done.4 = f32[56,8,128]{2,1,0:T(8,128)S(1)} collective-permute-done((f32[56,8,128]{2,1,0:T(8,128)S(1)}, f32[56,8,128]{2,1,0:T(8,128)S(1)}, u32[]{:S(2)}, u32[]{:S(2)}) %collective-permute-start.4) | collective-permute-done | bytes 229408 | tf_op jit(solution)/shard_map/ppermute | solution.py:429
  24.9 2.6 %collective-permute-start.6 = (f32[28,8,128]{2,1,0:T(8,128)S(1)}, f32[28,8,128]{2,1,0:T(8,128)S(1)}, u32[]{:S(2)}, u32[]{:S(2)}) collective-permute-start(f32[28,8,128]{2,1,0:T(8,128)S(1)} %get-tuple-element.26), channel_id=1, source_target_pairs={{0,2},{1,3},{2,0},{3,1},{4,6},{5,7},{6,4},{7,5},{8,10},{9,11},{10,... | collective-permute-start | bytes 344072 | tf_op jit(solution)/shard_map/ppermute | solution.py:429
  27.5 1.5 %collective-permute-start.7 = (f32[1,8,128]{2,1,0:T(8,128)S(1)}, f32[1,8,128]{2,1,0:T(8,128)S(1)}, u32[]{:S(2)}, u32[]{:S(2)}) collective-permute-start(f32[1,8,128]{2,1,0:T(8,128)S(1)} %get-tuple-element.23), channel_id=1, source_target_pairs={{0,4},{1,5},{2,6},{3,7},{4,0},{5,1},{6,2},{7,3},{8,12},{9,13},{10,... | collective-permute-start | bytes 12296 | tf_op jit(solution)/shard_map/ppermute | solution.py:429
  29.0 3.5 %collective-permute-done.7 = f32[1,8,128]{2,1,0:T(8,128)S(1)} collective-permute-done((f32[1,8,128]{2,1,0:T(8,128)S(1)}, f32[1,8,128]{2,1,0:T(8,128)S(1)}, u32[]{:S(2)}, u32[]{:S(2)}) %collective-permute-start.7) | collective-permute-done | bytes 4128 | tf_op jit(solution)/shard_map/ppermute | solution.py:429
  32.5 1.2 %collective-permute-done.8 = f32[1,8,128]{2,1,0:T(8,128)S(1)} collective-permute-done((f32[1,8,128]{2,1,0:T(8,128)S(1)}, f32[1,8,128]{2,1,0:T(8,128)S(1)}, u32[]{:S(2)}, u32[]{:S(2)}) %collective-permute-start.8) | collective-permute-done | bytes 4128 | tf_op jit(solution)/shard_map/ppermute | solution.py:429
  33.7 2.7 %collective-permute-start.9 = (f32[1,8,128]{2,1,0:T(8,128)S(1)}, f32[1,8,128]{2,1,0:T(8,128)S(1)}, u32[]{:S(2)}, u32[]{:S(2)}) collective-permute-start(f32[1,8,128]{2,1,0:T(8,128)S(1)} %add.44), channel_id=1, source_target_pairs={{0,8},{1,9},{2,10},{3,11},{4,12},{5,13},{6,14},{7,15},{8,0},{9,1},... | collective-permute-start | bytes 12296 | tf_op jit(solution)/shard_map/ppermute | solution.py:429
  36.4 1.8 %collective-permute-done.9 = f32[1,8,128]{2,1,0:T(8,128)S(1)} collective-permute-done((f32[1,8,128]{2,1,0:T(8,128)S(1)}, f32[1,8,128]{2,1,0:T(8,128)S(1)}, u32[]{:S(2)}, u32[]{:S(2)}) %collective-permute-start.9) | collective-permute-done | bytes 4128 | tf_op jit(solution)/shard_map/ppermute | solution.py:429
  38.3 1.6 %collective-permute-start.10 = (f32[29,8,128]{2,1,0:T(8,128)S(1)}, f32[29,8,128]{2,1,0:T(8,128)S(1)}, u32[]{:S(2)}, u32[]{:S(2)}) collective-permute-start(f32[29,8,128]{2,1,0:T(8,128)S(1)} %pad_maximum_fusion.1), channel_id=1, source_target_pairs={{0,16},{16,0},{1,17},{17,1},{2,18},{18,2},{3,19},{19,3},{4,20},{20... | collective-permute-start | bytes 356360 | tf_op jit(solution)/shard_map/ppermute | solution.py:463
  39.8 1.5 %collective-permute-start.12 = (f32[1,8,128]{2,1,0:T(8,128)S(1)}, f32[1,8,128]{2,1,0:T(8,128)S(1)}, u32[]{:S(2)}, u32[]{:S(2)}) collective-permute-start(f32[1,8,128]{2,1,0:T(8,128)S(1)} %add.45.refs_2_), channel_id=1, source_target_pairs={{0,18},{1,19},{2,16},{3,17},{4,22},{5,23},{6,20},{7,21},{8,26},{9,... | collective-permute-start | bytes 12296 | tf_op jit(solution)/shard_map/ppermute | solution.py:497
  41.8 2.5 %collective-permute-done.12.refs_4_ = f32[1,8,128]{2,1,0:T(8,128)S(1)} collective-permute-done((f32[1,8,128]{2,1,0:T(8,128)S(1)}, f32[1,8,128]{2,1,0:T(8,128)S(1)}, u32[]{:S(2)}, u32[]{:S(2)}) %collective-permute-start.12) | collective-permute-done | bytes 4128 | tf_op jit(solution)/shard_map/ppermute | solution.py:497
  44.3 0.6 %collective-permute-done.11.refs_3_ = f32[1,8,128]{2,1,0:T(8,128)S(1)} collective-permute-done((f32[1,8,128]{2,1,0:T(8,128)S(1)}, f32[1,8,128]{2,1,0:T(8,128)S(1)}, u32[]{:S(2)}, u32[]{:S(2)}) %collective-permute-start.11) | collective-permute-done | bytes 4128 | tf_op jit(solution)/shard_map/ppermute | solution.py:429
  44.9 0.7 %update.1 = (f32[2,32,896]{2,1,0:T(8,128)}, f32[1,1]{1,0:T(1,128)}) custom-call(f32[2,32,896]{2,1,0:T(8,128)S(1)} %bitcast.7, f32[2,2,8,128]{3,2,1,0:T(8,128)S(1)} %copy-done.4, f32[28,8,128]{2,1,0:T(8,128)S(1)} %fusion.refs_0_, f32[29,8,128]{2,1,0:T(8,128)S(1)} %collective-permute-done.10.refs_1_, f32[1,8,128]{2,1,0:T(8,128)S(1)} %add.45.refs_2_, ...), custom_call_target="tpu_custom_call" | custom-call | tf_op jit(solution)/shard_map/update/pallas_call | solution.py:176
  (35 shorter events, 1.5 us)
Async XLA Ops:
  0.6 15.0 %copy-start.3 = (f32[2,128,128]{2,1,0:T(8,128)S(1)}, f32[2,128,128]{2,1,0:T(8,128)}, u32[]{:S(2)}) copy-start(f32[2,128,128]{2,1,0:T(8,128)} %probe.1) | copy-start | bytes 393220
  2.4 6.4 %collective-permute-start = (f32[28,8,128]{2,1,0:T(8,128)}, f32[28,8,128]{2,1,0:T(8,128)S(1)}, u32[]{:S(2)}, u32[]{:S(2)}) collective-permute-start(f32[28,8,128]{2,1,0:T(8,128)} %get-tuple-element.16), channel_id=1, source_target_pairs={{0,16},{16,0},{1,17},{17,1},{2,18},{18,2},{3,19},{19,3},{4,20},{20... | collective-permute-start | bytes 344072 | tf_op jit(solution)/shard_map/ppermute | solution.py:463
  5.4 0.9 %copy-start = (f32[1,2,32,896]{3,2,1,0:T(8,128)S(1)}, f32[1,2,32,896]{3,2,1,0:T(8,128)}, u32[]{:S(2)}) copy-start(f32[1,2,32,896]{3,2,1,0:T(8,128)} %param.7) | copy-start | bytes 688132
  6.3 0.7 %copy-start.5 = (f32[2,2,2]{2,1,0:T(2,128)S(1)}, f32[2,2,2]{2,1,0:T(2,128)}, u32[]{:S(2)}) copy-start(f32[2,2,2]{2,1,0:T(2,128)} %paths.1) | copy-start | bytes 100
  7.0 11.5 %copy-start.7 = (s32[3,14]{1,0:T(4,128)S(1)}, s32[3,14]{1,0:T(4,128)}, u32[]{:S(2)}) copy-start(s32[3,14]{1,0:T(4,128)} %get-tuple-element.15.scalars) | copy-start | bytes 508
  7.0 11.5 %copy-start.8 = (bf16[1,1,14,128,128]{4,3,2,1,0:T(8,128)(2,1)S(1)}, bf16[1,1,14,128,128]{4,3,2,1,0:T(8,128)(2,1)}, u32[]{:S(2)}) copy-start(bf16[1,1,14,128,128]{4,3,2,1,0:T(8,128)(2,1)} %param.10) | copy-start | bytes 1376260
  8.8 3.4 %collective-permute-start.2 = (f32[28,8,128]{2,1,0:T(8,128)S(1)}, f32[28,8,128]{2,1,0:T(8,128)S(1)}, u32[]{:S(2)}, u32[]{:S(2)}) collective-permute-start(f32[28,8,128]{2,1,0:T(8,128)S(1)} %add.35.own), channel_id=1, source_target_pairs={{0,1},{1,0},{2,4},{3,5},{4,2},{5,3},{6,8},{7,9},{8,6},{9,7},{10,12... | collective-permute-start | bytes 344072 | tf_op jit(solution)/shard_map/ppermute | solution.py:429
  8.8 6.7 %collective-permute-start.1 = (f32[28,8,128]{2,1,0:T(8,128)S(1)}, f32[28,8,128]{2,1,0:T(8,128)S(1)}, u32[]{:S(2)}, u32[]{:S(2)}) collective-permute-start(f32[28,8,128]{2,1,0:T(8,128)S(1)} %add.35.own), channel_id=1, source_target_pairs={{0,2},{1,3},{2,0},{3,1},{4,6},{5,7},{6,4},{7,5},{8,10},{9,11},{10,... | collective-permute-start | bytes 344072 | tf_op jit(solution)/shard_map/ppermute | solution.py:429
  15.5 2.9 %collective-permute-start.3 = (f32[56,8,128]{2,1,0:T(8,128)S(1)}, f32[56,8,128]{2,1,0:T(8,128)S(1)}, u32[]{:S(2)}, u32[]{:S(2)}) collective-permute-start(f32[56,8,128]{2,1,0:T(8,128)S(1)} %pad_maximum_fusion), channel_id=1, source_target_pairs={{0,1},{1,0},{2,3},{3,2},{4,5},{5,4},{6,7},{7,6},{8,9},{9,8},{10,11... | collective-permute-start | bytes 688136 | tf_op jit(solution)/shard_map/ppermute | solution.py:429
  15.6 1.0 %copy-start.2 = (bf16[4,256,256]{2,1,0:T(8,128)(2,1)S(1)}, bf16[4,256,256]{2,1,0:T(8,128)(2,1)}, u32[]{:S(2)}) copy-start(bf16[4,256,256]{2,1,0:T(8,128)(2,1)} %constant.36.clone.tables) | copy-start | bytes 1572868
  16.7 0.7 %copy-start.6 = (s32[3,14]{1,0:T(4,128)S(1)}, s32[3,14]{1,0:T(4,128)}, u32[]{:S(2)}) copy-start(s32[3,14]{1,0:T(4,128)} %get-tuple-element.15.scalars) | copy-start | bytes 508
  18.5 26.4 %copy-start.1 = (f32[1,2,32,896]{3,2,1,0:T(8,128)S(1)}, f32[1,2,32,896]{3,2,1,0:T(8,128)}, u32[]{:S(2)}) copy-start(f32[1,2,32,896]{3,2,1,0:T(8,128)} %param.7) | copy-start | bytes 688132
  18.5 26.4 %copy-start.4 = (f32[2,2,8,128]{3,2,1,0:T(8,128)S(1)}, f32[2,2,8,128]{3,2,1,0:T(8,128)}, u32[]{:S(2)}) copy-start(f32[2,2,8,128]{3,2,1,0:T(8,128)} %get-tuple-element.14.factors) | copy-start | bytes 49156
  23.2 1.7 %collective-permute-start.4 = (f32[56,8,128]{2,1,0:T(8,128)S(1)}, f32[56,8,128]{2,1,0:T(8,128)S(1)}, u32[]{:S(2)}, u32[]{:S(2)}) collective-permute-start(f32[56,8,128]{2,1,0:T(8,128)S(1)} %get-tuple-element.20), channel_id=1, source_target_pairs={{0,1},{1,0},{2,3},{3,2},{4,5},{5,4},{6,7},{7,6},{8,9},{9,8},{10,11... | collective-permute-start | bytes 688136 | tf_op jit(solution)/shard_map/ppermute | solution.py:429
  24.9 13.3 %collective-permute-start.6 = (f32[28,8,128]{2,1,0:T(8,128)S(1)}, f32[28,8,128]{2,1,0:T(8,128)S(1)}, u32[]{:S(2)}, u32[]{:S(2)}) collective-permute-start(f32[28,8,128]{2,1,0:T(8,128)S(1)} %get-tuple-element.26), channel_id=1, source_target_pairs={{0,2},{1,3},{2,0},{3,1},{4,6},{5,7},{6,4},{7,5},{8,10},{9,11},{10,... | collective-permute-start | bytes 344072 | tf_op jit(solution)/shard_map/ppermute | solution.py:429
  27.4 10.8 %collective-permute-start.5 = (f32[28,8,128]{2,1,0:T(8,128)S(1)}, f32[28,8,128]{2,1,0:T(8,128)S(1)}, u32[]{:S(2)}, u32[]{:S(2)}) collective-permute-start(f32[28,8,128]{2,1,0:T(8,128)S(1)} %get-tuple-element.27), channel_id=1, source_target_pairs={{0,1},{1,0},{2,4},{3,5},{4,2},{5,3},{6,8},{7,9},{8,6},{9,7},{10,12... | collective-permute-start | bytes 344072 | tf_op jit(solution)/shard_map/ppermute | solution.py:429
  27.5 5.0 %collective-permute-start.7 = (f32[1,8,128]{2,1,0:T(8,128)S(1)}, f32[1,8,128]{2,1,0:T(8,128)S(1)}, u32[]{:S(2)}, u32[]{:S(2)}) collective-permute-start(f32[1,8,128]{2,1,0:T(8,128)S(1)} %get-tuple-element.23), channel_id=1, source_target_pairs={{0,4},{1,5},{2,6},{3,7},{4,0},{5,1},{6,2},{7,3},{8,12},{9,13},{10,... | collective-permute-start | bytes 12296 | tf_op jit(solution)/shard_map/ppermute | solution.py:429
  32.5 1.2 %collective-permute-start.8 = (f32[1,8,128]{2,1,0:T(8,128)S(1)}, f32[1,8,128]{2,1,0:T(8,128)S(1)}, u32[]{:S(2)}, u32[]{:S(2)}) collective-permute-start(f32[1,8,128]{2,1,0:T(8,128)S(1)} %add.43), channel_id=1, source_target_pairs={{0,1},{1,0},{2,3},{3,2},{4,5},{5,4},{6,7},{7,6},{8,9},{9,8},{10,11... | collective-permute-start | bytes 12296 | tf_op jit(solution)/shard_map/ppermute | solution.py:429
  33.7 4.5 %collective-permute-start.9 = (f32[1,8,128]{2,1,0:T(8,128)S(1)}, f32[1,8,128]{2,1,0:T(8,128)S(1)}, u32[]{:S(2)}, u32[]{:S(2)}) collective-permute-start(f32[1,8,128]{2,1,0:T(8,128)S(1)} %add.44), channel_id=1, source_target_pairs={{0,8},{1,9},{2,10},{3,11},{4,12},{5,13},{6,14},{7,15},{8,0},{9,1},... | collective-permute-start | bytes 12296 | tf_op jit(solution)/shard_map/ppermute | solution.py:429
  38.3 6.7 %collective-permute-start.10 = (f32[29,8,128]{2,1,0:T(8,128)S(1)}, f32[29,8,128]{2,1,0:T(8,128)S(1)}, u32[]{:S(2)}, u32[]{:S(2)}) collective-permute-start(f32[29,8,128]{2,1,0:T(8,128)S(1)} %pad_maximum_fusion.1), channel_id=1, source_target_pairs={{0,16},{16,0},{1,17},{17,1},{2,18},{18,2},{3,19},{19,3},{4,20},{20... | collective-permute-start | bytes 356360 | tf_op jit(solution)/shard_map/ppermute | solution.py:463
  39.8 4.5 %collective-permute-start.12 = (f32[1,8,128]{2,1,0:T(8,128)S(1)}, f32[1,8,128]{2,1,0:T(8,128)S(1)}, u32[]{:S(2)}, u32[]{:S(2)}) collective-permute-start(f32[1,8,128]{2,1,0:T(8,128)S(1)} %add.45.refs_2_), channel_id=1, source_target_pairs={{0,18},{1,19},{2,16},{3,17},{4,22},{5,23},{6,20},{7,21},{8,26},{9,... | collective-permute-start | bytes 12296 | tf_op jit(solution)/shard_map/ppermute | solution.py:497
  41.3 3.6 %collective-permute-start.11 = (f32[1,8,128]{2,1,0:T(8,128)S(1)}, f32[1,8,128]{2,1,0:T(8,128)S(1)}, u32[]{:S(2)}, u32[]{:S(2)}) collective-permute-start(f32[1,8,128]{2,1,0:T(8,128)S(1)} %add.45.refs_2_), channel_id=1, source_target_pairs={{0,2},{1,3},{2,0},{3,1},{4,6},{5,7},{6,4},{7,5},{8,10},{9,11},{10,... | collective-permute-start | bytes 12296 | tf_op jit(solution)/shard_map/ppermute | solution.py:429

commit v5 on v4

--- a/solution.py
+++ b/solution.py
@@ -14,6 +14,8 @@
 JIT = 16
 FLOOR_RATIO = 4.0
 LANES = 128
+TALL = 4
+BROAD = 2
 SUBS = 8
 HALF_PI = (1.5703125, 4.837512969970703125e-4, 7.54978995489188216e-8)
 
@@ -91,12 +93,12 @@
         scalars[0, p] = jitter[0, p]
         scalars[1, p] = jitter[1, p]
         scalars[2, p] = 0
-    scalars[2, 0] = lax.rem(column, 2)
+    second = lax.rem(column, 2)
+    scalars[2, 0] = second
     scalars[2, 1] = lax.rem(column // 2, 2)
     scalars[2, 2] = (column >= 2).astype(jnp.int32)
-    scalars[2, 3] = (column >= 1).astype(jnp.int32)
-    scalars[2, 4] = (column + 1 < columns).astype(jnp.int32)
-    scalars[2, 5] = (column + 2 < columns).astype(jnp.int32)
+    scalars[2, 3] = (column + 2 < columns).astype(jnp.int32)
+    scalars[2, 4] = jnp.where(second == 1, column + 1 < columns, column >= 1).astype(jnp.int32)
     layers, rows, cols = slab.shape
     for step in range(groups):
         source = lax.rem(group - step + groups, groups)
@@ -137,22 +139,26 @@
     return out[: groups - 1], out[groups - 1], out[groups]
 
 
-def own_kernel(slab, paths, term):
+def own_kernel(slab, paths, tables, term, kept):
     group = lax.axis_index("blk")
     for i, r, c in blocks_of(*slab.shape[1:]):
         term[i] = term_of(slab, paths, group, group, r, c)
-
-
-def own_term(slab, paths):
+    for i in range(tables.shape[0]):
+        kept[i] = tables[i]
+
+
+def own_term(slab, paths, patch):
+    vmem = pl.BlockSpec(memory_space=pltpu.VMEM)
+    tables = dft_tables(patch)
     return pl.pallas_call(
         own_kernel,
-        out_shape=listed(slab),
-        in_specs=[pl.BlockSpec(memory_space=pltpu.VMEM), pl.BlockSpec(memory_space=pltpu.SMEM)],
-        out_specs=pl.BlockSpec(memory_space=pltpu.VMEM),
+        out_shape=(listed(slab), jax.ShapeDtypeStruct(tables.shape, tables.dtype)),
+        in_specs=[vmem, pl.BlockSpec(memory_space=pltpu.SMEM), vmem],
+        out_specs=(vmem, vmem),
         compiler_params=pltpu.CompilerParams(vmem_limit_bytes=8 * 1024 * 1024),
         cost_estimate=pl.CostEstimate(flops=2**24, bytes_accessed=2**20, transcendentals=0),
         name="own",
-    )(slab, paths)
+    )(slab, paths, tables)
 
 
 def update_kernel(count, slab, factors, *refs):
@@ -183,7 +189,10 @@
     )(slab, factors, *grads, *sums)
 
 
-def prepare_kernel(number, scalars, probe, tables, rolled, kept, twice):
+FLAGS = ("second", "lower", "up2", "dn2", "relay")
+
+
+def prepare_kernel(number, scalars, probe, rolled, frames, twice):
     patch = probe.shape[1]
     for half in range(2):
         for part in range(2):
@@ -191,39 +200,76 @@
     for p in range(number):
         _, corner = window_place(p, patch)
         shift = corner + scalars[1, p]
-        start = patch - ROWS_DEV // 4 - scalars[0, p]
+        top = ROWS_DEV // 4 + scalars[0, p]
+        start = patch - top
         for part in range(2):
             value = pltpu.roll(twice[part, pl.ds(start, patch), :], shift, 1)
             rolled[p * patch : (p + 1) * patch, part * LANES : (part + 1) * LANES] = value
-    for i in range(tables.shape[0]):
-        kept[i] = tables[i]
+        frames[p] = jnp.full((SUBS, LANES), shift, jnp.int32)
+        frames[number + p] = jnp.full((SUBS, LANES), top, jnp.int32)
+    for i in range(len(FLAGS)):
+        frames[2 * number + i] = jnp.full((SUBS, LANES), scalars[2, i], jnp.int32)
 
 
 def prepared(scalars, probe):
     number, patch = scalars.shape[1], probe.shape[1]
-    tables = dft_tables(patch)
     vmem = pl.BlockSpec(memory_space=pltpu.VMEM)
     return pl.pallas_call(
         functools.partial(prepare_kernel, number),
         out_shape=(
             jax.ShapeDtypeStruct((number * patch, 2 * LANES), jnp.float32),
-            jax.ShapeDtypeStruct(tables.shape, tables.dtype),
+            jax.ShapeDtypeStruct((2 * number + len(FLAGS), SUBS, LANES), jnp.int32),
         ),
-        in_specs=[pl.BlockSpec(memory_space=pltpu.SMEM), vmem, vmem],
+        in_specs=[pl.BlockSpec(memory_space=pltpu.SMEM), vmem],
         out_specs=(vmem, vmem),
         scratch_shapes=[pltpu.VMEM((2, 2 * patch, patch), jnp.float32)],
         compiler_params=pltpu.CompilerParams(vmem_limit_bytes=16 * 1024 * 1024),
         cost_estimate=pl.CostEstimate(flops=2**27, bytes_accessed=2**22, transcendentals=0),
         name="prepare",
-    )(scalars, probe, tables)
+    )(scalars, probe)
+
+
+def flag_of(frames, name):
+    return frames[frames.shape[0] - len(FLAGS) + FLAGS.index(name)] == 1
+
+
+def phases_kernel(frames, own, mate, pair, next_pair, real, imag):
+    blocks = own.shape[0]
+    lower = flag_of(frames, "lower")
+    up2_ok = jnp.where(flag_of(frames, "up2"), 1.0, 0.0)
+    dn2_ok = jnp.where(flag_of(frames, "dn2"), 1.0, 0.0)
+    unused = ROWS_DEV // 4 // SUBS * (blocks * SUBS // ROWS_DEV)
+    for i in range(blocks):
+        s, c = sin_cos(own[i])
+        real[2 * blocks + i], imag[2 * blocks + i] = c, s
+        s, c = sin_cos(mate[i])
+        real[blocks + i], imag[blocks + i] = c, s
+        if i >= unused:
+            s, c = sin_cos(jnp.where(lower, pair[i], next_pair[i]))
+            real[i], imag[i] = c * up2_ok, s * up2_ok
+        if i < blocks - unused:
+            s, c = sin_cos(jnp.where(lower, next_pair[i], pair[i]))
+            real[4 * blocks + i], imag[4 * blocks + i] = c * dn2_ok, s * dn2_ok
+
+
+def phases(frames, own, mate, pair, next_pair):
+    vmem = pl.BlockSpec(memory_space=pltpu.VMEM)
+    out = jax.ShapeDtypeStruct((5 * own.shape[0], SUBS, LANES), jnp.float32)
+    return pl.pallas_call(
+        phases_kernel,
+        out_shape=(out, out),
+        in_specs=[vmem] * 5,
+        out_specs=(vmem, vmem),
+        compiler_params=pltpu.CompilerParams(vmem_limit_bytes=8 * 1024 * 1024),
+        cost_estimate=pl.CostEstimate(flops=2**27, bytes_accessed=2**22, transcendentals=0),
+        name="phases",
+    )(frames, own, mate, pair, next_pair)
 
 
 def strip_kernel(
-    scalars,
-    own,
-    mate,
-    pair,
-    next_pair,
+    frames,
+    here_real,
+    here_imag,
     relay,
     rolled,
     measured,
@@ -233,63 +279,50 @@
     by_pair,
     by_next,
     misfit,
-    obj_real,
-    obj_imag,
+    side_real,
+    side_imag,
     wave,
     mid,
     back,
 ):
     number, patch, _ = measured.shape
     rows = ROWS_DEV
-    tiles = own.shape[0] * SUBS // rows
-    far = rows - ROWS_DEV // 4
+    blocks = relay.shape[0]
+    tiles = blocks * SUBS // rows
     near = ROWS_DEV // 4 + JIT
     dot = functools.partial(lax.dot, preferred_element_type=jnp.float32)
-    jitter = scalars
-
-    def flag(index):
-        return jnp.full((SUBS, LANES), scalars[2, index], jnp.int32) == 1
-
-    is_second = flag(0)
-    is_lower = flag(1)
+    is_second = flag_of(frames, "second")
+    is_lower = flag_of(frames, "lower")
     fwd_high, fwd_low, inv_high, inv_low = (tables[i] for i in range(4))
 
-    def put(row, tile, phase, index):
-        s, c = sin_cos(phase)
-        if index is not None:
-            ok = scalars[2, index].astype(jnp.float32)
-            s = s * ok
-            c = c * ok
-        obj_real[row // SUBS * tiles + tile] = c
-        obj_imag[row // SUBS * tiles + tile] = s
-
-    for i, r, c in blocks_of(rows, tiles * LANES):
-        t = c // LANES
-        put(2 * rows + r, t, own[i], None)
-        put(rows + r, t, jnp.where(is_second, mate[i], relay[i]), 3)
-        put(3 * rows + r, t, jnp.where(is_second, relay[i], mate[i]), 4)
-        if r >= rows - far:
-            put(r, t, jnp.where(is_lower, pair[i], next_pair[i]), 2)
-        if r < far:
-            put(4 * rows + r, t, jnp.where(is_lower, next_pair[i], pair[i]), 5)
+    relay_ok = jnp.where(flag_of(frames, "relay"), 1.0, 0.0)
+    for i in range(blocks):
+        s, c = sin_cos(relay[i])
+        c, s = c * relay_ok, s * relay_ok
+        mate_c, mate_s = here_real[blocks + i], here_imag[blocks + i]
+        side_real[i] = jnp.where(is_second, mate_c, c)
+        side_imag[i] = jnp.where(is_second, mate_s, s)
+        side_real[blocks + i] = jnp.where(is_second, c, mate_c)
+        side_imag[blocks + i] = jnp.where(is_second, s, mate_s)
+    obj_real = (here_real, side_real)
+    obj_imag = (here_imag, side_imag)
 
     lane = lax.broadcasted_iota(jnp.int32, (SUBS, LANES), 1)
     sub = lax.broadcasted_iota(jnp.int32, (SUBS, LANES), 0)
 
-    def first_row(p):
-        return ROWS_DEV // 4 + jitter[0, p]
-
     def masks(p):
-        _, corner = window_place(p, patch)
-        after = lane >= corner + jitter[1, p]
-        below = [sub + k * SUBS >= first_row(p) for k in range(near // SUBS)]
+        after = lane >= frames[p]
+        below = [sub + k * SUBS >= frames[number + p] for k in range(near // SUBS)]
         return after, below
 
-    def pick(ref, p, k, after, below):
+    def pick(refs, p, k, after, below):
         tile, _ = window_place(p, patch)
 
         def at(row):
+            slot, ref = row // rows, refs[0]
             first = row // SUBS * tiles + tile
+            if slot in (1, 3):
+                ref, first = refs[1], first - (slot + 1) // 2 * blocks
             left = ref[first] if tile >= 0 else 0.0
             right = ref[first + 1] if tile + 1 < tiles else 0.0
             return jnp.where(after, left, right)
@@ -319,43 +352,49 @@
             wave[row : row + SUBS, :LANES] = a * o_real - b * o_imag
             wave[row : row + SUBS, LANES:] = a * o_imag + b * o_real
 
-    for p in range(0, number, 2):
-        high, low = parts_of(wave[p * patch : (p + 2) * patch, :])
-        mid[p * patch : (p + 2) * patch, :] = against(high, low, fwd_high, fwd_low)
+    for p in range(0, number, TALL):
+        span = slice(p * patch, min(p + TALL, number) * patch)
+        high, low = parts_of(wave[span, :])
+        mid[span, :] = against(high, low, fwd_high, fwd_low)
 
     def upright(value):
-        top = jnp.concatenate([value[:patch, :LANES], value[patch:, :LANES]], 1)
-        low = jnp.concatenate([value[:patch, LANES:], value[patch:, LANES:]], 1)
-        return jnp.concatenate([top, low], 0)
+        count = value.shape[0] // patch
+        parts = [
+            jnp.concatenate([value[i * patch : (i + 1) * patch, lanes] for i in range(count)], 1)
+            for lanes in (slice(0, LANES), slice(LANES, 2 * LANES))
+        ]
+        return jnp.concatenate(parts, 0)
 
     total = jnp.zeros((SUBS, LANES), jnp.float32)
-    for p in range(0, number, 2):
-        high, low = parts_of(upright(mid[p * patch : (p + 2) * patch, :]))
+    for p in range(0, number, BROAD):
+        count = min(BROAD, number - p)
+        high, low = parts_of(upright(mid[p * patch : (p + count) * patch, :]))
         spectrum = onto(inv_high, inv_low, high, low)
         real, imag = spectrum[:patch], spectrum[patch:]
-        target = jnp.concatenate([measured[p], measured[p + 1]], 1).astype(jnp.float32)
+        target = jnp.concatenate([measured[p + i] for i in range(count)], 1).astype(jnp.float32)
         power = real * real + imag * imag
         inverse = lax.rsqrt(jnp.maximum(power, 1e-30))
         error = power * inverse - target
         square = error * error
         for k in range(steps):
-            for half in range(2):
+            for half in range(count):
                 total += square[k * SUBS : (k + 1) * SUBS, half * LANES : (half + 1) * LANES]
         ratio = target * jnp.minimum(inverse, FLOOR_RATIO)
         high, low = parts_of(jnp.concatenate([ratio * real, ratio * imag], 0))
         undone = onto(fwd_high, fwd_low, high, low)
-        for half in range(2):
+        for half in range(count):
             row = (p + half) * patch
             lanes = slice(half * LANES, (half + 1) * LANES)
             back[row : row + patch, :LANES] = undone[:patch, lanes]
             back[row : row + patch, LANES:] = undone[patch:, lanes]
     misfit[0] = total
 
-    for p in range(0, number, 2):
-        high, low = parts_of(back[p * patch : (p + 2) * patch, :])
+    for p in range(0, number, TALL):
+        span = slice(p * patch, min(p + TALL, number) * patch)
+        high, low = parts_of(back[span, :])
         out = against(high, low, inv_high, inv_low)
-        w = wave[p * patch : (p + 2) * patch, :]
-        mid[p * patch : (p + 2) * patch, :LANES] = w[:, :LANES] * out[:, LANES:] - w[:, LANES:] * out[:, :LANES]
+        w = wave[span, :]
+        mid[span, :LANES] = w[:, :LANES] * out[:, LANES:] - w[:, LANES:] * out[:, :LANES]
 
     grads = {}
     for t in range(tiles):
@@ -389,16 +428,15 @@
         up2, up1, here, dn1, dn2 = (add_to(slot, r, c // LANES) for slot in range(5))
         mine[i] = here
         to_mate[i] = jnp.where(is_second, up1, dn1)
-        to_mate[own.shape[0] + i] = jnp.where(is_second, dn1, up1)
+        to_mate[blocks + i] = jnp.where(is_second, dn1, up1)
         by_pair[i] = jnp.where(is_lower, up2, dn2)
         by_next[i] = jnp.where(is_lower, dn2, up2)
 
 
-def strip_gradient(scalars, own, mate, pair, next_pair, relay, rolled, measured, tables):
+def strip_gradient(frames, here, relay, rolled, measured, tables):
     number, patch, _ = measured.shape
-    blocks = own.shape[0]
+    blocks = relay.shape[0]
     vmem = pl.BlockSpec(memory_space=pltpu.VMEM)
-    smem = pl.BlockSpec(memory_space=pltpu.SMEM)
 
     def block_list(count):
         return jax.ShapeDtypeStruct((count, SUBS, LANES), jnp.float32)
@@ -406,11 +444,11 @@
     return pl.pallas_call(
         strip_kernel,
         out_shape=tuple(block_list(n) for n in (blocks, 2 * blocks, blocks, blocks, 1)),
-        in_specs=[smem] + [vmem] * 8,
+        in_specs=[vmem] * 7,
         out_specs=(vmem,) * 5,
         scratch_shapes=[
-            pltpu.VMEM((5 * blocks, SUBS, LANES), jnp.float32),
-            pltpu.VMEM((5 * blocks, SUBS, LANES), jnp.float32),
+            pltpu.VMEM((2 * blocks, SUBS, LANES), jnp.float32),
+            pltpu.VMEM((2 * blocks, SUBS, LANES), jnp.float32),
             pltpu.VMEM((number * patch, 2 * LANES), jnp.float32),
             pltpu.VMEM((number * patch, 2 * LANES), jnp.float32),
             pltpu.VMEM((number * patch, 2 * LANES), jnp.float32),
@@ -420,7 +458,7 @@
             flops=24 * number * patch**3 * 4, bytes_accessed=4 * number * patch * patch, transcendentals=0
         ),
         name="strip",
-    )(scalars, own, mate, pair, next_pair, relay, rolled, measured, tables)
+    )(frames, *here, relay, rolled, measured, tables)
 
 
 def permuted(value, axis, target):
@@ -463,20 +501,19 @@
         return lax.ppermute(value, "blk", [(i, (i + step) % groups) for i in range(groups)])
 
     terms, factors, scalars = slab_terms(slab, path_lengths, jitter[:, 0, 0], step_sizes, groups)
-    own = own_term(slab, path_lengths)
+    own, tables = own_term(slab, path_lengths, probe.shape[-1])
     for step in range(1, groups):
         own = own + to_group(terms[step - 1], step)
 
     even = column % 2 == column // 2 % 2
     next_pair = across(own)
     pair = with_pair(own)
-    rolled, tables = prepared(scalars, probe)
-    both = with_mate(jnp.concatenate([own, jnp.where(even, pair, next_pair)], 0))
+    mate = with_mate(own)
+    rolled, frames = prepared(scalars, probe)
+    relay = with_mate(jnp.where(even, pair, next_pair))
+    here = phases(frames, own, mate, pair, next_pair)
     blocks = own.shape[0]
-    mate, relay = both[:blocks], both[blocks:]
-    mine, to_mate, by_pair, by_next, local = strip_gradient(
-        scalars, own, mate, pair, next_pair, relay, rolled, measured[0, 0], tables
-    )
+    mine, to_mate, by_pair, by_next, local = strip_gradient(frames, here, relay, rolled, measured[0, 0], tables)
     got = with_mate(to_mate)
     if groups != 2:
         local = joined(local, "blk", [2**k for k in range(groups.bit_length() - 1)])

time: 46 us -> 45.6 us (level)
  local copies, waits for them, and re-layouts: 3.38 us -> 4.24 us
  waiting for transfers between devices: 15.2 us -> 14.5 us
  Pallas kernels: 8.79 us -> 8.32 us
    ppermute x2, waiting for transfers between devices: 1.11 us -> 0.07 us  [to_group(): lax.ppermute(value, 'blk', [(i, (i + step) % groups) for i in range(group...]
    pallas_call x1, Pallas kernels: 4.61 us -> 3.61 us  [strip_gradient(): pl.pallas_call(strip_kernel, out_shape=tuple((block_list(n) for n in (blo...]
    unnamed x18 -> x16, local copies, waits for them, and re-layouts: 3.36 us -> 4.24 us
    pallas_call x1 -> x2, Pallas kernels: 0.61 us -> 1.18 us  [the longest x1 0.62 us: own_term(): pl.pallas_call(own_kernel, out_shape=(listed(slab), jax.ShapeDtypeStruct(...]
    ppermute x10 -> x11, waiting for transfers between devices: 11.6 us -> 12 us  [permuted(): return lax.ppermute(value, axis, pairs)]
    ppermute x10 -> x11, starting transfers between devices: 11.3 us -> 11.3 us  [permuted(): return lax.ppermute(value, axis, pairs)]
  transfers between devices with their start and end apart: 13 -> 14, of which waited for: 8 -> 8; matrix products, arithmetic and copies ran while one was open for 0% -> 0% of each run, Pallas kernels for 4% -> 5%
where the time goes in v5:
time: 45.6 us; the launch traced here: 45.3 us
  starting transfers between devices  17.4 us (38%)
  waiting for transfers between devices  14.5 us (32%)
  Pallas kernels  8.32 us (18%)
  local copies, waits for them, and re-layouts  4.24 us (9%)
  between operations  0.76 us (2%)
    ppermute x11, waiting for transfers between devices, permuted(): return lax.ppermute(value, axis, pairs)  12 us
    ppermute x11, starting transfers between devices, permuted(): return lax.ppermute(value, axis, pairs)  11.3 us
    ppermute x2, starting transfers between devices, to_group(): lax.ppermute(value, 'blk', [(i, (i + step) % groups) for i in range(group...  4.31 us
    unnamed x16, local copies, waits for them, and re-layouts  4.24 us
    pallas_call x1, Pallas kernels, strip_gradient(): pl.pallas_call(strip_kernel, out_shape=tuple((block_list(n) for n in (blo...  3.61 us
    ppermute x1, waiting for transfers between devices, program(): sums.append(lax.ppermute(local, ('blk', 'wide'), pairs))  2.36 us
    ppermute x1, starting transfers between devices, program(): sums.append(lax.ppermute(local, ('blk', 'wide'), pairs))  1.78 us
    pallas_call x1, Pallas kernels, slab_terms(): pl.pallas_call(functools.partial(terms_kernel, groups), out_shape=[listed...  1.67 us
  transfers between devices with their start and end apart: 14, of which 8 were waited for; matrix products, arithmetic and copies ran while one was open for 0% of the time, Pallas kernels for 5%

profile of v5, /device:TPU:0, one launch (start us, length us, event | category | flops | bytes accessed | tf_op | source)
XLA Modules:
  0.0 45.3 jit_solution(18379079417455260087)
XLA Ops:
  0.6 1.7 %terms.1 = (f32[28,8,128]{2,1,0:T(8,128)}, f32[2,2,8,128]{3,2,1,0:T(8,128)}, s32[3,14]{1,0:T(4,128)}) custom-call(f32[2,32,896]{2,1,0:T(8,128)} %bitcast.5, f32[2,2,2]{2,1,0:T(2,128)} %paths.1, s32[2,14]{1,0:T(2,128)} %bitcast.9, f32[2]{0:T(128)} %steps_hbm.1), custom_call_target="tpu_custom_call" | custom-call | tf_op jit(solution)/shard_map/terms/pallas_call | solution.py:121
  2.3 3.0 %collective-permute-start = (f32[28,8,128]{2,1,0:T(8,128)}, f32[28,8,128]{2,1,0:T(8,128)S(1)}, u32[]{:S(2)}, u32[]{:S(2)}) collective-permute-start(f32[28,8,128]{2,1,0:T(8,128)} %get-tuple-element.22), channel_id=1, source_target_pairs={{0,16},{16,0},{1,17},{17,1},{2,18},{18,2},{3,19},{19,3},{4,20},{20... | collective-permute-start | bytes 344072 | tf_op jit(solution)/shard_map/ppermute | solution.py:501
  5.3 0.9 %copy-done = f32[1,2,32,896]{3,2,1,0:T(8,128)S(1)} copy-done((f32[1,2,32,896]{3,2,1,0:T(8,128)S(1)}, f32[1,2,32,896]{3,2,1,0:T(8,128)}, u32[]{:S(2)}) %copy-start) | copy-done | bytes 229400
  6.3 1.0 %copy-done.2 = bf16[4,256,256]{2,1,0:T(8,128)(2,1)S(1)} copy-done((bf16[4,256,256]{2,1,0:T(8,128)(2,1)S(1)}, bf16[4,256,256]{2,1,0:T(8,128)(2,1)}, u32[]{:S(2)}) %copy-start.2) | copy-done | bytes 524312
  7.3 0.7 %copy-done.4 = f32[2,2,2]{2,1,0:T(2,128)S(1)} copy-done((f32[2,2,2]{2,1,0:T(2,128)S(1)}, f32[2,2,2]{2,1,0:T(2,128)}, u32[]{:S(2)}) %copy-start.4) | copy-done | bytes 56
  8.0 0.6 %own.1 = (f32[28,8,128]{2,1,0:T(8,128)S(1)}, bf16[4,256,256]{2,1,0:T(8,128)(2,1)S(1)}) custom-call(f32[2,32,896]{2,1,0:T(8,128)S(1)} %bitcast.6, f32[2,2,2]{2,1,0:T(2,128)S(1)} %copy-done.4, bf16[4,256,256]{2,1,0:T(8,128)(2,1)S(1)} %copy-done.2), custom_call_target="tpu_custom_call" | custom-call | flops 16777216 | bytes 1048576 | tf_op jit(solution)/shard_map/own/pallas_call | solution.py:153
  8.8 3.3 %collective-permute-start.2 = (f32[28,8,128]{2,1,0:T(8,128)S(1)}, f32[28,8,128]{2,1,0:T(8,128)S(1)}, u32[]{:S(2)}, u32[]{:S(2)}) collective-permute-start(f32[28,8,128]{2,1,0:T(8,128)S(1)} %add.35.own), channel_id=1, source_target_pairs={{0,2},{1,3},{2,0},{3,1},{4,6},{5,7},{6,4},{7,5},{8,10},{9,11},{10,... | collective-permute-start | bytes 344072 | tf_op jit(solution)/shard_map/ppermute | solution.py:467
  12.1 3.7 %collective-permute-done.2.pair = f32[28,8,128]{2,1,0:T(8,128)S(1)} collective-permute-done((f32[28,8,128]{2,1,0:T(8,128)S(1)}, f32[28,8,128]{2,1,0:T(8,128)S(1)}, u32[]{:S(2)}, u32[]{:S(2)}) %collective-permute-start.2) | collective-permute-done | bytes 114720 | tf_op jit(solution)/shard_map/ppermute | solution.py:467
  15.8 0.9 %copy-done.6 = f32[2,128,128]{2,1,0:T(8,128)S(1)} copy-done((f32[2,128,128]{2,1,0:T(8,128)S(1)}, f32[2,128,128]{2,1,0:T(8,128)}, u32[]{:S(2)}) %copy-start.6) | copy-done | bytes 131096
  16.7 0.7 %copy-done.7 = s32[3,14]{1,0:T(4,128)S(1)} copy-done((s32[3,14]{1,0:T(4,128)S(1)}, s32[3,14]{1,0:T(4,128)}, u32[]{:S(2)}) %copy-start.7) | copy-done | bytes 192
  17.4 1.1 %prepare.1 = (f32[1792,256]{1,0:T(8,128)S(1)}, s32[33,8,128]{2,1,0:T(8,128)S(1)}) custom-call(s32[3,14]{1,0:T(4,128)S(1)} %copy-done.7, f32[2,128,128]{2,1,0:T(8,128)S(1)} %copy-done.6), custom_call_target="tpu_custom_call" | custom-call | flops 134217728 | bytes 4194304 | tf_op jit(solution)/shard_map/prepare/pallas_call | solution.py:217
  19.1 3.6 %strip.1 = (f32[28,8,128]{2,1,0:T(8,128)S(1)}, f32[56,8,128]{2,1,0:T(8,128)S(1)}, f32[28,8,128]{2,1,0:T(8,128)S(1)}, f32[28,8,128]{2,1,0:T(8,128)S(1)}, f32[1,8,128]{2,1,0:T(8,128)S(1)}) custom-call(s32[33,8,128]{2,1,0:T(8,128)S(1)} %get-tuple-element.20.frames, f32[140,8,128]{2,1,0:T(8,128)S(1)} %get-tuple-element.23.here_real, ...), custom_call_target="tpu_custom_call" | custom-call | flops 2818572288 | bytes 917504 | tf_op jit(solution)/shard_map/strip/pallas_call | solution.py:444
  23.3 1.1 %collective-permute-done.5 = f32[56,8,128]{2,1,0:T(8,128)S(1)} collective-permute-done((f32[56,8,128]{2,1,0:T(8,128)S(1)}, f32[56,8,128]{2,1,0:T(8,128)S(1)}, u32[]{:S(2)}, u32[]{:S(2)}) %collective-permute-start.5) | collective-permute-done | bytes 229408 | tf_op jit(solution)/shard_map/ppermute | solution.py:467
  24.5 2.5 %collective-permute-start.7 = (f32[28,8,128]{2,1,0:T(8,128)S(1)}, f32[28,8,128]{2,1,0:T(8,128)S(1)}, u32[]{:S(2)}, u32[]{:S(2)}) collective-permute-start(f32[28,8,128]{2,1,0:T(8,128)S(1)} %get-tuple-element.34), channel_id=1, source_target_pairs={{0,2},{1,3},{2,0},{3,1},{4,6},{5,7},{6,4},{7,5},{8,10},{9,11},{10,... | collective-permute-start | bytes 344072 | tf_op jit(solution)/shard_map/ppermute | solution.py:467
  27.1 1.5 %collective-permute-start.8 = (f32[1,8,128]{2,1,0:T(8,128)S(1)}, f32[1,8,128]{2,1,0:T(8,128)S(1)}, u32[]{:S(2)}, u32[]{:S(2)}) collective-permute-start(f32[1,8,128]{2,1,0:T(8,128)S(1)} %get-tuple-element.31), channel_id=1, source_target_pairs={{0,4},{1,5},{2,6},{3,7},{4,0},{5,1},{6,2},{7,3},{8,12},{9,13},{10,... | collective-permute-start | bytes 12296 | tf_op jit(solution)/shard_map/ppermute | solution.py:467
  28.6 3.5 %collective-permute-done.8 = f32[1,8,128]{2,1,0:T(8,128)S(1)} collective-permute-done((f32[1,8,128]{2,1,0:T(8,128)S(1)}, f32[1,8,128]{2,1,0:T(8,128)S(1)}, u32[]{:S(2)}, u32[]{:S(2)}) %collective-permute-start.8) | collective-permute-done | bytes 4128 | tf_op jit(solution)/shard_map/ppermute | solution.py:467
  32.1 1.2 %collective-permute-done.9 = f32[1,8,128]{2,1,0:T(8,128)S(1)} collective-permute-done((f32[1,8,128]{2,1,0:T(8,128)S(1)}, f32[1,8,128]{2,1,0:T(8,128)S(1)}, u32[]{:S(2)}, u32[]{:S(2)}) %collective-permute-start.9) | collective-permute-done | bytes 4128 | tf_op jit(solution)/shard_map/ppermute | solution.py:467
  33.3 2.7 %collective-permute-start.10 = (f32[1,8,128]{2,1,0:T(8,128)S(1)}, f32[1,8,128]{2,1,0:T(8,128)S(1)}, u32[]{:S(2)}, u32[]{:S(2)}) collective-permute-start(f32[1,8,128]{2,1,0:T(8,128)S(1)} %add.44), channel_id=1, source_target_pairs={{0,8},{1,9},{2,10},{3,11},{4,12},{5,13},{6,14},{7,15},{8,0},{9,1},... | collective-permute-start | bytes 12296 | tf_op jit(solution)/shard_map/ppermute | solution.py:467
  36.0 1.8 %collective-permute-done.10 = f32[1,8,128]{2,1,0:T(8,128)S(1)} collective-permute-done((f32[1,8,128]{2,1,0:T(8,128)S(1)}, f32[1,8,128]{2,1,0:T(8,128)S(1)}, u32[]{:S(2)}, u32[]{:S(2)}) %collective-permute-start.10) | collective-permute-done | bytes 4128 | tf_op jit(solution)/shard_map/ppermute | solution.py:467
  37.9 1.3 %collective-permute-start.11 = (f32[29,8,128]{2,1,0:T(8,128)S(1)}, f32[29,8,128]{2,1,0:T(8,128)S(1)}, u32[]{:S(2)}, u32[]{:S(2)}) collective-permute-start(f32[29,8,128]{2,1,0:T(8,128)S(1)} %pad_maximum_fusion), channel_id=1, source_target_pairs={{0,16},{16,0},{1,17},{17,1},{2,18},{18,2},{3,19},{19,3},{4,20},{20... | collective-permute-start | bytes 356360 | tf_op jit(solution)/shard_map/ppermute | solution.py:501
  39.1 1.8 %collective-permute-start.13 = (f32[1,8,128]{2,1,0:T(8,128)S(1)}, f32[1,8,128]{2,1,0:T(8,128)S(1)}, u32[]{:S(2)}, u32[]{:S(2)}) collective-permute-start(f32[1,8,128]{2,1,0:T(8,128)S(1)} %add.45.refs_2_), channel_id=1, source_target_pairs={{0,18},{1,19},{2,16},{3,17},{4,22},{5,23},{6,20},{7,21},{8,26},{9,... | collective-permute-start | bytes 12296 | tf_op jit(solution)/shard_map/ppermute | solution.py:534
  41.4 2.4 %collective-permute-done.13.refs_4_ = f32[1,8,128]{2,1,0:T(8,128)S(1)} collective-permute-done((f32[1,8,128]{2,1,0:T(8,128)S(1)}, f32[1,8,128]{2,1,0:T(8,128)S(1)}, u32[]{:S(2)}, u32[]{:S(2)}) %collective-permute-start.13) | collective-permute-done | bytes 4128 | tf_op jit(solution)/shard_map/ppermute | solution.py:534
  43.8 0.8 %collective-permute-done.12.refs_3_ = f32[1,8,128]{2,1,0:T(8,128)S(1)} collective-permute-done((f32[1,8,128]{2,1,0:T(8,128)S(1)}, f32[1,8,128]{2,1,0:T(8,128)S(1)}, u32[]{:S(2)}, u32[]{:S(2)}) %collective-permute-start.12) | collective-permute-done | bytes 4128 | tf_op jit(solution)/shard_map/ppermute | solution.py:467
  44.5 0.7 %update.1 = (f32[2,32,896]{2,1,0:T(8,128)}, f32[1,1]{1,0:T(1,128)}) custom-call(f32[2,32,896]{2,1,0:T(8,128)S(1)} %bitcast.7, f32[2,2,8,128]{3,2,1,0:T(8,128)S(1)} %copy-done.3, f32[28,8,128]{2,1,0:T(8,128)S(1)} %fusion.refs_0_, f32[29,8,128]{2,1,0:T(8,128)S(1)} %collective-permute-done.11.refs_1_, f32[1,8,128]{2,1,0:T(8,128)S(1)} %add.45.refs_2_, ...), custom_call_target="tpu_custom_call" | custom-call | tf_op jit(solution)/shard_map/update/pallas_call | solution.py:182
  (34 shorter events, 2.1 us)
Async XLA Ops:
  2.3 6.4 %collective-permute-start = (f32[28,8,128]{2,1,0:T(8,128)}, f32[28,8,128]{2,1,0:T(8,128)S(1)}, u32[]{:S(2)}, u32[]{:S(2)}) collective-permute-start(f32[28,8,128]{2,1,0:T(8,128)} %get-tuple-element.22), channel_id=1, source_target_pairs={{0,16},{16,0},{1,17},{17,1},{2,18},{18,2},{3,19},{19,3},{4,20},{20... | collective-permute-start | bytes 344072 | tf_op jit(solution)/shard_map/ppermute | solution.py:501
  5.3 0.9 %copy-start = (f32[1,2,32,896]{3,2,1,0:T(8,128)S(1)}, f32[1,2,32,896]{3,2,1,0:T(8,128)}, u32[]{:S(2)}) copy-start(f32[1,2,32,896]{3,2,1,0:T(8,128)} %param.7) | copy-start | bytes 688132
  6.3 1.0 %copy-start.2 = (bf16[4,256,256]{2,1,0:T(8,128)(2,1)S(1)}, bf16[4,256,256]{2,1,0:T(8,128)(2,1)}, u32[]{:S(2)}) copy-start(bf16[4,256,256]{2,1,0:T(8,128)(2,1)} %constant.36.clone.tables) | copy-start | bytes 1572868
  7.3 0.7 %copy-start.4 = (f32[2,2,2]{2,1,0:T(2,128)S(1)}, f32[2,2,2]{2,1,0:T(2,128)}, u32[]{:S(2)}) copy-start(f32[2,2,2]{2,1,0:T(2,128)} %paths.1) | copy-start | bytes 100
  8.0 11.1 %copy-start.5 = (bf16[1,1,14,128,128]{4,3,2,1,0:T(8,128)(2,1)S(1)}, bf16[1,1,14,128,128]{4,3,2,1,0:T(8,128)(2,1)}, u32[]{:S(2)}) copy-start(bf16[1,1,14,128,128]{4,3,2,1,0:T(8,128)(2,1)} %param.10) | copy-start | bytes 1376260
  8.7 3.4 %collective-permute-start.3 = (f32[28,8,128]{2,1,0:T(8,128)S(1)}, f32[28,8,128]{2,1,0:T(8,128)S(1)}, u32[]{:S(2)}, u32[]{:S(2)}) collective-permute-start(f32[28,8,128]{2,1,0:T(8,128)S(1)} %add.35.own), channel_id=1, source_target_pairs={{0,1},{1,0},{2,4},{3,5},{4,2},{5,3},{6,8},{7,9},{8,6},{9,7},{10,12... | collective-permute-start | bytes 344072 | tf_op jit(solution)/shard_map/ppermute | solution.py:467
  8.8 6.9 %collective-permute-start.2 = (f32[28,8,128]{2,1,0:T(8,128)S(1)}, f32[28,8,128]{2,1,0:T(8,128)S(1)}, u32[]{:S(2)}, u32[]{:S(2)}) collective-permute-start(f32[28,8,128]{2,1,0:T(8,128)S(1)} %add.35.own), channel_id=1, source_target_pairs={{0,2},{1,3},{2,0},{3,1},{4,6},{5,7},{6,4},{7,5},{8,10},{9,11},{10,... | collective-permute-start | bytes 344072 | tf_op jit(solution)/shard_map/ppermute | solution.py:467
  12.1 6.5 %collective-permute-start.1 = (f32[28,8,128]{2,1,0:T(8,128)S(1)}, f32[28,8,128]{2,1,0:T(8,128)S(1)}, u32[]{:S(2)}, u32[]{:S(2)}) collective-permute-start(f32[28,8,128]{2,1,0:T(8,128)S(1)} %add.35.own), channel_id=1, source_target_pairs={{0,1},{1,0},{2,3},{3,2},{4,5},{5,4},{6,7},{7,6},{8,9},{9,8},{10,11... | collective-permute-start | bytes 344072 | tf_op jit(solution)/shard_map/ppermute | solution.py:467
  15.7 3.3 %collective-permute-start.4 = (f32[28,8,128]{2,1,0:T(8,128)S(1)}, f32[28,8,128]{2,1,0:T(8,128)S(1)}, u32[]{:S(2)}, u32[]{:S(2)}) collective-permute-start(f32[28,8,128]{2,1,0:T(8,128)S(1)} %broadcast_select_fusion), channel_id=1, source_target_pairs={{0,1},{1,0},{2,3},{3,2},{4,5},{5,4},{6,7},{7,6},{8,9},{9,8},{10,11... | collective-permute-start | bytes 344072 | tf_op jit(solution)/shard_map/ppermute | solution.py:467
  15.8 0.9 %copy-start.6 = (f32[2,128,128]{2,1,0:T(8,128)S(1)}, f32[2,128,128]{2,1,0:T(8,128)}, u32[]{:S(2)}) copy-start(f32[2,128,128]{2,1,0:T(8,128)} %probe.1) | copy-start | bytes 393220
  16.7 0.7 %copy-start.7 = (s32[3,14]{1,0:T(4,128)S(1)}, s32[3,14]{1,0:T(4,128)}, u32[]{:S(2)}) copy-start(s32[3,14]{1,0:T(4,128)} %get-tuple-element.19.scalars) | copy-start | bytes 508
  19.1 25.4 %copy-start.1 = (f32[1,2,32,896]{3,2,1,0:T(8,128)S(1)}, f32[1,2,32,896]{3,2,1,0:T(8,128)}, u32[]{:S(2)}) copy-start(f32[1,2,32,896]{3,2,1,0:T(8,128)} %param.7) | copy-start | bytes 688132
  19.1 25.4 %copy-start.3 = (f32[2,2,8,128]{3,2,1,0:T(8,128)S(1)}, f32[2,2,8,128]{3,2,1,0:T(8,128)}, u32[]{:S(2)}) copy-start(f32[2,2,8,128]{3,2,1,0:T(8,128)} %get-tuple-element.18.factors) | copy-start | bytes 49156
  22.7 1.7 %collective-permute-start.5 = (f32[56,8,128]{2,1,0:T(8,128)S(1)}, f32[56,8,128]{2,1,0:T(8,128)S(1)}, u32[]{:S(2)}, u32[]{:S(2)}) collective-permute-start(f32[56,8,128]{2,1,0:T(8,128)S(1)} %get-tuple-element.28), channel_id=1, source_target_pairs={{0,1},{1,0},{2,3},{3,2},{4,5},{5,4},{6,7},{7,6},{8,9},{9,8},{10,11... | collective-permute-start | bytes 688136 | tf_op jit(solution)/shard_map/ppermute | solution.py:467
  24.5 13.3 %collective-permute-start.7 = (f32[28,8,128]{2,1,0:T(8,128)S(1)}, f32[28,8,128]{2,1,0:T(8,128)S(1)}, u32[]{:S(2)}, u32[]{:S(2)}) collective-permute-start(f32[28,8,128]{2,1,0:T(8,128)S(1)} %get-tuple-element.34), channel_id=1, source_target_pairs={{0,2},{1,3},{2,0},{3,1},{4,6},{5,7},{6,4},{7,5},{8,10},{9,11},{10,... | collective-permute-start | bytes 344072 | tf_op jit(solution)/shard_map/ppermute | solution.py:467
  27.0 10.8 %collective-permute-start.6 = (f32[28,8,128]{2,1,0:T(8,128)S(1)}, f32[28,8,128]{2,1,0:T(8,128)S(1)}, u32[]{:S(2)}, u32[]{:S(2)}) collective-permute-start(f32[28,8,128]{2,1,0:T(8,128)S(1)} %get-tuple-element.35), channel_id=1, source_target_pairs={{0,1},{1,0},{2,4},{3,5},{4,2},{5,3},{6,8},{7,9},{8,6},{9,7},{10,12... | collective-permute-start | bytes 344072 | tf_op jit(solution)/shard_map/ppermute | solution.py:467
  27.1 5.0 %collective-permute-start.8 = (f32[1,8,128]{2,1,0:T(8,128)S(1)}, f32[1,8,128]{2,1,0:T(8,128)S(1)}, u32[]{:S(2)}, u32[]{:S(2)}) collective-permute-start(f32[1,8,128]{2,1,0:T(8,128)S(1)} %get-tuple-element.31), channel_id=1, source_target_pairs={{0,4},{1,5},{2,6},{3,7},{4,0},{5,1},{6,2},{7,3},{8,12},{9,13},{10,... | collective-permute-start | bytes 12296 | tf_op jit(solution)/shard_map/ppermute | solution.py:467
  32.1 1.2 %collective-permute-start.9 = (f32[1,8,128]{2,1,0:T(8,128)S(1)}, f32[1,8,128]{2,1,0:T(8,128)S(1)}, u32[]{:S(2)}, u32[]{:S(2)}) collective-permute-start(f32[1,8,128]{2,1,0:T(8,128)S(1)} %add.43), channel_id=1, source_target_pairs={{0,1},{1,0},{2,3},{3,2},{4,5},{5,4},{6,7},{7,6},{8,9},{9,8},{10,11... | collective-permute-start | bytes 12296 | tf_op jit(solution)/shard_map/ppermute | solution.py:467
  33.3 4.5 %collective-permute-start.10 = (f32[1,8,128]{2,1,0:T(8,128)S(1)}, f32[1,8,128]{2,1,0:T(8,128)S(1)}, u32[]{:S(2)}, u32[]{:S(2)}) collective-permute-start(f32[1,8,128]{2,1,0:T(8,128)S(1)} %add.44), channel_id=1, source_target_pairs={{0,8},{1,9},{2,10},{3,11},{4,12},{5,13},{6,14},{7,15},{8,0},{9,1},... | collective-permute-start | bytes 12296 | tf_op jit(solution)/shard_map/ppermute | solution.py:467
  37.9 6.7 %collective-permute-start.11 = (f32[29,8,128]{2,1,0:T(8,128)S(1)}, f32[29,8,128]{2,1,0:T(8,128)S(1)}, u32[]{:S(2)}, u32[]{:S(2)}) collective-permute-start(f32[29,8,128]{2,1,0:T(8,128)S(1)} %pad_maximum_fusion), channel_id=1, source_target_pairs={{0,16},{16,0},{1,17},{17,1},{2,18},{18,2},{3,19},{19,3},{4,20},{20... | collective-permute-start | bytes 356360 | tf_op jit(solution)/shard_map/ppermute | solution.py:501
  39.1 4.6 %collective-permute-start.13 = (f32[1,8,128]{2,1,0:T(8,128)S(1)}, f32[1,8,128]{2,1,0:T(8,128)S(1)}, u32[]{:S(2)}, u32[]{:S(2)}) collective-permute-start(f32[1,8,128]{2,1,0:T(8,128)S(1)} %add.45.refs_2_), channel_id=1, source_target_pairs={{0,18},{1,19},{2,16},{3,17},{4,22},{5,23},{6,20},{7,21},{8,26},{9,... | collective-permute-start | bytes 12296 | tf_op jit(solution)/shard_map/ppermute | solution.py:534
  40.9 3.6 %collective-permute-start.12 = (f32[1,8,128]{2,1,0:T(8,128)S(1)}, f32[1,8,128]{2,1,0:T(8,128)S(1)}, u32[]{:S(2)}, u32[]{:S(2)}) collective-permute-start(f32[1,8,128]{2,1,0:T(8,128)S(1)} %add.45.refs_2_), channel_id=1, source_target_pairs={{0,2},{1,3},{2,0},{3,1},{4,6},{5,7},{6,4},{7,5},{8,10},{9,11},{10,... | collective-permute-start | bytes 12296 | tf_op jit(solution)/shard_map/ppermute | solution.py:467

commit v6 on v5

--- a/solution.py
+++ b/solution.py
@@ -15,6 +15,7 @@
 FLOOR_RATIO = 4.0
 LANES = 128
 TALL = 4
+SIDE = 14
 BROAD = 2
 SUBS = 8
 HALF_PI = (1.5703125, 4.837512969970703125e-4, 7.54978995489188216e-8)
@@ -233,43 +234,120 @@
     return frames[frames.shape[0] - len(FLAGS) + FLAGS.index(name)] == 1
 
 
-def phases_kernel(frames, own, mate, pair, next_pair, real, imag):
+def frame_masks(frames, number, p):
+    lane = lax.broadcasted_iota(jnp.int32, (SUBS, LANES), 1)
+    sub = lax.broadcasted_iota(jnp.int32, (SUBS, LANES), 0)
+    near = ROWS_DEV // 4 + JIT
+    return lane >= frames[p], [sub + k * SUBS >= frames[number + p] for k in range(near // SUBS)]
+
+
+def object_at(ref, first_block, row_block, p, patch, tiles, after):
+    tile, _ = window_place(p, patch)
+    first = first_block + row_block * tiles + tile
+    left = ref[first] if tile >= 0 else 0.0
+    right = ref[first + 1] if tile + 1 < tiles else 0.0
+    return jnp.where(after, left, right)
+
+
+def put_wave(wave, rolled, row, source, real, imag):
+    a, b = rolled[pl.ds(source, SUBS), :LANES], rolled[pl.ds(source, SUBS), LANES:]
+    wave[row : row + SUBS, :LANES] = a * real - b * imag
+    wave[row : row + SUBS, LANES:] = a * imag + b * real
+
+
+def against(high, low, t_high, t_low):
+    left = jnp.concatenate([high, low, high], 1)
+    return lax.dot(left, jnp.concatenate([t_high, t_high, t_low], 0), preferred_element_type=jnp.float32)
+
+
+def onto(t_high, t_low, high, low):
+    right = jnp.concatenate([high, low, high], 0)
+    return lax.dot(jnp.concatenate([t_high, t_high, t_low], 1), right, preferred_element_type=jnp.float32)
+
+
+def side_rows():
+    second = lax.rem(lax.axis_index("wide"), 2)
+    upper, lower = ROWS_DEV, 3 * ROWS_DEV
+    return jnp.where(second == 1, upper, lower), jnp.where(second == 1, lower, upper)
+
+
+def ahead_kernel(frames, own, mate, pair, next_pair, rolled, tables, wave, mid, real, imag):
     blocks = own.shape[0]
+    patch = rolled.shape[1] // 2
+    number = rolled.shape[0] // patch
+    tiles = blocks * SUBS // ROWS_DEV
+    steps = ROWS_DEV // SUBS
     lower = flag_of(frames, "lower")
     up2_ok = jnp.where(flag_of(frames, "up2"), 1.0, 0.0)
     dn2_ok = jnp.where(flag_of(frames, "dn2"), 1.0, 0.0)
-    unused = ROWS_DEV // 4 // SUBS * (blocks * SUBS // ROWS_DEV)
+    unused = ROWS_DEV // 4 // SUBS * tiles
     for i in range(blocks):
-        s, c = sin_cos(own[i])
-        real[2 * blocks + i], imag[2 * blocks + i] = c, s
-        s, c = sin_cos(mate[i])
-        real[blocks + i], imag[blocks + i] = c, s
         if i >= unused:
             s, c = sin_cos(jnp.where(lower, pair[i], next_pair[i]))
             real[i], imag[i] = c * up2_ok, s * up2_ok
         if i < blocks - unused:
             s, c = sin_cos(jnp.where(lower, next_pair[i], pair[i]))
-            real[4 * blocks + i], imag[4 * blocks + i] = c * dn2_ok, s * dn2_ok
-
-
-def phases(frames, own, mate, pair, next_pair):
+            real[blocks + i], imag[blocks + i] = c * dn2_ok, s * dn2_ok
+        s, c = sin_cos(own[i])
+        real[2 * blocks + i], imag[2 * blocks + i] = c, s
+        s, c = sin_cos(mate[i])
+        real[3 * blocks + i], imag[3 * blocks + i] = c, s
+
+    mate_row, _ = side_rows()
+    near = ROWS_DEV // 4 + JIT
+    t_high, t_low = tables[0], tables[1]
+    for p in range(number):
+        after, below = frame_masks(frames, number, p)
+        place = (p, patch, tiles, after)
+        for k in range(steps):
+            row = k * SUBS
+            parts = []
+            for ref in (real, imag):
+                if row + SUBS <= ROWS_DEV // 4:
+                    parts.append(object_at(ref, blocks, k, *place))
+                elif row < near:
+                    up = object_at(ref, 0, k, *place)
+                    parts.append(jnp.where(below[k], up, object_at(ref, blocks, k, *place)))
+                else:
+                    parts.append(object_at(ref, 0, k, *place))
+            put_wave(wave, rolled, p * patch + row, p * patch + row, *parts)
+            parts = [object_at(ref, 2 * blocks, k, *place) for ref in (real, imag)]
+            row += p * patch + 2 * ROWS_DEV
+            put_wave(wave, rolled, row, row, *parts)
+            row = k * SUBS
+            parts = [object_at(ref, 3 * blocks, k, *place) for ref in (real, imag)]
+            source = pl.multiple_of(p * patch + mate_row + row, SUBS)
+            put_wave(wave, rolled, p * patch + ROWS_DEV + row, source, *parts)
+
+    here = 3 * ROWS_DEV
+    for p in range(0, number, TALL):
+        windows = range(p, min(p + TALL, number))
+        value = jnp.concatenate([wave[q * patch : q * patch + here, :] for q in windows], 0)
+        out = against(*parts_of(value), t_high, t_low)
+        for i, q in enumerate(windows):
+            mid[q * patch : q * patch + here, :] = out[i * here : (i + 1) * here]
+
+
+def ahead(frames, own, mate, pair, next_pair, rolled, tables):
     vmem = pl.BlockSpec(memory_space=pltpu.VMEM)
-    out = jax.ShapeDtypeStruct((5 * own.shape[0], SUBS, LANES), jnp.float32)
+    out = jax.ShapeDtypeStruct(rolled.shape, jnp.float32)
+    scratch = pltpu.VMEM((4 * own.shape[0], SUBS, LANES), jnp.float32)
     return pl.pallas_call(
-        phases_kernel,
+        ahead_kernel,
         out_shape=(out, out),
-        in_specs=[vmem] * 5,
+        in_specs=[vmem] * 7,
         out_specs=(vmem, vmem),
-        compiler_params=pltpu.CompilerParams(vmem_limit_bytes=8 * 1024 * 1024),
+        scratch_shapes=[scratch, scratch],
+        compiler_params=pltpu.CompilerParams(vmem_limit_bytes=24 * 1024 * 1024),
         cost_estimate=pl.CostEstimate(flops=2**27, bytes_accessed=2**22, transcendentals=0),
-        name="phases",
-    )(frames, own, mate, pair, next_pair)
+        name="ahead",
+    )(frames, own, mate, pair, next_pair, rolled, tables)
 
 
 def strip_kernel(
     frames,
-    here_real,
-    here_imag,
+    wave,
+    mid,
     relay,
     rolled,
     measured,
@@ -279,18 +357,19 @@
     by_pair,
     by_next,
     misfit,
-    side_real,
-    side_imag,
-    wave,
-    mid,
+    real,
+    imag,
+    side_wave,
+    side_mid,
     back,
+    terms,
 ):
     number, patch, _ = measured.shape
     rows = ROWS_DEV
     blocks = relay.shape[0]
     tiles = blocks * SUBS // rows
+    steps = patch // SUBS
     near = ROWS_DEV // 4 + JIT
-    dot = functools.partial(lax.dot, preferred_element_type=jnp.float32)
     is_second = flag_of(frames, "second")
     is_lower = flag_of(frames, "lower")
     fwd_high, fwd_low, inv_high, inv_low = (tables[i] for i in range(4))
@@ -298,64 +377,24 @@
     relay_ok = jnp.where(flag_of(frames, "relay"), 1.0, 0.0)
     for i in range(blocks):
         s, c = sin_cos(relay[i])
-        c, s = c * relay_ok, s * relay_ok
-        mate_c, mate_s = here_real[blocks + i], here_imag[blocks + i]
-        side_real[i] = jnp.where(is_second, mate_c, c)
-        side_imag[i] = jnp.where(is_second, mate_s, s)
-        side_real[blocks + i] = jnp.where(is_second, c, mate_c)
-        side_imag[blocks + i] = jnp.where(is_second, s, mate_s)
-    obj_real = (here_real, side_real)
-    obj_imag = (here_imag, side_imag)
-
-    lane = lax.broadcasted_iota(jnp.int32, (SUBS, LANES), 1)
-    sub = lax.broadcasted_iota(jnp.int32, (SUBS, LANES), 0)
-
-    def masks(p):
-        after = lane >= frames[p]
-        below = [sub + k * SUBS >= frames[number + p] for k in range(near // SUBS)]
-        return after, below
-
-    def pick(refs, p, k, after, below):
-        tile, _ = window_place(p, patch)
-
-        def at(row):
-            slot, ref = row // rows, refs[0]
-            first = row // SUBS * tiles + tile
-            if slot in (1, 3):
-                ref, first = refs[1], first - (slot + 1) // 2 * blocks
-            left = ref[first] if tile >= 0 else 0.0
-            right = ref[first + 1] if tile + 1 < tiles else 0.0
-            return jnp.where(after, left, right)
-
-        row = k * SUBS
-        if row + SUBS <= ROWS_DEV // 4:
-            return at(row + patch)
-        if row < near:
-            return jnp.where(below[k], at(row), at(row + patch))
-        return at(row)
-
-    def against(high, low, t_high, t_low):
-        return dot(jnp.concatenate([high, low, high], 1), jnp.concatenate([t_high, t_high, t_low], 0))
-
-    def onto(t_high, t_low, high, low):
-        return dot(jnp.concatenate([t_high, t_high, t_low], 1), jnp.concatenate([high, low, high], 0))
-
-    steps = patch // SUBS
+        real[i], imag[i] = c * relay_ok, s * relay_ok
+    _, relay_row = side_rows()
     for p in range(number):
-        after, below = masks(p)
-        for k in range(steps):
-            o_real = pick(obj_real, p, k, after, below)
-            o_imag = pick(obj_imag, p, k, after, below)
-            row = p * patch + k * SUBS
-            a = rolled[row : row + SUBS, :LANES]
-            b = rolled[row : row + SUBS, LANES:]
-            wave[row : row + SUBS, :LANES] = a * o_real - b * o_imag
-            wave[row : row + SUBS, LANES:] = a * o_imag + b * o_real
-
-    for p in range(0, number, TALL):
-        span = slice(p * patch, min(p + TALL, number) * patch)
-        high, low = parts_of(wave[span, :])
-        mid[span, :] = against(high, low, fwd_high, fwd_low)
+        after, _ = frame_masks(frames, number, p)
+        for k in range(rows // SUBS):
+            parts = [object_at(ref, 0, k, p, patch, tiles, after) for ref in (real, imag)]
+            source = pl.multiple_of(p * patch + relay_row + k * SUBS, SUBS)
+            put_wave(side_wave, rolled, p * rows + k * SUBS, source, *parts)
+    for p in range(0, number, SIDE):
+        span = slice(p * rows, min(p + SIDE, number) * rows)
+        side_mid[span, :] = against(*parts_of(side_wave[span, :]), fwd_high, fwd_low)
+    second = relay_row > 2 * rows
+
+    def window_rows(whole, side, p):
+        at = p * patch
+        mates, others = whole[at + rows : at + 2 * rows, :], side[p * rows : (p + 1) * rows, :]
+        upper, lower = jnp.where(second, mates, others), jnp.where(second, others, mates)
+        return jnp.concatenate([whole[at : at + rows, :], upper, whole[at + 2 * rows : at + 3 * rows, :], lower], 0)
 
     def upright(value):
         count = value.shape[0] // patch
@@ -368,7 +407,7 @@
     total = jnp.zeros((SUBS, LANES), jnp.float32)
     for p in range(0, number, BROAD):
         count = min(BROAD, number - p)
-        high, low = parts_of(upright(mid[p * patch : (p + count) * patch, :]))
+        high, low = parts_of(upright(jnp.concatenate([window_rows(mid, side_mid, p + i) for i in range(count)], 0)))
         spectrum = onto(inv_high, inv_low, high, low)
         real, imag = spectrum[:patch], spectrum[patch:]
         target = jnp.concatenate([measured[p + i] for i in range(count)], 1).astype(jnp.float32)
@@ -393,8 +432,9 @@
         span = slice(p * patch, min(p + TALL, number) * patch)
         high, low = parts_of(back[span, :])
         out = against(high, low, inv_high, inv_low)
-        w = wave[span, :]
-        mid[span, :LANES] = w[:, :LANES] * out[:, LANES:] - w[:, LANES:] * out[:, :LANES]
+        windows = range(p, min(p + TALL, number))
+        w = jnp.concatenate([window_rows(wave, side_wave, q) for q in windows], 0)
+        terms[span, :] = w[:, :LANES] * out[:, LANES:] - w[:, LANES:] * out[:, :LANES]
 
     grads = {}
     for t in range(tiles):
@@ -402,13 +442,13 @@
         for p in range(number):
             tile, _ = window_place(p, patch)
             if t in (tile, tile + 1):
-                after, below = masks(p)
+                after, below = frame_masks(frames, number, p)
                 meets.append((p, after if t == tile else jnp.logical_not(after), below))
         for k in range(steps):
             row = k * SUBS
             here = there = None
             for p, mask, below in meets:
-                term = jnp.where(mask, mid[p * patch + row : p * patch + row + SUBS, :LANES], 0.0)
+                term = jnp.where(mask, terms[p * patch + row : p * patch + row + SUBS, :], 0.0)
                 if row + SUBS <= ROWS_DEV // 4:
                     there = term if there is None else there + term
                 elif row < near:
@@ -433,7 +473,7 @@
         by_next[i] = jnp.where(is_lower, dn2, up2)
 
 
-def strip_gradient(frames, here, relay, rolled, measured, tables):
+def strip_gradient(frames, wave, mid, relay, rolled, measured, tables):
     number, patch, _ = measured.shape
     blocks = relay.shape[0]
     vmem = pl.BlockSpec(memory_space=pltpu.VMEM)
@@ -441,24 +481,26 @@
     def block_list(count):
         return jax.ShapeDtypeStruct((count, SUBS, LANES), jnp.float32)
 
+    side = pltpu.VMEM((number * ROWS_DEV, 2 * LANES), jnp.float32)
     return pl.pallas_call(
         strip_kernel,
         out_shape=tuple(block_list(n) for n in (blocks, 2 * blocks, blocks, blocks, 1)),
         in_specs=[vmem] * 7,
         out_specs=(vmem,) * 5,
         scratch_shapes=[
-            pltpu.VMEM((2 * blocks, SUBS, LANES), jnp.float32),
-            pltpu.VMEM((2 * blocks, SUBS, LANES), jnp.float32),
+            pltpu.VMEM((blocks, SUBS, LANES), jnp.float32),
+            pltpu.VMEM((blocks, SUBS, LANES), jnp.float32),
+            side,
+            side,
             pltpu.VMEM((number * patch, 2 * LANES), jnp.float32),
-            pltpu.VMEM((number * patch, 2 * LANES), jnp.float32),
-            pltpu.VMEM((number * patch, 2 * LANES), jnp.float32),
+            pltpu.VMEM((number * patch, LANES), jnp.float32),
         ],
         compiler_params=pltpu.CompilerParams(vmem_limit_bytes=40 * 1024 * 1024),
         cost_estimate=pl.CostEstimate(
             flops=24 * number * patch**3 * 4, bytes_accessed=4 * number * patch * patch, transcendentals=0
         ),
         name="strip",
-    )(frames, *here, relay, rolled, measured, tables)
+    )(frames, wave, mid, relay, rolled, measured, tables)
 
 
 def permuted(value, axis, target):
@@ -511,9 +553,9 @@
     mate = with_mate(own)
     rolled, frames = prepared(scalars, probe)
     relay = with_mate(jnp.where(even, pair, next_pair))
-    here = phases(frames, own, mate, pair, next_pair)
+    wave, mid = ahead(frames, own, mate, pair, next_pair, rolled, tables)
     blocks = own.shape[0]
-    mine, to_mate, by_pair, by_next, local = strip_gradient(frames, here, relay, rolled, measured[0, 0], tables)
+    mine, to_mate, by_pair, by_next, local = strip_gradient(frames, wave, mid, relay, rolled, measured[0, 0], tables)
     got = with_mate(to_mate)
     if groups != 2:
         local = joined(local, "blk", [2**k for k in range(groups.bit_length() - 1)])

time: 45.6 us -> 45.8 us (level)
    pallas_call x1, Pallas kernels: 0.56 us -> 1.22 us  [ahead(): pl.pallas_call(ahead_kernel, out_shape=(out, out), in_specs=[vmem] * 7, o...]
  transfers between devices with their start and end apart: 14 -> 14, of which waited for: 8 -> 8; matrix products, arithmetic and copies ran while one was open for 0% -> 0% of each run, Pallas kernels for 5% -> 7%
where the time goes in v6:
time: 45.8 us; the launch traced here: 45.5 us
  starting transfers between devices  17.4 us (38%)
  waiting for transfers between devices  14.5 us (32%)
  Pallas kernels  8.58 us (19%)
  local copies, waits for them, and re-layouts  4.24 us (9%)
  between operations  0.77 us (2%)
    ppermute x11, waiting for transfers between devices, permuted(): return lax.ppermute(value, axis, pairs)  12 us
    ppermute x11, starting transfers between devices, permuted(): return lax.ppermute(value, axis, pairs)  11.3 us
    ppermute x2, starting transfers between devices, to_group(): lax.ppermute(value, 'blk', [(i, (i + step) % groups) for i in range(group...  4.32 us
    unnamed x16, local copies, waits for them, and re-layouts  4.24 us
    pallas_call x1, Pallas kernels, strip_gradient(): pl.pallas_call(strip_kernel, out_shape=tuple((block_list(n) for n in (blo...  3.21 us
    ppermute x1, waiting for transfers between devices, program(): sums.append(lax.ppermute(local, ('blk', 'wide'), pairs))  2.36 us
    ppermute x1, starting transfers between devices, program(): sums.append(lax.ppermute(local, ('blk', 'wide'), pairs))  1.78 us
    pallas_call x1, Pallas kernels, slab_terms(): pl.pallas_call(functools.partial(terms_kernel, groups), out_shape=[listed...  1.67 us
  transfers between devices with their start and end apart: 14, of which 8 were waited for; matrix products, arithmetic and copies ran while one was open for 0% of the time, Pallas kernels for 7%

profile of v6, /device:TPU:0, one launch (start us, length us, event | category | flops | bytes accessed | tf_op | source)
XLA Modules:
  0.0 45.5 jit_solution(3494545745552779212)
XLA Ops:
  0.6 1.7 %terms.1 = (f32[28,8,128]{2,1,0:T(8,128)}, f32[2,2,8,128]{3,2,1,0:T(8,128)}, s32[3,14]{1,0:T(4,128)}) custom-call(f32[2,32,896]{2,1,0:T(8,128)} %bitcast.5, f32[2,2,2]{2,1,0:T(2,128)} %paths.1, s32[2,14]{1,0:T(2,128)} %bitcast.9, f32[2]{0:T(128)} %steps_hbm.1), custom_call_target="tpu_custom_call" | custom-call | tf_op jit(solution)/shard_map/terms/pallas_call | solution.py:122
  2.3 3.0 %collective-permute-start = (f32[28,8,128]{2,1,0:T(8,128)}, f32[28,8,128]{2,1,0:T(8,128)S(1)}, u32[]{:S(2)}, u32[]{:S(2)}) collective-permute-start(f32[28,8,128]{2,1,0:T(8,128)} %get-tuple-element.22), channel_id=1, source_target_pairs={{0,16},{16,0},{1,17},{17,1},{2,18},{18,2},{3,19},{19,3},{4,20},{20... | collective-permute-start | bytes 344072 | tf_op jit(solution)/shard_map/ppermute | solution.py:543
  5.3 0.9 %copy-done = f32[1,2,32,896]{3,2,1,0:T(8,128)S(1)} copy-done((f32[1,2,32,896]{3,2,1,0:T(8,128)S(1)}, f32[1,2,32,896]{3,2,1,0:T(8,128)}, u32[]{:S(2)}) %copy-start) | copy-done | bytes 229400
  6.3 1.0 %copy-done.2 = bf16[4,256,256]{2,1,0:T(8,128)(2,1)S(1)} copy-done((bf16[4,256,256]{2,1,0:T(8,128)(2,1)S(1)}, bf16[4,256,256]{2,1,0:T(8,128)(2,1)}, u32[]{:S(2)}) %copy-start.2) | copy-done | bytes 524312
  7.3 0.7 %copy-done.4 = f32[2,2,2]{2,1,0:T(2,128)S(1)} copy-done((f32[2,2,2]{2,1,0:T(2,128)S(1)}, f32[2,2,2]{2,1,0:T(2,128)}, u32[]{:S(2)}) %copy-start.4) | copy-done | bytes 56
  8.8 3.3 %collective-permute-start.2 = (f32[28,8,128]{2,1,0:T(8,128)S(1)}, f32[28,8,128]{2,1,0:T(8,128)S(1)}, u32[]{:S(2)}, u32[]{:S(2)}) collective-permute-start(f32[28,8,128]{2,1,0:T(8,128)S(1)} %add.35.own), channel_id=1, source_target_pairs={{0,2},{1,3},{2,0},{3,1},{4,6},{5,7},{6,4},{7,5},{8,10},{9,11},{10,... | collective-permute-start | bytes 344072 | tf_op jit(solution)/shard_map/ppermute | solution.py:509
  12.1 3.6 %collective-permute-done.2.pair = f32[28,8,128]{2,1,0:T(8,128)S(1)} collective-permute-done((f32[28,8,128]{2,1,0:T(8,128)S(1)}, f32[28,8,128]{2,1,0:T(8,128)S(1)}, u32[]{:S(2)}, u32[]{:S(2)}) %collective-permute-start.2) | collective-permute-done | bytes 114720 | tf_op jit(solution)/shard_map/ppermute | solution.py:509
  15.8 0.9 %copy-done.6 = f32[2,128,128]{2,1,0:T(8,128)S(1)} copy-done((f32[2,128,128]{2,1,0:T(8,128)S(1)}, f32[2,128,128]{2,1,0:T(8,128)}, u32[]{:S(2)}) %copy-start.6) | copy-done | bytes 131096
  16.7 0.7 %copy-done.7 = s32[3,14]{1,0:T(4,128)S(1)} copy-done((s32[3,14]{1,0:T(4,128)S(1)}, s32[3,14]{1,0:T(4,128)}, u32[]{:S(2)}) %copy-start.7) | copy-done | bytes 192
  17.4 1.1 %prepare.1 = (f32[1792,256]{1,0:T(8,128)S(1)}, s32[33,8,128]{2,1,0:T(8,128)S(1)}) custom-call(s32[3,14]{1,0:T(4,128)S(1)} %copy-done.7, f32[2,128,128]{2,1,0:T(8,128)S(1)} %copy-done.6), custom_call_target="tpu_custom_call" | custom-call | flops 134217728 | bytes 4194304 | tf_op jit(solution)/shard_map/prepare/pallas_call | solution.py:218
  18.5 1.2 %ahead.1 = (f32[1792,256]{1,0:T(8,128)S(1)}, f32[1792,256]{1,0:T(8,128)S(1)}) custom-call(s32[33,8,128]{2,1,0:T(8,128)S(1)} %get-tuple-element.20.frames, f32[28,8,128]{2,1,0:T(8,128)S(1)} %add.35.own, f32[28,8,128]{2,1,0:T(8,128)S(1)} %collective-permute-done.1.mate, f32[28,8,128]{2,1,0:T(8,128)S(1)} %collective-permute-done.2.pair, ...), custom_call_target="tpu_custom_call" | custom-call | flops 134217728 | bytes 4194304 | tf_op jit(solution)/shard_map/ahead/pallas_call | solution.py:335
  19.8 3.2 %strip.1 = (f32[28,8,128]{2,1,0:T(8,128)S(1)}, f32[56,8,128]{2,1,0:T(8,128)S(1)}, f32[28,8,128]{2,1,0:T(8,128)S(1)}, f32[28,8,128]{2,1,0:T(8,128)S(1)}, f32[1,8,128]{2,1,0:T(8,128)S(1)}) custom-call(s32[33,8,128]{2,1,0:T(8,128)S(1)} %get-tuple-element.20.frames, f32[1792,256]{1,0:T(8,128)S(1)} %get-tuple-element.25.wave, ...), custom_call_target="tpu_custom_call" | custom-call | flops 2818572288 | bytes 917504 | tf_op jit(solution)/shard_map/strip/pallas_call | solution.py:485
  23.6 1.1 %collective-permute-done.5 = f32[56,8,128]{2,1,0:T(8,128)S(1)} collective-permute-done((f32[56,8,128]{2,1,0:T(8,128)S(1)}, f32[56,8,128]{2,1,0:T(8,128)S(1)}, u32[]{:S(2)}, u32[]{:S(2)}) %collective-permute-start.5) | collective-permute-done | bytes 229408 | tf_op jit(solution)/shard_map/ppermute | solution.py:509
  24.7 2.5 %collective-permute-start.7 = (f32[28,8,128]{2,1,0:T(8,128)S(1)}, f32[28,8,128]{2,1,0:T(8,128)S(1)}, u32[]{:S(2)}, u32[]{:S(2)}) collective-permute-start(f32[28,8,128]{2,1,0:T(8,128)S(1)} %get-tuple-element.34), channel_id=1, source_target_pairs={{0,2},{1,3},{2,0},{3,1},{4,6},{5,7},{6,4},{7,5},{8,10},{9,11},{10,... | collective-permute-start | bytes 344072 | tf_op jit(solution)/shard_map/ppermute | solution.py:509
  27.3 1.5 %collective-permute-start.8 = (f32[1,8,128]{2,1,0:T(8,128)S(1)}, f32[1,8,128]{2,1,0:T(8,128)S(1)}, u32[]{:S(2)}, u32[]{:S(2)}) collective-permute-start(f32[1,8,128]{2,1,0:T(8,128)S(1)} %get-tuple-element.31), channel_id=1, source_target_pairs={{0,4},{1,5},{2,6},{3,7},{4,0},{5,1},{6,2},{7,3},{8,12},{9,13},{10,... | collective-permute-start | bytes 12296 | tf_op jit(solution)/shard_map/ppermute | solution.py:509
  28.8 3.5 %collective-permute-done.8 = f32[1,8,128]{2,1,0:T(8,128)S(1)} collective-permute-done((f32[1,8,128]{2,1,0:T(8,128)S(1)}, f32[1,8,128]{2,1,0:T(8,128)S(1)}, u32[]{:S(2)}, u32[]{:S(2)}) %collective-permute-start.8) | collective-permute-done | bytes 4128 | tf_op jit(solution)/shard_map/ppermute | solution.py:509
  32.4 1.2 %collective-permute-done.9 = f32[1,8,128]{2,1,0:T(8,128)S(1)} collective-permute-done((f32[1,8,128]{2,1,0:T(8,128)S(1)}, f32[1,8,128]{2,1,0:T(8,128)S(1)}, u32[]{:S(2)}, u32[]{:S(2)}) %collective-permute-start.9) | collective-permute-done | bytes 4128 | tf_op jit(solution)/shard_map/ppermute | solution.py:509
  33.5 2.7 %collective-permute-start.10 = (f32[1,8,128]{2,1,0:T(8,128)S(1)}, f32[1,8,128]{2,1,0:T(8,128)S(1)}, u32[]{:S(2)}, u32[]{:S(2)}) collective-permute-start(f32[1,8,128]{2,1,0:T(8,128)S(1)} %add.44), channel_id=1, source_target_pairs={{0,8},{1,9},{2,10},{3,11},{4,12},{5,13},{6,14},{7,15},{8,0},{9,1},... | collective-permute-start | bytes 12296 | tf_op jit(solution)/shard_map/ppermute | solution.py:509
  36.2 1.8 %collective-permute-done.10 = f32[1,8,128]{2,1,0:T(8,128)S(1)} collective-permute-done((f32[1,8,128]{2,1,0:T(8,128)S(1)}, f32[1,8,128]{2,1,0:T(8,128)S(1)}, u32[]{:S(2)}, u32[]{:S(2)}) %collective-permute-start.10) | collective-permute-done | bytes 4128 | tf_op jit(solution)/shard_map/ppermute | solution.py:509
  38.1 1.3 %collective-permute-start.11 = (f32[29,8,128]{2,1,0:T(8,128)S(1)}, f32[29,8,128]{2,1,0:T(8,128)S(1)}, u32[]{:S(2)}, u32[]{:S(2)}) collective-permute-start(f32[29,8,128]{2,1,0:T(8,128)S(1)} %pad_maximum_fusion), channel_id=1, source_target_pairs={{0,16},{16,0},{1,17},{17,1},{2,18},{18,2},{3,19},{19,3},{4,20},{20... | collective-permute-start | bytes 356360 | tf_op jit(solution)/shard_map/ppermute | solution.py:543
  39.4 1.8 %collective-permute-start.13 = (f32[1,8,128]{2,1,0:T(8,128)S(1)}, f32[1,8,128]{2,1,0:T(8,128)S(1)}, u32[]{:S(2)}, u32[]{:S(2)}) collective-permute-start(f32[1,8,128]{2,1,0:T(8,128)S(1)} %add.45.refs_2_), channel_id=1, source_target_pairs={{0,18},{1,19},{2,16},{3,17},{4,22},{5,23},{6,20},{7,21},{8,26},{9,... | collective-permute-start | bytes 12296 | tf_op jit(solution)/shard_map/ppermute | solution.py:576
  41.7 2.4 %collective-permute-done.13.refs_4_ = f32[1,8,128]{2,1,0:T(8,128)S(1)} collective-permute-done((f32[1,8,128]{2,1,0:T(8,128)S(1)}, f32[1,8,128]{2,1,0:T(8,128)S(1)}, u32[]{:S(2)}, u32[]{:S(2)}) %collective-permute-start.13) | collective-permute-done | bytes 4128 | tf_op jit(solution)/shard_map/ppermute | solution.py:576
  44.0 0.8 %collective-permute-done.12.refs_3_ = f32[1,8,128]{2,1,0:T(8,128)S(1)} collective-permute-done((f32[1,8,128]{2,1,0:T(8,128)S(1)}, f32[1,8,128]{2,1,0:T(8,128)S(1)}, u32[]{:S(2)}, u32[]{:S(2)}) %collective-permute-start.12) | collective-permute-done | bytes 4128 | tf_op jit(solution)/shard_map/ppermute | solution.py:509
  44.8 0.7 %update.1 = (f32[2,32,896]{2,1,0:T(8,128)}, f32[1,1]{1,0:T(1,128)}) custom-call(f32[2,32,896]{2,1,0:T(8,128)S(1)} %bitcast.7, f32[2,2,8,128]{3,2,1,0:T(8,128)S(1)} %copy-done.3, f32[28,8,128]{2,1,0:T(8,128)S(1)} %fusion.refs_0_, f32[29,8,128]{2,1,0:T(8,128)S(1)} %collective-permute-done.11.refs_1_, f32[1,8,128]{2,1,0:T(8,128)S(1)} %add.45.refs_2_, ...), custom_call_target="tpu_custom_call" | custom-call | tf_op jit(solution)/shard_map/update/pallas_call | solution.py:183
  (34 shorter events, 2.1 us)
Async XLA Ops:
  2.3 6.4 %collective-permute-start = (f32[28,8,128]{2,1,0:T(8,128)}, f32[28,8,128]{2,1,0:T(8,128)S(1)}, u32[]{:S(2)}, u32[]{:S(2)}) collective-permute-start(f32[28,8,128]{2,1,0:T(8,128)} %get-tuple-element.22), channel_id=1, source_target_pairs={{0,16},{16,0},{1,17},{17,1},{2,18},{18,2},{3,19},{19,3},{4,20},{20... | collective-permute-start | bytes 344072 | tf_op jit(solution)/shard_map/ppermute | solution.py:543
  5.3 0.9 %copy-start = (f32[1,2,32,896]{3,2,1,0:T(8,128)S(1)}, f32[1,2,32,896]{3,2,1,0:T(8,128)}, u32[]{:S(2)}) copy-start(f32[1,2,32,896]{3,2,1,0:T(8,128)} %param.7) | copy-start | bytes 688132
  6.3 1.0 %copy-start.2 = (bf16[4,256,256]{2,1,0:T(8,128)(2,1)S(1)}, bf16[4,256,256]{2,1,0:T(8,128)(2,1)}, u32[]{:S(2)}) copy-start(bf16[4,256,256]{2,1,0:T(8,128)(2,1)} %constant.36.clone.tables) | copy-start | bytes 1572868
  7.3 0.7 %copy-start.4 = (f32[2,2,2]{2,1,0:T(2,128)S(1)}, f32[2,2,2]{2,1,0:T(2,128)}, u32[]{:S(2)}) copy-start(f32[2,2,2]{2,1,0:T(2,128)} %paths.1) | copy-start | bytes 100
  8.7 3.4 %collective-permute-start.3 = (f32[28,8,128]{2,1,0:T(8,128)S(1)}, f32[28,8,128]{2,1,0:T(8,128)S(1)}, u32[]{:S(2)}, u32[]{:S(2)}) collective-permute-start(f32[28,8,128]{2,1,0:T(8,128)S(1)} %add.35.own), channel_id=1, source_target_pairs={{0,1},{1,0},{2,4},{3,5},{4,2},{5,3},{6,8},{7,9},{8,6},{9,7},{10,12... | collective-permute-start | bytes 344072 | tf_op jit(solution)/shard_map/ppermute | solution.py:509
  8.8 6.9 %collective-permute-start.2 = (f32[28,8,128]{2,1,0:T(8,128)S(1)}, f32[28,8,128]{2,1,0:T(8,128)S(1)}, u32[]{:S(2)}, u32[]{:S(2)}) collective-permute-start(f32[28,8,128]{2,1,0:T(8,128)S(1)} %add.35.own), channel_id=1, source_target_pairs={{0,2},{1,3},{2,0},{3,1},{4,6},{5,7},{6,4},{7,5},{8,10},{9,11},{10,... | collective-permute-start | bytes 344072 | tf_op jit(solution)/shard_map/ppermute | solution.py:509
  12.1 7.7 %copy-start.5 = (bf16[1,1,14,128,128]{4,3,2,1,0:T(8,128)(2,1)S(1)}, bf16[1,1,14,128,128]{4,3,2,1,0:T(8,128)(2,1)}, u32[]{:S(2)}) copy-start(bf16[1,1,14,128,128]{4,3,2,1,0:T(8,128)(2,1)} %param.10) | copy-start | bytes 1376260
  12.1 6.5 %collective-permute-start.1 = (f32[28,8,128]{2,1,0:T(8,128)S(1)}, f32[28,8,128]{2,1,0:T(8,128)S(1)}, u32[]{:S(2)}, u32[]{:S(2)}) collective-permute-start(f32[28,8,128]{2,1,0:T(8,128)S(1)} %add.35.own), channel_id=1, source_target_pairs={{0,1},{1,0},{2,3},{3,2},{4,5},{5,4},{6,7},{7,6},{8,9},{9,8},{10,11... | collective-permute-start | bytes 344072 | tf_op jit(solution)/shard_map/ppermute | solution.py:509
  15.7 4.0 %collective-permute-start.4 = (f32[28,8,128]{2,1,0:T(8,128)S(1)}, f32[28,8,128]{2,1,0:T(8,128)S(1)}, u32[]{:S(2)}, u32[]{:S(2)}) collective-permute-start(f32[28,8,128]{2,1,0:T(8,128)S(1)} %broadcast_select_fusion), channel_id=1, source_target_pairs={{0,1},{1,0},{2,3},{3,2},{4,5},{5,4},{6,7},{7,6},{8,9},{9,8},{10,11... | collective-permute-start | bytes 344072 | tf_op jit(solution)/shard_map/ppermute | solution.py:509
  15.8 0.9 %copy-start.6 = (f32[2,128,128]{2,1,0:T(8,128)S(1)}, f32[2,128,128]{2,1,0:T(8,128)}, u32[]{:S(2)}) copy-start(f32[2,128,128]{2,1,0:T(8,128)} %probe.1) | copy-start | bytes 393220
  16.7 0.7 %copy-start.7 = (s32[3,14]{1,0:T(4,128)S(1)}, s32[3,14]{1,0:T(4,128)}, u32[]{:S(2)}) copy-start(s32[3,14]{1,0:T(4,128)} %get-tuple-element.19.scalars) | copy-start | bytes 508
  19.8 25.0 %copy-start.1 = (f32[1,2,32,896]{3,2,1,0:T(8,128)S(1)}, f32[1,2,32,896]{3,2,1,0:T(8,128)}, u32[]{:S(2)}) copy-start(f32[1,2,32,896]{3,2,1,0:T(8,128)} %param.7) | copy-start | bytes 688132
  19.8 25.0 %copy-start.3 = (f32[2,2,8,128]{3,2,1,0:T(8,128)S(1)}, f32[2,2,8,128]{3,2,1,0:T(8,128)}, u32[]{:S(2)}) copy-start(f32[2,2,8,128]{3,2,1,0:T(8,128)} %get-tuple-element.18.factors) | copy-start | bytes 49156
  23.0 1.7 %collective-permute-start.5 = (f32[56,8,128]{2,1,0:T(8,128)S(1)}, f32[56,8,128]{2,1,0:T(8,128)S(1)}, u32[]{:S(2)}, u32[]{:S(2)}) collective-permute-start(f32[56,8,128]{2,1,0:T(8,128)S(1)} %get-tuple-element.28), channel_id=1, source_target_pairs={{0,1},{1,0},{2,3},{3,2},{4,5},{5,4},{6,7},{7,6},{8,9},{9,8},{10,11... | collective-permute-start | bytes 688136 | tf_op jit(solution)/shard_map/ppermute | solution.py:509
  24.7 13.3 %collective-permute-start.7 = (f32[28,8,128]{2,1,0:T(8,128)S(1)}, f32[28,8,128]{2,1,0:T(8,128)S(1)}, u32[]{:S(2)}, u32[]{:S(2)}) collective-permute-start(f32[28,8,128]{2,1,0:T(8,128)S(1)} %get-tuple-element.34), channel_id=1, source_target_pairs={{0,2},{1,3},{2,0},{3,1},{4,6},{5,7},{6,4},{7,5},{8,10},{9,11},{10,... | collective-permute-start | bytes 344072 | tf_op jit(solution)/shard_map/ppermute | solution.py:509
  27.3 10.8 %collective-permute-start.6 = (f32[28,8,128]{2,1,0:T(8,128)S(1)}, f32[28,8,128]{2,1,0:T(8,128)S(1)}, u32[]{:S(2)}, u32[]{:S(2)}) collective-permute-start(f32[28,8,128]{2,1,0:T(8,128)S(1)} %get-tuple-element.35), channel_id=1, source_target_pairs={{0,1},{1,0},{2,4},{3,5},{4,2},{5,3},{6,8},{7,9},{8,6},{9,7},{10,12... | collective-permute-start | bytes 344072 | tf_op jit(solution)/shard_map/ppermute | solution.py:509
  27.3 5.0 %collective-permute-start.8 = (f32[1,8,128]{2,1,0:T(8,128)S(1)}, f32[1,8,128]{2,1,0:T(8,128)S(1)}, u32[]{:S(2)}, u32[]{:S(2)}) collective-permute-start(f32[1,8,128]{2,1,0:T(8,128)S(1)} %get-tuple-element.31), channel_id=1, source_target_pairs={{0,4},{1,5},{2,6},{3,7},{4,0},{5,1},{6,2},{7,3},{8,12},{9,13},{10,... | collective-permute-start | bytes 12296 | tf_op jit(solution)/shard_map/ppermute | solution.py:509
  32.4 1.2 %collective-permute-start.9 = (f32[1,8,128]{2,1,0:T(8,128)S(1)}, f32[1,8,128]{2,1,0:T(8,128)S(1)}, u32[]{:S(2)}, u32[]{:S(2)}) collective-permute-start(f32[1,8,128]{2,1,0:T(8,128)S(1)} %add.43), channel_id=1, source_target_pairs={{0,1},{1,0},{2,3},{3,2},{4,5},{5,4},{6,7},{7,6},{8,9},{9,8},{10,11... | collective-permute-start | bytes 12296 | tf_op jit(solution)/shard_map/ppermute | solution.py:509
  33.5 4.5 %collective-permute-start.10 = (f32[1,8,128]{2,1,0:T(8,128)S(1)}, f32[1,8,128]{2,1,0:T(8,128)S(1)}, u32[]{:S(2)}, u32[]{:S(2)}) collective-permute-start(f32[1,8,128]{2,1,0:T(8,128)S(1)} %add.44), channel_id=1, source_target_pairs={{0,8},{1,9},{2,10},{3,11},{4,12},{5,13},{6,14},{7,15},{8,0},{9,1},... | collective-permute-start | bytes 12296 | tf_op jit(solution)/shard_map/ppermute | solution.py:509
  38.1 6.7 %collective-permute-start.11 = (f32[29,8,128]{2,1,0:T(8,128)S(1)}, f32[29,8,128]{2,1,0:T(8,128)S(1)}, u32[]{:S(2)}, u32[]{:S(2)}) collective-permute-start(f32[29,8,128]{2,1,0:T(8,128)S(1)} %pad_maximum_fusion), channel_id=1, source_target_pairs={{0,16},{16,0},{1,17},{17,1},{2,18},{18,2},{3,19},{19,3},{4,20},{20... | collective-permute-start | bytes 356360 | tf_op jit(solution)/shard_map/ppermute | solution.py:543
  39.4 4.6 %collective-permute-start.13 = (f32[1,8,128]{2,1,0:T(8,128)S(1)}, f32[1,8,128]{2,1,0:T(8,128)S(1)}, u32[]{:S(2)}, u32[]{:S(2)}) collective-permute-start(f32[1,8,128]{2,1,0:T(8,128)S(1)} %add.45.refs_2_), channel_id=1, source_target_pairs={{0,18},{1,19},{2,16},{3,17},{4,22},{5,23},{6,20},{7,21},{8,26},{9,... | collective-permute-start | bytes 12296 | tf_op jit(solution)/shard_map/ppermute | solution.py:576
  41.2 3.6 %collective-permute-start.12 = (f32[1,8,128]{2,1,0:T(8,128)S(1)}, f32[1,8,128]{2,1,0:T(8,128)S(1)}, u32[]{:S(2)}, u32[]{:S(2)}) collective-permute-start(f32[1,8,128]{2,1,0:T(8,128)S(1)} %add.45.refs_2_), channel_id=1, source_target_pairs={{0,2},{1,3},{2,0},{3,1},{4,6},{5,7},{6,4},{7,5},{8,10},{9,11},{10,... | collective-permute-start | bytes 12296 | tf_op jit(solution)/shard_map/ppermute | solution.py:509

commit v7 on v6

--- a/solution.py
+++ b/solution.py
@@ -14,8 +14,8 @@
 JIT = 16
 FLOOR_RATIO = 4.0
 LANES = 128
-TALL = 4
-SIDE = 14
+TALL = 2
+SIDE = 7
 BROAD = 2
 SUBS = 8
 HALF_PI = (1.5703125, 4.837512969970703125e-4, 7.54978995489188216e-8)
@@ -162,32 +162,28 @@
     )(slab, paths, tables)
 
 
-def update_kernel(count, slab, factors, *refs):
-    grads, sums, out, total = refs[:count], refs[count:-2], refs[-2], refs[-1]
+def update_kernel(slab, factors, *refs):
+    grads, out = refs[:-1], refs[-1]
     layers, rows, cols = slab.shape
-    blocks = grads[0].shape[0]
-    value = sums[0][0]
-    if len(sums) == 3:
-        value = (value + sums[1][0]) + (grads[1][blocks] + sums[2][0])
-    total[0, 0] = jnp.sum(value)
     for layer in range(layers):
         for i, r, c in blocks_of(rows, cols):
             value = slab[layer, r : r + SUBS, c : c + LANES]
-            for step in range(count):
-                value = value - factors[step, layer] * grads[step][i]
+            for step, grad in enumerate(grads):
+                value = value - factors[step, layer] * grad[i]
             out[layer, r : r + SUBS, c : c + LANES] = value
 
 
-def updated(slab, factors, grads, sums):
+def updated(slab, factors, grads):
     vmem = pl.BlockSpec(memory_space=pltpu.VMEM)
     return pl.pallas_call(
-        functools.partial(update_kernel, len(grads)),
-        out_shape=(jax.ShapeDtypeStruct(slab.shape, slab.dtype), jax.ShapeDtypeStruct((1, 1), jnp.float32)),
-        in_specs=[vmem] * (2 + len(grads) + len(sums)),
-        out_specs=(vmem, pl.BlockSpec(memory_space=pltpu.SMEM)),
+        update_kernel,
+        out_shape=jax.ShapeDtypeStruct(slab.shape, slab.dtype),
+        in_specs=[vmem] * (2 + len(grads)),
+        out_specs=vmem,
         compiler_params=pltpu.CompilerParams(vmem_limit_bytes=8 * 1024 * 1024),
+        cost_estimate=pl.CostEstimate(flops=2**24, bytes_accessed=2**20, transcendentals=0),
         name="update",
-    )(slab, factors, *grads, *sums)
+    )(slab, factors, *grads)
 
 
 FLAGS = ("second", "lower", "up2", "dn2", "relay")
@@ -559,27 +555,29 @@
     got = with_mate(to_mate)
     if groups != 2:
         local = joined(local, "blk", [2**k for k in range(groups.bit_length() - 1)])
-    local = joined(local, "wide", [4])
+    local = joined(local, "wide", [2])
     mine = mine + got[:blocks]
     passed = got[blocks:]
     zero = jnp.zeros_like(passed)
     from_pair = with_pair(by_pair + jnp.where(even, passed, zero))
     from_next = across(by_next + jnp.where(even, zero, passed))
     local = joined(local, "wide", [1])
-    local = joined(local, "wide", [2**k for k in range(3, columns.bit_length() - 1)])
+    local = joined(local, "wide", [8] + [2**k for k in range(4, columns.bit_length() - 1)])
     gradient = mine + (from_next + from_pair)
     grads = [gradient]
     if groups == 2:
         grads.append(to_group(jnp.concatenate([gradient, local], 0), 1))
-        sums = [local, with_pair(local)]
-        pairs = [(i, (i + columns) % (2 * columns) ^ 2) for i in range(2 * columns)]
+        sums = [local, permuted(local, "wide", lambda i: i ^ 4)]
+        pairs = [(i, (i + columns) % (2 * columns) ^ 4) for i in range(2 * columns)]
         sums.append(lax.ppermute(local, ("blk", "wide"), pairs))
     else:
         for step in range(1, groups):
             grads.append(to_group(gradient, step))
-        sums = [joined(local, "wide", [2])]
-    new, total = updated(slab, factors, grads, sums)
-    return (new[None], total[0, 0])
+        sums = [joined(local, "wide", [4])]
+    new = updated(slab, factors, grads)
+    if groups == 2:
+        sums = [(sums[0] + sums[1]) + (grads[1][blocks:] + sums[2])]
+    return (new[None], jnp.sum(sums[0]))
 
 
 def solution(mesh):

time: 45.8 us -> 47 us (1.026)
  starting transfers between devices: 17.4 us -> 19.7 us
  waiting for transfers between devices: 14.5 us -> 12.8 us
  other arithmetic: 0.1 us -> 0.7 us
    ppermute x1, waiting for transfers between devices: 2.36 us -> 0.11 us  [program(): sums.append(lax.ppermute(local, ('blk', 'wide'), pairs))]
    ppermute x11, starting transfers between devices: 11.3 us -> 13.2 us  [permuted(): return lax.ppermute(value, axis, pairs)]
    ppermute x2, waiting for transfers between devices: 0.07 us -> 1.46 us  [to_group(): lax.ppermute(value, 'blk', [(i, (i + step) % groups) for i in range(group...]
    ppermute x11, waiting for transfers between devices: 12 us -> 11.2 us  [permuted(): return lax.ppermute(value, axis, pairs)]
    reduce_sum x0 -> x1, other arithmetic: none -> 0.6 us  [program(): return (new[None], jnp.sum(sums[0]))]
  transfers between devices with their start and end apart: 14 -> 14, of which waited for: 8 -> 9; matrix products, arithmetic and copies ran while one was open for 0% -> 0% of each run, Pallas kernels for 7% -> 8%
where the time goes in v7:
time: 47 us; the launch traced here: 46.7 us
  starting transfers between devices  19.7 us (42%)
  waiting for transfers between devices  12.8 us (27%)
  Pallas kernels  8.54 us (18%)
  local copies, waits for them, and re-layouts  4.24 us (9%)
  between operations  0.77 us (2%)
  other arithmetic  0.7 us (1%)
    ppermute x11, starting transfers between devices, permuted(): return lax.ppermute(value, axis, pairs)  13.2 us
    ppermute x11, waiting for transfers between devices, permuted(): return lax.ppermute(value, axis, pairs)  11.2 us
    ppermute x2, starting transfers between devices, to_group(): lax.ppermute(value, 'blk', [(i, (i + step) % groups) for i in range(group...  4.32 us
    unnamed x16, local copies, waits for them, and re-layouts  4.24 us
    pallas_call x1, Pallas kernels, strip_gradient(): pl.pallas_call(strip_kernel, out_shape=tuple((block_list(n) for n in (blo...  3.17 us
    ppermute x1, starting transfers between devices, program(): sums.append(lax.ppermute(local, ('blk', 'wide'), pairs))  2.15 us
    pallas_call x1, Pallas kernels, slab_terms(): pl.pallas_call(functools.partial(terms_kernel, groups), out_shape=[listed...  1.67 us
    ppermute x2, waiting for transfers between devices, to_group(): lax.ppermute(value, 'blk', [(i, (i + step) % groups) for i in range(group...  1.46 us
  transfers between devices with their start and end apart: 14, of which 9 were waited for; matrix products, arithmetic and copies ran while one was open for 0% of the time, Pallas kernels for 8%

profile of v7, /device:TPU:0, one launch (start us, length us, event | category | flops | bytes accessed | tf_op | source)
XLA Modules:
  0.0 46.7 jit_solution(1196292005435796052)
XLA Ops:
  0.6 1.7 %terms.1 = (f32[28,8,128]{2,1,0:T(8,128)}, f32[2,2,8,128]{3,2,1,0:T(8,128)}, s32[3,14]{1,0:T(4,128)}) custom-call(f32[2,32,896]{2,1,0:T(8,128)} %bitcast.4, f32[2,2,2]{2,1,0:T(2,128)} %paths.1, s32[2,14]{1,0:T(2,128)} %bitcast.9, f32[2]{0:T(128)} %steps_hbm.1), custom_call_target="tpu_custom_call" | custom-call | tf_op jit(solution)/shard_map/terms/pallas_call | solution.py:122
  2.3 3.0 %collective-permute-start = (f32[28,8,128]{2,1,0:T(8,128)}, f32[28,8,128]{2,1,0:T(8,128)S(1)}, u32[]{:S(2)}, u32[]{:S(2)}) collective-permute-start(f32[28,8,128]{2,1,0:T(8,128)} %get-tuple-element.20), channel_id=1, source_target_pairs={{0,16},{16,0},{1,17},{17,1},{2,18},{18,2},{3,19},{19,3},{4,20},{20... | collective-permute-start | bytes 344072 | tf_op jit(solution)/shard_map/ppermute | solution.py:539
  5.3 0.9 %copy-done = f32[1,2,32,896]{3,2,1,0:T(8,128)S(1)} copy-done((f32[1,2,32,896]{3,2,1,0:T(8,128)S(1)}, f32[1,2,32,896]{3,2,1,0:T(8,128)}, u32[]{:S(2)}) %copy-start) | copy-done | bytes 229400
  6.3 1.0 %copy-done.2 = bf16[4,256,256]{2,1,0:T(8,128)(2,1)S(1)} copy-done((bf16[4,256,256]{2,1,0:T(8,128)(2,1)S(1)}, bf16[4,256,256]{2,1,0:T(8,128)(2,1)}, u32[]{:S(2)}) %copy-start.2) | copy-done | bytes 524312
  7.3 0.7 %copy-done.4 = f32[2,2,2]{2,1,0:T(2,128)S(1)} copy-done((f32[2,2,2]{2,1,0:T(2,128)S(1)}, f32[2,2,2]{2,1,0:T(2,128)}, u32[]{:S(2)}) %copy-start.4) | copy-done | bytes 56
  8.8 3.3 %collective-permute-start.2 = (f32[28,8,128]{2,1,0:T(8,128)S(1)}, f32[28,8,128]{2,1,0:T(8,128)S(1)}, u32[]{:S(2)}, u32[]{:S(2)}) collective-permute-start(f32[28,8,128]{2,1,0:T(8,128)S(1)} %add.44.own), channel_id=1, source_target_pairs={{0,2},{1,3},{2,0},{3,1},{4,6},{5,7},{6,4},{7,5},{8,10},{9,11},{10,... | collective-permute-start | bytes 344072 | tf_op jit(solution)/shard_map/ppermute | solution.py:505
  12.1 3.6 %collective-permute-done.2.pair = f32[28,8,128]{2,1,0:T(8,128)S(1)} collective-permute-done((f32[28,8,128]{2,1,0:T(8,128)S(1)}, f32[28,8,128]{2,1,0:T(8,128)S(1)}, u32[]{:S(2)}, u32[]{:S(2)}) %collective-permute-start.2) | collective-permute-done | bytes 114720 | tf_op jit(solution)/shard_map/ppermute | solution.py:505
  15.8 0.9 %copy-done.6 = f32[2,128,128]{2,1,0:T(8,128)S(1)} copy-done((f32[2,128,128]{2,1,0:T(8,128)S(1)}, f32[2,128,128]{2,1,0:T(8,128)}, u32[]{:S(2)}) %copy-start.6) | copy-done | bytes 131096
  16.7 0.7 %copy-done.7 = s32[3,14]{1,0:T(4,128)S(1)} copy-done((s32[3,14]{1,0:T(4,128)S(1)}, s32[3,14]{1,0:T(4,128)}, u32[]{:S(2)}) %copy-start.7) | copy-done | bytes 192
  17.4 1.1 %prepare.1 = (f32[1792,256]{1,0:T(8,128)S(1)}, s32[33,8,128]{2,1,0:T(8,128)S(1)}) custom-call(s32[3,14]{1,0:T(4,128)S(1)} %copy-done.7, f32[2,128,128]{2,1,0:T(8,128)S(1)} %copy-done.6), custom_call_target="tpu_custom_call" | custom-call | flops 134217728 | bytes 4194304 | tf_op jit(solution)/shard_map/prepare/pallas_call | solution.py:214
  18.5 1.2 %ahead.1 = (f32[1792,256]{1,0:T(8,128)S(1)}, f32[1792,256]{1,0:T(8,128)S(1)}) custom-call(s32[33,8,128]{2,1,0:T(8,128)S(1)} %get-tuple-element.18.frames, f32[28,8,128]{2,1,0:T(8,128)S(1)} %add.44.own, f32[28,8,128]{2,1,0:T(8,128)S(1)} %collective-permute-done.1.mate, f32[28,8,128]{2,1,0:T(8,128)S(1)} %collective-permute-done.2.pair, ...), custom_call_target="tpu_custom_call" | custom-call | flops 134217728 | bytes 4194304 | tf_op jit(solution)/shard_map/ahead/pallas_call | solution.py:331
  19.8 3.2 %strip.1 = (f32[28,8,128]{2,1,0:T(8,128)S(1)}, f32[56,8,128]{2,1,0:T(8,128)S(1)}, f32[28,8,128]{2,1,0:T(8,128)S(1)}, f32[28,8,128]{2,1,0:T(8,128)S(1)}, f32[1,8,128]{2,1,0:T(8,128)S(1)}) custom-call(s32[33,8,128]{2,1,0:T(8,128)S(1)} %get-tuple-element.18.frames, f32[1792,256]{1,0:T(8,128)S(1)} %get-tuple-element.23.wave, ...), custom_call_target="tpu_custom_call" | custom-call | flops 2818572288 | bytes 917504 | tf_op jit(solution)/shard_map/strip/pallas_call | solution.py:481
  23.5 1.1 %collective-permute-done.5 = f32[56,8,128]{2,1,0:T(8,128)S(1)} collective-permute-done((f32[56,8,128]{2,1,0:T(8,128)S(1)}, f32[56,8,128]{2,1,0:T(8,128)S(1)}, u32[]{:S(2)}, u32[]{:S(2)}) %collective-permute-start.5) | collective-permute-done | bytes 229408 | tf_op jit(solution)/shard_map/ppermute | solution.py:505
  24.7 2.5 %collective-permute-start.7 = (f32[28,8,128]{2,1,0:T(8,128)S(1)}, f32[28,8,128]{2,1,0:T(8,128)S(1)}, u32[]{:S(2)}, u32[]{:S(2)}) collective-permute-start(f32[28,8,128]{2,1,0:T(8,128)S(1)} %get-tuple-element.30), channel_id=1, source_target_pairs={{0,2},{1,3},{2,0},{3,1},{4,6},{5,7},{6,4},{7,5},{8,10},{9,11},{10,... | collective-permute-start | bytes 344072 | tf_op jit(solution)/shard_map/ppermute | solution.py:505
  27.3 2.9 %collective-permute-start.8 = (f32[1,8,128]{2,1,0:T(8,128)S(1)}, f32[1,8,128]{2,1,0:T(8,128)S(1)}, u32[]{:S(2)}, u32[]{:S(2)}) collective-permute-start(f32[1,8,128]{2,1,0:T(8,128)S(1)} %get-tuple-element.29), channel_id=1, source_target_pairs={{0,2},{1,3},{2,0},{3,1},{4,6},{5,7},{6,4},{7,5},{8,10},{9,11},{10,... | collective-permute-start | bytes 12296 | tf_op jit(solution)/shard_map/ppermute | solution.py:505
  30.3 2.4 %collective-permute-done.8 = f32[1,8,128]{2,1,0:T(8,128)S(1)} collective-permute-done((f32[1,8,128]{2,1,0:T(8,128)S(1)}, f32[1,8,128]{2,1,0:T(8,128)S(1)}, u32[]{:S(2)}, u32[]{:S(2)}) %collective-permute-start.8) | collective-permute-done | bytes 4128 | tf_op jit(solution)/shard_map/ppermute | solution.py:505
  32.7 1.2 %collective-permute-done.9 = f32[1,8,128]{2,1,0:T(8,128)S(1)} collective-permute-done((f32[1,8,128]{2,1,0:T(8,128)S(1)}, f32[1,8,128]{2,1,0:T(8,128)S(1)}, u32[]{:S(2)}, u32[]{:S(2)}) %collective-permute-start.9) | collective-permute-done | bytes 4128 | tf_op jit(solution)/shard_map/ppermute | solution.py:505
  33.9 3.6 %collective-permute-start.10 = (f32[1,8,128]{2,1,0:T(8,128)S(1)}, f32[1,8,128]{2,1,0:T(8,128)S(1)}, u32[]{:S(2)}, u32[]{:S(2)}) collective-permute-start(f32[1,8,128]{2,1,0:T(8,128)S(1)} %add.53), channel_id=1, source_target_pairs={{0,8},{1,9},{2,10},{3,11},{4,12},{5,13},{6,14},{7,15},{8,0},{9,1},... | collective-permute-start | bytes 12296 | tf_op jit(solution)/shard_map/ppermute | solution.py:505
  37.5 1.6 %collective-permute-done.10 = f32[1,8,128]{2,1,0:T(8,128)S(1)} collective-permute-done((f32[1,8,128]{2,1,0:T(8,128)S(1)}, f32[1,8,128]{2,1,0:T(8,128)S(1)}, u32[]{:S(2)}, u32[]{:S(2)}) %collective-permute-start.10) | collective-permute-done | bytes 4128 | tf_op jit(solution)/shard_map/ppermute | solution.py:505
  39.1 1.3 %collective-permute-start.11 = (f32[29,8,128]{2,1,0:T(8,128)S(1)}, f32[29,8,128]{2,1,0:T(8,128)S(1)}, u32[]{:S(2)}, u32[]{:S(2)}) collective-permute-start(f32[29,8,128]{2,1,0:T(8,128)S(1)} %pad_maximum_fusion), channel_id=1, source_target_pairs={{0,16},{16,0},{1,17},{17,1},{2,18},{18,2},{3,19},{19,3},{4,20},{20... | collective-permute-start | bytes 356360 | tf_op jit(solution)/shard_map/ppermute | solution.py:539
  40.4 2.2 %collective-permute-start.13 = (f32[1,8,128]{2,1,0:T(8,128)S(1)}, f32[1,8,128]{2,1,0:T(8,128)S(1)}, u32[]{:S(2)}, u32[]{:S(2)}) collective-permute-start(f32[1,8,128]{2,1,0:T(8,128)S(1)} %add.54), channel_id=1, source_target_pairs={{0,20},{1,21},{2,22},{3,23},{4,16},{5,17},{6,18},{7,19},{8,28},{9,... | collective-permute-start | bytes 12296 | tf_op jit(solution)/shard_map/ppermute | solution.py:572
  42.7 1.4 %collective-permute-done.11.refs_1_ = f32[29,8,128]{2,1,0:T(8,128)S(1)} collective-permute-done((f32[29,8,128]{2,1,0:T(8,128)S(1)}, f32[29,8,128]{2,1,0:T(8,128)S(1)}, u32[]{:S(2)}, u32[]{:S(2)}) %collective-permute-start.11) | collective-permute-done | bytes 118816 | tf_op jit(solution)/shard_map/ppermute | solution.py:539
  44.1 0.7 %update.1 = f32[2,32,896]{2,1,0:T(8,128)} custom-call(f32[2,32,896]{2,1,0:T(8,128)S(1)} %bitcast.6, f32[2,2,8,128]{3,2,1,0:T(8,128)S(1)} %copy-done.3, f32[28,8,128]{2,1,0:T(8,128)S(1)} %fusion.refs_0_, f32[29,8,128]{2,1,0:T(8,128)S(1)} %collective-permute-done.11.refs_1_), custom_call_target="tpu_custom_call" | custom-call | flops 16777216 | bytes 1048576 | tf_op jit(solution)/shard_map/update/pallas_call | solution.py:178
  44.9 1.3 %collective-permute-done.12 = f32[1,8,128]{2,1,0:T(8,128)S(1)} collective-permute-done((f32[1,8,128]{2,1,0:T(8,128)S(1)}, f32[1,8,128]{2,1,0:T(8,128)S(1)}, u32[]{:S(2)}, u32[]{:S(2)}) %collective-permute-start.12) | collective-permute-done | bytes 4128 | tf_op jit(solution)/shard_map/ppermute | solution.py:505
  (35 shorter events, 2.5 us)
Async XLA Ops:
  2.3 6.4 %collective-permute-start = (f32[28,8,128]{2,1,0:T(8,128)}, f32[28,8,128]{2,1,0:T(8,128)S(1)}, u32[]{:S(2)}, u32[]{:S(2)}) collective-permute-start(f32[28,8,128]{2,1,0:T(8,128)} %get-tuple-element.20), channel_id=1, source_target_pairs={{0,16},{16,0},{1,17},{17,1},{2,18},{18,2},{3,19},{19,3},{4,20},{20... | collective-permute-start | bytes 344072 | tf_op jit(solution)/shard_map/ppermute | solution.py:539
  5.3 0.9 %copy-start = (f32[1,2,32,896]{3,2,1,0:T(8,128)S(1)}, f32[1,2,32,896]{3,2,1,0:T(8,128)}, u32[]{:S(2)}) copy-start(f32[1,2,32,896]{3,2,1,0:T(8,128)} %param.7) | copy-start | bytes 688132
  6.3 1.0 %copy-start.2 = (bf16[4,256,256]{2,1,0:T(8,128)(2,1)S(1)}, bf16[4,256,256]{2,1,0:T(8,128)(2,1)}, u32[]{:S(2)}) copy-start(bf16[4,256,256]{2,1,0:T(8,128)(2,1)} %constant.37.clone.tables) | copy-start | bytes 1572868
  7.3 0.7 %copy-start.4 = (f32[2,2,2]{2,1,0:T(2,128)S(1)}, f32[2,2,2]{2,1,0:T(2,128)}, u32[]{:S(2)}) copy-start(f32[2,2,2]{2,1,0:T(2,128)} %paths.1) | copy-start | bytes 100
  8.7 3.4 %collective-permute-start.3 = (f32[28,8,128]{2,1,0:T(8,128)S(1)}, f32[28,8,128]{2,1,0:T(8,128)S(1)}, u32[]{:S(2)}, u32[]{:S(2)}) collective-permute-start(f32[28,8,128]{2,1,0:T(8,128)S(1)} %add.44.own), channel_id=1, source_target_pairs={{0,1},{1,0},{2,4},{3,5},{4,2},{5,3},{6,8},{7,9},{8,6},{9,7},{10,12... | collective-permute-start | bytes 344072 | tf_op jit(solution)/shard_map/ppermute | solution.py:505
  8.8 6.9 %collective-permute-start.2 = (f32[28,8,128]{2,1,0:T(8,128)S(1)}, f32[28,8,128]{2,1,0:T(8,128)S(1)}, u32[]{:S(2)}, u32[]{:S(2)}) collective-permute-start(f32[28,8,128]{2,1,0:T(8,128)S(1)} %add.44.own), channel_id=1, source_target_pairs={{0,2},{1,3},{2,0},{3,1},{4,6},{5,7},{6,4},{7,5},{8,10},{9,11},{10,... | collective-permute-start | bytes 344072 | tf_op jit(solution)/shard_map/ppermute | solution.py:505
  12.1 7.7 %copy-start.5 = (bf16[1,1,14,128,128]{4,3,2,1,0:T(8,128)(2,1)S(1)}, bf16[1,1,14,128,128]{4,3,2,1,0:T(8,128)(2,1)}, u32[]{:S(2)}) copy-start(bf16[1,1,14,128,128]{4,3,2,1,0:T(8,128)(2,1)} %param.10) | copy-start | bytes 1376260
  12.1 6.4 %collective-permute-start.1 = (f32[28,8,128]{2,1,0:T(8,128)S(1)}, f32[28,8,128]{2,1,0:T(8,128)S(1)}, u32[]{:S(2)}, u32[]{:S(2)}) collective-permute-start(f32[28,8,128]{2,1,0:T(8,128)S(1)} %add.44.own), channel_id=1, source_target_pairs={{0,1},{1,0},{2,3},{3,2},{4,5},{5,4},{6,7},{7,6},{8,9},{9,8},{10,11... | collective-permute-start | bytes 344072 | tf_op jit(solution)/shard_map/ppermute | solution.py:505
  15.7 4.0 %collective-permute-start.4 = (f32[28,8,128]{2,1,0:T(8,128)S(1)}, f32[28,8,128]{2,1,0:T(8,128)S(1)}, u32[]{:S(2)}, u32[]{:S(2)}) collective-permute-start(f32[28,8,128]{2,1,0:T(8,128)S(1)} %broadcast_select_fusion), channel_id=1, source_target_pairs={{0,1},{1,0},{2,3},{3,2},{4,5},{5,4},{6,7},{7,6},{8,9},{9,8},{10,11... | collective-permute-start | bytes 344072 | tf_op jit(solution)/shard_map/ppermute | solution.py:505
  15.8 0.9 %copy-start.6 = (f32[2,128,128]{2,1,0:T(8,128)S(1)}, f32[2,128,128]{2,1,0:T(8,128)}, u32[]{:S(2)}) copy-start(f32[2,128,128]{2,1,0:T(8,128)} %probe.1) | copy-start | bytes 393220
  16.7 0.7 %copy-start.7 = (s32[3,14]{1,0:T(4,128)S(1)}, s32[3,14]{1,0:T(4,128)}, u32[]{:S(2)}) copy-start(s32[3,14]{1,0:T(4,128)} %get-tuple-element.17.scalars) | copy-start | bytes 508
  19.8 24.3 %copy-start.1 = (f32[1,2,32,896]{3,2,1,0:T(8,128)S(1)}, f32[1,2,32,896]{3,2,1,0:T(8,128)}, u32[]{:S(2)}) copy-start(f32[1,2,32,896]{3,2,1,0:T(8,128)} %param.7) | copy-start | bytes 688132
  19.8 24.3 %copy-start.3 = (f32[2,2,8,128]{3,2,1,0:T(8,128)S(1)}, f32[2,2,8,128]{3,2,1,0:T(8,128)}, u32[]{:S(2)}) copy-start(f32[2,2,8,128]{3,2,1,0:T(8,128)} %get-tuple-element.16.factors) | copy-start | bytes 49156
  23.0 1.7 %collective-permute-start.5 = (f32[56,8,128]{2,1,0:T(8,128)S(1)}, f32[56,8,128]{2,1,0:T(8,128)S(1)}, u32[]{:S(2)}, u32[]{:S(2)}) collective-permute-start(f32[56,8,128]{2,1,0:T(8,128)S(1)} %get-tuple-element.26), channel_id=1, source_target_pairs={{0,1},{1,0},{2,3},{3,2},{4,5},{5,4},{6,7},{7,6},{8,9},{9,8},{10,11... | collective-permute-start | bytes 688136 | tf_op jit(solution)/shard_map/ppermute | solution.py:505
  24.7 14.4 %collective-permute-start.7 = (f32[28,8,128]{2,1,0:T(8,128)S(1)}, f32[28,8,128]{2,1,0:T(8,128)S(1)}, u32[]{:S(2)}, u32[]{:S(2)}) collective-permute-start(f32[28,8,128]{2,1,0:T(8,128)S(1)} %get-tuple-element.30), channel_id=1, source_target_pairs={{0,2},{1,3},{2,0},{3,1},{4,6},{5,7},{6,4},{7,5},{8,10},{9,11},{10,... | collective-permute-start | bytes 344072 | tf_op jit(solution)/shard_map/ppermute | solution.py:505
  27.2 11.8 %collective-permute-start.6 = (f32[28,8,128]{2,1,0:T(8,128)S(1)}, f32[28,8,128]{2,1,0:T(8,128)S(1)}, u32[]{:S(2)}, u32[]{:S(2)}) collective-permute-start(f32[28,8,128]{2,1,0:T(8,128)S(1)} %get-tuple-element.31), channel_id=1, source_target_pairs={{0,1},{1,0},{2,4},{3,5},{4,2},{5,3},{6,8},{7,9},{8,6},{9,7},{10,12... | collective-permute-start | bytes 344072 | tf_op jit(solution)/shard_map/ppermute | solution.py:505
  27.3 5.4 %collective-permute-start.8 = (f32[1,8,128]{2,1,0:T(8,128)S(1)}, f32[1,8,128]{2,1,0:T(8,128)S(1)}, u32[]{:S(2)}, u32[]{:S(2)}) collective-permute-start(f32[1,8,128]{2,1,0:T(8,128)S(1)} %get-tuple-element.29), channel_id=1, source_target_pairs={{0,2},{1,3},{2,0},{3,1},{4,6},{5,7},{6,4},{7,5},{8,10},{9,11},{10,... | collective-permute-start | bytes 12296 | tf_op jit(solution)/shard_map/ppermute | solution.py:505
  32.7 1.2 %collective-permute-start.9 = (f32[1,8,128]{2,1,0:T(8,128)S(1)}, f32[1,8,128]{2,1,0:T(8,128)S(1)}, u32[]{:S(2)}, u32[]{:S(2)}) collective-permute-start(f32[1,8,128]{2,1,0:T(8,128)S(1)} %add.52), channel_id=1, source_target_pairs={{0,1},{1,0},{2,3},{3,2},{4,5},{5,4},{6,7},{7,6},{8,9},{9,8},{10,11... | collective-permute-start | bytes 12296 | tf_op jit(solution)/shard_map/ppermute | solution.py:505
  33.9 5.1 %collective-permute-start.10 = (f32[1,8,128]{2,1,0:T(8,128)S(1)}, f32[1,8,128]{2,1,0:T(8,128)S(1)}, u32[]{:S(2)}, u32[]{:S(2)}) collective-permute-start(f32[1,8,128]{2,1,0:T(8,128)S(1)} %add.53), channel_id=1, source_target_pairs={{0,8},{1,9},{2,10},{3,11},{4,12},{5,13},{6,14},{7,15},{8,0},{9,1},... | collective-permute-start | bytes 12296 | tf_op jit(solution)/shard_map/ppermute | solution.py:505
  39.1 4.9 %collective-permute-start.11 = (f32[29,8,128]{2,1,0:T(8,128)S(1)}, f32[29,8,128]{2,1,0:T(8,128)S(1)}, u32[]{:S(2)}, u32[]{:S(2)}) collective-permute-start(f32[29,8,128]{2,1,0:T(8,128)S(1)} %pad_maximum_fusion), channel_id=1, source_target_pairs={{0,16},{16,0},{1,17},{17,1},{2,18},{18,2},{3,19},{19,3},{4,20},{20... | collective-permute-start | bytes 356360 | tf_op jit(solution)/shard_map/ppermute | solution.py:539
  40.4 4.5 %collective-permute-start.13 = (f32[1,8,128]{2,1,0:T(8,128)S(1)}, f32[1,8,128]{2,1,0:T(8,128)S(1)}, u32[]{:S(2)}, u32[]{:S(2)}) collective-permute-start(f32[1,8,128]{2,1,0:T(8,128)S(1)} %add.54), channel_id=1, source_target_pairs={{0,20},{1,21},{2,22},{3,23},{4,16},{5,17},{6,18},{7,19},{8,28},{9,... | collective-permute-start | bytes 12296 | tf_op jit(solution)/shard_map/ppermute | solution.py:572
  42.5 3.6 %collective-permute-start.12 = (f32[1,8,128]{2,1,0:T(8,128)S(1)}, f32[1,8,128]{2,1,0:T(8,128)S(1)}, u32[]{:S(2)}, u32[]{:S(2)}) collective-permute-start(f32[1,8,128]{2,1,0:T(8,128)S(1)} %add.54), channel_id=1, source_target_pairs={{0,4},{1,5},{2,6},{3,7},{4,0},{5,1},{6,2},{7,3},{8,12},{9,13},{10,... | collective-permute-start | bytes 12296 | tf_op jit(solution)/shard_map/ppermute | solution.py:505
